TPU v7x, 16 devices: a 4x2x1 block of a 4x4x8 slice. The times are simulated.
16 devices in a mesh: dp: 2 (over y, z), ep: 8 (over x, core).
Axes of the slice: x: 4, y: 2, z: 1, core: 2. Of those that a mesh axis runs over, the one named last changes fastest.
The devices are a block of a 4x4x8 slice.
Arguments:
- grad_y: bfloat16 [2048, 1024], P(('dp', 'ep')), parts along dimension 0
- gate_vals: float32 [2048, 8], P(('dp', 'ep')), parts along dimension 0
- topk_idx: int32 [2048, 8], P(('dp', 'ep')), parts along dimension 0
- slot_ids: int32 [2048, 8], P(('dp', 'ep')), parts along dimension 0
- pair_counts: int32 [16, 32], P(('dp', 'ep')), parts along dimension 0
- y_routed: bfloat16 [2048, 8, 1024], P(('dp', 'ep')), parts along dimension 0
- x_disp: bfloat16 [64, 512, 1024], P(('dp', 'ep')), parts along dimension 0
- h_gate: bfloat16 [64, 512, 512], P(('dp', 'ep')), parts along dimension 0
- h_up: bfloat16 [64, 512, 512], P(('dp', 'ep')), parts along dimension 0
- w_gate: bfloat16 [32, 1024, 512], P('ep')
- w_up: bfloat16 [32, 1024, 512], P('ep')
- w_down: bfloat16 [32, 512, 1024], P('ep')
Outputs:
- output 1: bfloat16 [2048, 1024], P(('dp', 'ep')), parts along dimension 0
- output 2: float32 [2048, 8], P(('dp', 'ep')), parts along dimension 0
- output 3: float32 [64, 1024, 512], P(('dp', 'ep')), parts along dimension 0
- output 4: float32 [64, 1024, 512], P(('dp', 'ep')), parts along dimension 0
- output 5: float32 [64, 512, 1024], P(('dp', 'ep')), parts along dimension 0
There are 2 independent parts. A program takes and returns all parts, laid end to end along the dimension named above; an argument that names none is the same for every part.
All inputs are finite; a program needn't handle non-finite values.
Results may differ from a plain program's by a relative error of at most 0.0149547.
Values are sent between devices in bfloat16 or wider.
A program may use at most 768 MiB of HBM per device.

v0:
```python
import jax
import jax.numpy as jnp
from jax import lax
from jax.sharding import PartitionSpec as P


def build_send(grad_y, gate_vals, topk_idx, slot_ids, n_exp, cap_rows):
    tok_dev, top_k = topk_idx.shape
    dest_row = jnp.where(slot_ids >= 0, topk_idx * cap_rows + slot_ids, n_exp * cap_rows).reshape(-1)
    row_source = jnp.full((n_exp * cap_rows,), tok_dev * top_k, jnp.int32).at[dest_row].set(jnp.arange(tok_dev * top_k, dtype=jnp.int32), mode="drop")
    dy_rows = jnp.take(grad_y, row_source // top_k, axis=0, mode="fill", fill_value=0)
    gate_rows = jnp.take(gate_vals.reshape(-1), row_source, mode="fill", fill_value=0)
    return (gate_rows[:, None] * dy_rows).astype(jnp.bfloat16).reshape(n_exp, cap_rows, grad_y.shape[1])


def gather_back(ret_rows, topk_idx, slot_ids, cap_rows):
    tok_dev, top_k = topk_idx.shape
    src_row = jnp.where(slot_ids >= 0, topk_idx * cap_rows + slot_ids, ret_rows.shape[0]).reshape(-1)
    picked = jnp.take(ret_rows, src_row, axis=0, mode="fill", fill_value=0).reshape(tok_dev, top_k, ret_rows.shape[1])
    return jnp.sum(picked, axis=1, dtype=jnp.float32).astype(jnp.bfloat16)


def expert_grads(grad_rows, x_rows, hg_rows, hu_rows, w_gate, w_up, w_down):
    grad_hidden = jnp.einsum("erd,efd->erf", grad_rows, w_down, preferred_element_type=jnp.float32).astype(jnp.bfloat16)
    gate_f = hg_rows.astype(jnp.float32)
    up_f = hu_rows.astype(jnp.float32)
    gate_sig = jax.nn.sigmoid(gate_f)
    gate_act = gate_f * gate_sig
    hidden_act = (gate_act * up_f).astype(jnp.bfloat16)
    grad_h = grad_hidden.astype(jnp.float32)
    grad_hgate = (grad_h * up_f * gate_sig * (1.0 + gate_f * (1.0 - gate_sig))).astype(jnp.bfloat16)
    grad_hup = (grad_h * gate_act).astype(jnp.bfloat16)
    grad_wdown = jnp.einsum("erf,erd->efd", hidden_act, grad_rows, preferred_element_type=jnp.float32)
    grad_wgate = jnp.einsum("erd,erf->edf", x_rows, grad_hgate, preferred_element_type=jnp.float32)
    grad_wup = jnp.einsum("erd,erf->edf", x_rows, grad_hup, preferred_element_type=jnp.float32)
    grad_disp = (jnp.einsum("erf,edf->erd", grad_hgate, w_gate, preferred_element_type=jnp.float32) + jnp.einsum("erf,edf->erd", grad_hup, w_up, preferred_element_type=jnp.float32)).astype(jnp.bfloat16)
    return grad_disp, grad_wgate, grad_wup, grad_wdown


def solution(mesh):
    n_dev = mesh.shape["ep"]
    rows_spec = P(("dp", "ep"), None)
    cube_spec = P(("dp", "ep"), None, None)
    weight_spec = P("ep", None, None)

    def local_step(grad_y, gate_vals, topk_idx, slot_ids, pair_counts, y_routed, x_disp, h_gate, h_up, w_gate, w_up, w_down):
        n_loc = w_gate.shape[0]
        n_exp = n_loc * n_dev
        cap_rows = x_disp.shape[1] // n_dev
        model_dim = grad_y.shape[1]
        grad_gate = jnp.einsum("td,tkd->tk", grad_y, y_routed, preferred_element_type=jnp.float32)
        send_rows = build_send(grad_y, gate_vals, topk_idx, slot_ids, n_exp, cap_rows)
        recv_rows = lax.all_to_all(send_rows.reshape(n_dev, n_loc, cap_rows, model_dim), "ep", 0, 1)
        recv_counts = lax.all_to_all(pair_counts.reshape(n_dev, n_loc), "ep", 0, 1)
        keep_row = lax.broadcasted_iota(jnp.int32, (n_loc, n_dev, cap_rows), 2) < recv_counts[:, :, None]
        grad_rows = jnp.where(keep_row[..., None], recv_rows, jnp.zeros((), jnp.bfloat16)).reshape(n_loc, n_dev * cap_rows, model_dim)
        grad_disp, grad_wgate, grad_wup, grad_wdown = expert_grads(grad_rows, x_disp, h_gate, h_up, w_gate, w_up, w_down)
        ret_rows = lax.all_to_all(grad_disp.reshape(n_loc, n_dev, cap_rows, model_dim), "ep", 1, 0)
        grad_x = gather_back(ret_rows.reshape(n_exp * cap_rows, model_dim), topk_idx, slot_ids, cap_rows)
        return grad_x, grad_gate, grad_wgate, grad_wup, grad_wdown

    return jax.shard_map(local_step, mesh=mesh, in_specs=(rows_spec, rows_spec, rows_spec, rows_spec, rows_spec, cube_spec, cube_spec, cube_spec, cube_spec, weight_spec, weight_spec, weight_spec), out_specs=(rows_spec, rows_spec, cube_spec, cube_spec, cube_spec), check_vma=False)
```

profile of v0, /device:TPU:112, one launch (start us, length us, event | category | flops | bytes accessed | tf_op | source)
XLA Modules:
  0.0 185.5 jit_solution(6640641705909561554)
XLA Ops:
  0.6 0.0 copy-start
  0.6 0.5 broadcast.117
  1.2 1.4 reduce.4
  2.6 0.7 broadcast_in_dim_reshape.6
  3.3 5.3 %all-to-all-start = ((s32[8,4,1]{1,2,0:T(1,128)}), s32[8,4,1]{1,2,0:T(1,128)S(1)}, u32[]{:S(2)}, u32[]{:S(2)}) async-start(s32[8,4,1]{1,2,0:T(1,128)} %bitcast), calls=%async_computation | async-start | bytes 8192 | tf_op jit(solution)/shard_map/all_to_all | solution.py:54
  8.6 0.7 compare_and_fusion.1
  9.3 0.1 copy.52
  9.4 0.1 reshape.115
  9.5 4.3 %scatter_custom_fusion = s32[2048]{0:T(1024)S(1)} fusion(s32[1024]{0:T(1024)S(1)} %bitcast.42, s32[1024]{0:T(1024)S(1)} %iota.18, s32[]{:T(128)} %constant.61.clone.1), kind=kCustom, calls=%fused_computation.48 | custom fusion | bytes 8196 | tf_op jit(solution)/shard_map/scatter | solution.py:10
  13.9 0.8 copy.53
  14.7 0.1 reshape.116
  14.8 0.0 copy-start.2
  14.8 8.6 %gather_fusion = f32[2048]{0:T(1024)S(1)} fusion(f32[1024]{0:T(1024)S(1)} %reshape.116, s32[2048]{0:T(1024)S(1)} %get-tuple-element.27), kind=kCustom, calls=%fused_computation | custom fusion | bytes 24576 | tf_op jit(solution)/shard_map/jit(_take)/gather | solution.py:12
  23.4 0.1 mul.43
  23.5 0.1 broadcast_in_dim.61
  23.5 0.0 copy-done.2
  23.5 9.6 %gather_fusion.1 = bf16[2048,1024]{1,0:T(8,128)(2,1)} fusion(bf16[128,1024]{1,0:T(8,128)(2,1)S(1)} %copy-done.2, s32[2048]{0:T(1024)S(1)} %get-tuple-element.28), kind=kCustom, calls=%fused_computation.1 | custom fusion | bytes 8396800 | tf_op jit(solution)/shard_map/jit(_take)/gather | solution.py:11
  33.1 4.2 %multiply_convert_fusion = bf16[8,4,1,64,1024]{4,3,1,2,0:T(8,128)(2,1)} fusion(bf16[8,4,1,64,1024]{4,3,1,2,0:T(8,128)(2,1)} %bitcast.38, f32[8,4,64]{2,1,0:T(4,128)S(1)} %mul.43, pred[8,4,64]{2,1,0:T(4,128)(4,1)S(1)} %broadcast_in_dim.61), kind=kLoop, calls=%fused_computation.5 | loop fusion | flops 8388608 | bytes 8398848 | tf_op jit(solution)/shard_map/convert_element_type | solution.py:13
  37.3 0.0 all-to-all-done
  37.3 4.8 %all-to-all-start.1 = ((bf16[8,4,1,64,1024]{4,3,1,2,0:T(8,128)(2,1)}), bf16[8,4,1,64,1024]{4,3,1,2,0:T(8,128)(2,1)}, u32[]{:S(2)}, u32[]{:S(2)}) async-start(bf16[8,4,1,64,1024]{4,3,1,2,0:T(8,128)(2,1)} %multiply_convert_fusion), calls=%async_computation.1 | async-start | bytes 8388608 | tf_op jit(solution)/shard_map/all_to_all | solution.py:53
  42.1 0.1 iota.16
  42.2 0.1 copy.49
  42.4 0.0 copy-done
  42.4 1.4 fusion.16
  43.7 0.7 copy.63
  44.4 0.1 copy.51
  44.5 0.1 lt.54
  44.6 0.1 lt.55
  44.7 47.1 %all-to-all-done.1 = bf16[8,4,1,64,1024]{4,3,1,2,0:T(8,128)(2,1)} async-done(((bf16[8,4,1,64,1024]{4,3,1,2,0:T(8,128)(2,1)}), bf16[8,4,1,64,1024]{4,3,1,2,0:T(8,128)(2,1)}, u32[]{:S(2)}, u32[]{:S(2)}) %all-to-all-start.1) | async-done | bytes 4194336 | tf_op jit(solution)/shard_map/all_to_all | solution.py:53
  91.8 0.0 copy-start.4
  91.8 2.9 %copy.55 = bf16[8,4,1,64,1024]{4,3,0,1,2:T(8,128)(2,1)S(1)} copy(bf16[8,4,1,64,1024]{4,3,1,2,0:T(8,128)(2,1)} %all-to-all-done.1) | data formatting | bytes 8388608 | tf_op jit(solution)/shard_map/all_to_all | solution.py:53
  94.7 0.0 copy-start.3
  94.7 2.0 %copy-done.3 = bf16[8,4,1,64,1024]{4,3,0,1,2:T(8,128)(2,1)} copy-done((bf16[8,4,1,64,1024]{4,3,0,1,2:T(8,128)(2,1)}, bf16[8,4,1,64,1024]{4,3,0,1,2:T(8,128)(2,1)S(1)}, u32[]{:S(2)}) %copy-start.3) | copy-done | bytes 4194328
  96.6 0.0 copy-done.4
  96.6 0.0 copy-start.5
  96.6 0.0 copy-start.7
  96.6 0.0 copy-start.8
  96.6 3.6 %fusion.15 = bf16[4,512,512]{2,1,0:T(8,128)(2,1)} fusion(bf16[4,512,1024]{2,1,0:T(8,128)(2,1)S(1)} %copy-done.4, bf16[4,512,1024]{2,1,0:T(8,128)(2,1)S(1)} %bitcast.39, pred[4,512]{1,0:T(4,128)(4,1)S(1)} %broadcast_compare_fusion), kind=kOutput, calls=%fused_computation.30 | convolution fusion | flops 2150629376 | bytes 10487808 | tf_op jit(solution)/shard_map/erd,efd->erf/dot_general | solution.py:24
  100.3 0.0 copy-done.5
  100.3 0.0 copy-done.7
  100.3 0.6 copy-done.8
  100.9 0.0 copy-start.6
  100.9 8.3 %fusion.29 = f32[4,512,1024]{2,1,0:T(8,128)} fusion(bf16[4,1024,512]{2,1,0:T(8,128)(2,1)S(1)} %copy-done.5, bf16[4,512,512]{2,1,0:T(8,128)(2,1)S(1)} %copy-done.7, bf16[4,512,512]{2,1,0:T(8,128)(2,1)} %fusion.15, bf16[4,512,512]{2,1,0:T(8,128)(2,1)S(1)} %copy-done.8), kind=kOutput, calls=%fused_computation.57 | convolution fusion | flops 2161115136 | bytes 18874368 | tf_op jit(solution)/shard_map/erf,edf->erd/dot_general | solution.py:36
  109.1 0.0 copy-done.6
  109.1 7.2 %add_convert_fusion = bf16[4,512,1024]{2,1,0:T(8,128)(2,1)S(1)} fusion(f32[4,512,1024]{2,1,0:T(8,128)} %fusion.29, bf16[4,1024,512]{2,1,0:T(8,128)(2,1)S(1)} %copy-done.6, bf16[4,512,512]{2,1,0:T(8,128)(2,1)} %fusion.15, bf16[4,512,512]{2,1,0:T(8,128)(2,1)} %param.19), kind=kOutput, calls=%fused_computation.4 | convolution fusion | flops 2160066560 | bytes 20971520 | tf_op jit(solution)/shard_map/erf,edf->erd/dot_general | solution.py:36
  116.4 2.7 %copy.56 = bf16[1,4,8,64,1024]{4,3,1,0,2:T(8,128)(2,1)} copy(bf16[1,4,8,64,1024]{4,3,2,1,0:T(8,128)(2,1)S(1)} %bitcast.41) | data formatting | bytes 8388608 | tf_op jit(solution)/shard_map/broadcast_in_dim;reshape | solution.py:58
  119.0 4.9 %all-to-all-start.2 = ((bf16[1,4,8,64,1024]{4,3,1,0,2:T(8,128)(2,1)}), bf16[1,4,8,64,1024]{4,3,1,0,2:T(8,128)(2,1)}, u32[]{:S(2)}, u32[]{:S(2)}) async-start(bf16[1,4,8,64,1024]{4,3,1,0,2:T(8,128)(2,1)} %copy.56), calls=%async_computation.2 | async-start | bytes 8388608 | tf_op jit(solution)/shard_map/all_to_all | solution.py:58
  124.0 9.9 %convolution_bitcast_fusion.1 = f32[4,1024,512]{1,2,0:T(8,128)} fusion(bf16[4,512,1024]{2,1,0:T(8,128)(2,1)} %param.18, bf16[4,512,512]{2,1,0:T(8,128)(2,1)S(1)} %copy-done.7, bf16[4,512,512]{2,1,0:T(8,128)(2,1)} %fusion.15, bf16[4,512,512]{2,1,0:T(8,128)(2,1)} %param.19), kind=kOutput, calls=%fused_computation.25 | convolution fusion | flops 2161115136 | bytes 18874368 | tf_op jit(solution)/shard_map/erd,erf->edf/dot_general | solution.py:34
  133.9 8.7 %copy.60 = f32[4,1024,512]{2,1,0:T(8,128)} copy(f32[4,1024,512]{1,2,0:T(8,128)} %convolution_bitcast_fusion.1) | data formatting | bytes 16777216
  142.5 9.4 %convolution_bitcast_fusion = f32[4,1024,512]{1,2,0:T(8,128)} fusion(bf16[4,512,1024]{2,1,0:T(8,128)(2,1)} %param.18, bf16[4,512,512]{2,1,0:T(8,128)(2,1)} %fusion.15, bf16[4,512,512]{2,1,0:T(8,128)(2,1)} %param.19), kind=kOutput, calls=%fused_computation.24 | convolution fusion | flops 2155872256 | bytes 16777216 | tf_op jit(solution)/shard_map/erd,erf->edf/dot_general | solution.py:35
  151.9 8.7 %copy.61 = f32[4,1024,512]{2,1,0:T(8,128)} copy(f32[4,1024,512]{1,2,0:T(8,128)} %convolution_bitcast_fusion) | data formatting | bytes 16777216
  160.6 9.1 %fusion.9 = f32[4,512,1024]{2,1,0:T(8,128)} fusion(bf16[4,512,1024]{2,1,0:T(8,128)(2,1)} %bitcast.40, pred[4,512]{1,0:T(4,128)(4,1)S(1)} %broadcast_compare_fusion, bf16[4,512,512]{2,1,0:T(8,128)(2,1)S(1)} %copy-done.7, bf16[4,512,512]{2,1,0:T(8,128)(2,1)} %param.19), kind=kOutput, calls=%fused_computation.22 | convolution fusion | flops 2157969408 | bytes 16779264 | tf_op jit(solution)/shard_map/erf,erd->efd/dot_general | solution.py:33
  169.7 3.5 %all-to-all-done.2 = bf16[1,4,8,64,1024]{4,3,1,0,2:T(8,128)(2,1)} async-done(((bf16[1,4,8,64,1024]{4,3,1,0,2:T(8,128)(2,1)}), bf16[1,4,8,64,1024]{4,3,1,0,2:T(8,128)(2,1)}, u32[]{:S(2)}, u32[]{:S(2)}) %all-to-all-start.2) | async-done | bytes 4194336 | tf_op jit(solution)/shard_map/all_to_all | solution.py:58
  173.2 0.0 copy-start.1
  173.2 8.9 %gather_fusion.2 = bf16[1024,1024]{1,0:T(8,128)(2,1)} fusion(bf16[2048,1024]{1,0:T(8,128)(2,1)} %bitcast.13, s32[1024]{0:T(1024)S(1)} %broadcast_clamp_fusion.1), kind=kCustom, calls=%fused_computation.2 | custom fusion | bytes 4198400 | tf_op jit(solution)/shard_map/jit(_take)/gather | solution.py:19
  182.1 3.4 %fusion.12 = bf16[128,1024]{1,0:T(8,128)(2,1)} fusion(bf16[1024,1024]{1,0:T(8,128)(2,1)} %gather_fusion.2, pred[128,8]{1,0:T(8,128)(4,1)S(1)} %copy.49), kind=kLoop, calls=%fused_computation.27 | loop fusion | flops 1966080 | bytes 2360320 | tf_op jit(solution)/shard_map/reduce_sum | solution.py:20
  185.5 0.0 copy-done.1
  (8 shorter events, 0.1 us)
Async XLA Ops:
  0.6 41.7 %copy-start = (bf16[128,8,1024]{2,1,0:T(8,128)(2,1)S(1)}, bf16[128,8,1024]{2,1,0:T(8,128)(2,1)}, u32[]{:S(2)}) copy-start(bf16[128,8,1024]{2,1,0:T(8,128)(2,1)} %param.17) | copy-start | bytes 6291460
  3.3 34.1 %all-to-all-start = ((s32[8,4,1]{1,2,0:T(1,128)}), s32[8,4,1]{1,2,0:T(1,128)S(1)}, u32[]{:S(2)}, u32[]{:S(2)}) async-start(s32[8,4,1]{1,2,0:T(1,128)} %bitcast), calls=%async_computation | async-start | bytes 8192 | tf_op jit(solution)/shard_map/all_to_all | solution.py:54
  14.8 8.8 %copy-start.2 = (bf16[128,1024]{1,0:T(8,128)(2,1)S(1)}, bf16[128,1024]{1,0:T(8,128)(2,1)}, u32[]{:S(2)}) copy-start(bf16[128,1024]{1,0:T(8,128)(2,1)} %param.12) | copy-start | bytes 786436
  37.3 54.5 %all-to-all-start.1 = ((bf16[8,4,1,64,1024]{4,3,1,2,0:T(8,128)(2,1)}), bf16[8,4,1,64,1024]{4,3,1,2,0:T(8,128)(2,1)}, u32[]{:S(2)}, u32[]{:S(2)}) async-start(bf16[8,4,1,64,1024]{4,3,1,2,0:T(8,128)(2,1)} %multiply_convert_fusion), calls=%async_computation.1 | async-start | bytes 8388608 | tf_op jit(solution)/shard_map/all_to_all | solution.py:53
  91.8 4.8 %copy-start.4 = (bf16[4,512,1024]{2,1,0:T(8,128)(2,1)S(1)}, bf16[4,512,1024]{2,1,0:T(8,128)(2,1)}, u32[]{:S(2)}) copy-start(bf16[4,512,1024]{2,1,0:T(8,128)(2,1)} %param.23) | copy-start | bytes 12582916
  94.7 2.0 %copy-start.3 = (bf16[8,4,1,64,1024]{4,3,0,1,2:T(8,128)(2,1)}, bf16[8,4,1,64,1024]{4,3,0,1,2:T(8,128)(2,1)S(1)}, u32[]{:S(2)}) copy-start(bf16[8,4,1,64,1024]{4,3,0,1,2:T(8,128)(2,1)S(1)} %copy.55) | copy-start | bytes 12582916
  96.6 3.6 %copy-start.5 = (bf16[4,1024,512]{2,1,0:T(8,128)(2,1)S(1)}, bf16[4,1024,512]{2,1,0:T(8,128)(2,1)}, u32[]{:S(2)}) copy-start(bf16[4,1024,512]{2,1,0:T(8,128)(2,1)} %param.21) | copy-start | bytes 12582916
  96.6 3.6 %copy-start.7 = (bf16[4,512,512]{2,1,0:T(8,128)(2,1)S(1)}, bf16[4,512,512]{2,1,0:T(8,128)(2,1)}, u32[]{:S(2)}) copy-start(bf16[4,512,512]{2,1,0:T(8,128)(2,1)} %param.20) | copy-start | bytes 6291460
  96.6 4.2 %copy-start.8 = (bf16[4,512,512]{2,1,0:T(8,128)(2,1)S(1)}, bf16[4,512,512]{2,1,0:T(8,128)(2,1)}, u32[]{:S(2)}) copy-start(bf16[4,512,512]{2,1,0:T(8,128)(2,1)} %param.19) | copy-start | bytes 6291460
  100.9 8.3 %copy-start.6 = (bf16[4,1024,512]{2,1,0:T(8,128)(2,1)S(1)}, bf16[4,1024,512]{2,1,0:T(8,128)(2,1)}, u32[]{:S(2)}) copy-start(bf16[4,1024,512]{2,1,0:T(8,128)(2,1)} %param.22) | copy-start | bytes 12582916
  119.0 54.2 %all-to-all-start.2 = ((bf16[1,4,8,64,1024]{4,3,1,0,2:T(8,128)(2,1)}), bf16[1,4,8,64,1024]{4,3,1,0,2:T(8,128)(2,1)}, u32[]{:S(2)}, u32[]{:S(2)}) async-start(bf16[1,4,8,64,1024]{4,3,1,0,2:T(8,128)(2,1)} %copy.56), calls=%async_computation.2 | async-start | bytes 8388608 | tf_op jit(solution)/shard_map/all_to_all | solution.py:58
  173.2 12.3 %copy-start.1 = (bf16[128,8,1024]{2,1,0:T(8,128)(2,1)S(1)}, bf16[128,8,1024]{2,1,0:T(8,128)(2,1)}, u32[]{:S(2)}) copy-start(bf16[128,8,1024]{2,1,0:T(8,128)(2,1)} %param.17) | copy-start | bytes 6291460
where the time goes:
time: 186 us
  local copies, waits for them, and re-layouts  60.4 us (32%)
  waiting for transfers between devices  50.7 us (27%)
  matrix products  48.8 us (26%)
  starting transfers between devices  15 us (8%)
  other arithmetic  9.79 us (5%)
    all_to_all x1, waiting for transfers between devices, local_step(): lax.all_to_all(send_rows.reshape(n_dev, n_loc, cap_rows, model_dim), 'ep'...  47.1 us
    unnamed x22, local copies, waits for them, and re-layouts  21.2 us
    dot_general x1, matrix products, expert_grads(): jnp.einsum('erd,erf->edf', x_rows, grad_hgate, preferred_element_type=jnp...  9.89 us
    gather x1, local copies, waits for them, and re-layouts, build_send(): jnp.take(grad_y, row_source // top_k, axis=0, mode='fill', fill_value=0)  9.61 us
    dot_general x1, matrix products, expert_grads(): jnp.einsum('erd,erf->edf', x_rows, grad_hup, preferred_element_type=jnp.f...  9.4 us
    dot_general x1, matrix products, expert_grads(): jnp.einsum('erf,erd->efd', hidden_act, grad_rows, preferred_element_type=...  9.08 us
    gather x1, local copies, waits for them, and re-layouts, gather_back(): jnp.take(ret_rows, src_row, axis=0, mode='fill', fill_value=0)  8.9 us
    gather x1, local copies, waits for them, and re-layouts, build_send(): jnp.take(gate_vals.reshape(-1), row_source, mode='fill', fill_value=0)  8.58 us
  transfers between devices with their start and end apart: 3, of which 2 were waited for; matrix products, arithmetic and copies ran while one was open for 41% of the time, Pallas kernels for 0%

commit v1 on v0

v1 whole, which is shorter than its diff:
```python
import jax
import jax.numpy as jnp
from jax import lax
from jax.sharding import PartitionSpec as P


def solution(mesh):
    n_dev = mesh.shape["ep"]
    rows_spec = P(("dp", "ep"), None)
    cube_spec = P(("dp", "ep"), None, None)
    weight_spec = P("ep", None, None)

    def local_step(grad_y, gate_vals, topk_idx, slot_ids, pair_counts, y_routed, x_disp, h_gate, h_up, w_gate, w_up, w_down):
        n_loc = w_gate.shape[0]
        cap = x_disp.shape[1] // n_dev
        tok, model = grad_y.shape
        me = lax.axis_index("ep")
        gy_all = lax.all_gather(grad_y, "ep", axis=0)
        meta = jnp.stack([gate_vals.T, jnp.where(slot_ids >= 0, topk_idx * cap + slot_ids, -1).astype(jnp.float32).T], 0)
        meta_all = lax.all_gather(meta, "ep", axis=0)
        gates = meta_all[:, 0]
        dest = meta_all[:, 1].astype(jnp.int32) - me * (n_loc * cap)
        slot_iota = jnp.arange(n_loc * cap, dtype=jnp.int32)
        hit = dest[:, None, :, :] == slot_iota[None, :, None, None]
        sel = jnp.any(hit, axis=2)
        onehot = sel.astype(jnp.bfloat16)
        gate_row = jnp.sum(jnp.where(hit, gates[:, None], 0.0), axis=(2, 3))
        picked = jnp.einsum("srt,std->srd", onehot, gy_all, preferred_element_type=jnp.float32)
        d_rows = (gate_row[..., None] * picked).astype(jnp.bfloat16)
        d_rows = d_rows.reshape(n_dev, n_loc, cap, model).transpose(1, 0, 2, 3).reshape(n_loc, n_dev * cap, model)
        grad_gate = jnp.einsum("td,tkd->tk", grad_y, y_routed, preferred_element_type=jnp.float32)

        grad_hidden = jnp.einsum("erd,efd->erf", d_rows, w_down, preferred_element_type=jnp.float32).astype(jnp.bfloat16)
        gate_f = h_gate.astype(jnp.float32)
        up_f = h_up.astype(jnp.float32)
        gate_sig = jax.nn.sigmoid(gate_f)
        gate_act = gate_f * gate_sig
        hidden_act = (gate_act * up_f).astype(jnp.bfloat16)
        grad_h = grad_hidden.astype(jnp.float32)
        dh1 = (grad_h * up_f * gate_sig * (1.0 + gate_f * (1.0 - gate_sig))).astype(jnp.bfloat16)
        dh3 = (grad_h * gate_act).astype(jnp.bfloat16)
        r = (jnp.einsum("erf,edf->erd", dh1, w_gate, preferred_element_type=jnp.float32) + jnp.einsum("erf,edf->erd", dh3, w_up, preferred_element_type=jnp.float32)).astype(jnp.bfloat16)
        r = r.reshape(n_loc, n_dev, cap, model).transpose(1, 0, 2, 3).reshape(n_dev, n_loc * cap, model)
        part = jnp.einsum("srt,srd->std", onehot, r, preferred_element_type=jnp.float32)
        gx = lax.psum_scatter(part, "ep", scatter_dimension=0, tiled=False)
        grad_x = gx.astype(jnp.bfloat16)
        grad_wdown = jnp.einsum("erf,erd->efd", hidden_act, d_rows, preferred_element_type=jnp.float32)
        grad_wgate = jnp.einsum("erd,erf->edf", x_disp, dh1, preferred_element_type=jnp.float32)
        grad_wup = jnp.einsum("erd,erf->edf", x_disp, dh3, preferred_element_type=jnp.float32)
        return grad_x, grad_gate, grad_wgate, grad_wup, grad_wdown

    return jax.shard_map(local_step, mesh=mesh, in_specs=(rows_spec, rows_spec, rows_spec, rows_spec, rows_spec, cube_spec, cube_spec, cube_spec, cube_spec, weight_spec, weight_spec, weight_spec), out_specs=(rows_spec, rows_spec, cube_spec, cube_spec, cube_spec), check_vma=False)
```

time: 186 us -> 127 us (0.68)
  waiting for transfers between devices: 50.7 us -> 0.79 us
  local copies, waits for them, and re-layouts: 60.4 us -> 24.3 us
  blocking collectives: 0 us -> 24.4 us
  starting transfers between devices: 15 us -> 0.12 us
  between operations: 0.76 us -> 14.2 us
  matrix products: 48.8 us -> 52 us
    all_to_all x3 -> x0, waiting for transfers between devices: 50.7 us -> none  [the longest x1 47.1 us: local_step(): lax.all_to_all(send_rows.reshape(n_dev, n_loc, cap_rows, model_dim), 'ep'...]
    gather x3 -> x0, local copies, waits for them, and re-layouts: 27.1 us -> none  [the longest x1 9.61 us: build_send(): jnp.take(grad_y, row_source // top_k, axis=0, mode='fill', fill_value=0)]
    all_gather x0 -> x1, blocking collectives: none -> 24.4 us  [local_step(): meta_all = lax.all_gather(meta, 'ep', axis=0)]
    all_to_all x3 -> x0, starting transfers between devices: 15 us -> none  [the longest x1 5.3 us: local_step(): recv_counts = lax.all_to_all(pair_counts.reshape(n_dev, n_loc), 'ep', 0, 1)]
    scatter x1 -> x0, local copies, waits for them, and re-layouts: 4.32 us -> none  [build_send(): jnp.full((n_exp * cap_rows,), tok_dev * top_k, jnp.int32).at[dest_row]]
    reduce_or x0 -> x1, other arithmetic: none -> 3.8 us  [local_step(): sel = jnp.any(hit, axis=2)]
    another operation x2 -> x0, local copies, waits for them, and re-layouts: 3.37 us -> none  [the longest x1 2.69 us: local_step(): lax.all_to_all(grad_disp.reshape(n_loc, n_dev, cap_rows, model_dim), 'ep'...]
    dot_general x6 -> x8, matrix products: 47.5 us -> 50.6 us  [the longest x1 10.5 us: local_step(): jnp.einsum('erd,erf->edf', x_disp, dh1, preferred_element_type=jnp.float32)]
  transfers between devices with their start and end apart: 3 -> 2, of which waited for: 2 -> 0; matrix products, arithmetic and copies ran while one was open for 41% -> 45% of each run, Pallas kernels for 0% -> 0%
where the time goes in v1:
time: 127 us
  matrix products  52 us (41%)
  blocking collectives  24.4 us (19%)
  local copies, waits for them, and re-layouts  24.3 us (19%)
  between operations  14.2 us (11%)
  other arithmetic  11 us (9%)
    all_gather x1, blocking collectives, local_step(): meta_all = lax.all_gather(meta, 'ep', axis=0)  24.4 us
    unnamed x24, local copies, waits for them, and re-layouts  22.5 us
    dot_general x1, matrix products, local_step(): jnp.einsum('erd,erf->edf', x_disp, dh1, preferred_element_type=jnp.float32)  10.5 us
    dot_general x1, matrix products, local_step(): jnp.einsum('erf,erd->efd', hidden_act, d_rows, preferred_element_type=jnp...  9.53 us
    dot_general x1, matrix products, local_step(): jnp.einsum('erd,erf->edf', x_disp, dh3, preferred_element_type=jnp.float32)  8.76 us
    dot_general x1, matrix products, local_step(): jnp.einsum('erf,edf->erd', dh3, w_up, preferred_element_type=jnp.float32)  7.23 us
    dot_general x1, matrix products, local_step(): jnp.einsum('erf,edf->erd', dh1, w_gate, preferred_element_type=jnp.float32)  6.42 us
    reduce_sum x1, other arithmetic, local_step(): gate_row = jnp.sum(jnp.where(hit, gates[:, None], 0.0), axis=(2, 3))  3.98 us
  transfers between devices with their start and end apart: 2, of which 0 were waited for; matrix products, arithmetic and copies ran while one was open for 45% of the time, Pallas kernels for 0%

profile of v1, /device:TPU:112, one launch (start us, length us, event | category | flops | bytes accessed | tf_op | source)
XLA Modules:
  0.0 126.8 jit_solution(614291205256564804)
XLA Ops:
  7.2 0.0 copy-start
  7.2 0.1 all-gather.4.cloned.1.call-start
  7.3 0.7 all-gather.4.cloned.1.call-update
  8.0 0.1 reduce-scatter.2.cloned.1.call-start
  8.1 0.7 convert_bitcast_fusion.1
  8.8 0.7 pad_maximum_fusion
  9.5 24.4 %all-gather = f32[16,8,128]{2,1,0:T(8,128)S(1)} all-gather(f32[2,8,128]{2,1,0:T(8,128)S(1)} %pad_maximum_fusion), channel_id=2, replica_groups=mesh['dp'=2,'ep'=8] {'ep'}, dimensions={0}, use_global_device_ids=true | all-gather | bytes 73728 | tf_op jit(solution)/shard_map/all_gather | solution.py:20
  33.9 3.8 %fusion = pred[8,256,128]{2,1,0:T(8,128)(4,1)S(1)} fusion(s32[8,8,128]{2,1,0:T(8,128)S(1)} %fusion.15), kind=kLoop, calls=%fused_computation.4 | loop fusion | flops 3932160 | bytes 294912 | tf_op jit(solution)/shard_map/reduce_or | solution.py:25
  37.7 4.0 %select_reduce_fusion = f32[8,256]{1,0:T(8,128)S(1)} fusion(f32[8,8,128]{2,1,0:T(8,128)S(1)} %slice_bitcast_fusion, s32[8,8,128]{2,1,0:T(8,128)S(1)} %fusion.15), kind=kLoop, calls=%fused_computation.2 | loop fusion | flops 6289408 | bytes 73728 | tf_op jit(solution)/shard_map/reduce_sum | solution.py:27
  41.7 0.0 all-gather.4.cloned.1.call-done
  41.7 2.8 %multiply_convert_fusion = bf16[8,256,1024]{2,1,0:T(8,128)(2,1)S(1)} fusion(f32[8,256]{1,0:T(8,128)S(1)} %select_reduce_fusion, pred[8,256,128]{2,1,0:T(8,128)(4,1)S(1)} %fusion, bf16[8,128,1024]{2,1,0:T(8,128)(2,1)} %bitcast.46), kind=kOutput, calls=%fused_computation.1 | convolution fusion | flops 541065216 | bytes 6561792 | tf_op jit(solution)/shard_map/srt,std->srd/dot_general | solution.py:28
  44.6 0.0 copy-start.4
  44.6 0.7 copy.32
  45.3 0.0 copy-start.2
  45.3 2.0 %copy-done.2 = bf16[4,8,64,1024]{3,2,1,0:T(8,128)(2,1)} copy-done((bf16[4,8,64,1024]{3,2,1,0:T(8,128)(2,1)}, bf16[4,8,64,1024]{3,2,1,0:T(8,128)(2,1)S(1)}, u32[]{:S(2)}) %copy-start.2) | copy-done | bytes 4194328
  47.3 0.7 copy-done.4
  48.1 0.0 copy-start.5
  48.1 0.0 copy-start.7
  48.1 0.0 copy-start.8
  48.1 2.6 %convolution_convert_fusion = bf16[4,512,512]{2,1,0:T(8,128)(2,1)S(1)} fusion(bf16[4,512,1024]{2,1,0:T(8,128)(2,1)S(1)} %bitcast.43, bf16[4,512,1024]{2,1,0:T(8,128)(2,1)S(1)} %copy-done.4), kind=kOutput, calls=%fused_computation.23 | convolution fusion | flops 2148532224 | bytes 10485760 | tf_op jit(solution)/shard_map/erd,efd->erf/dot_general | solution.py:33
  50.6 0.0 copy-start.10
  50.6 1.3 %copy-done.10 = bf16[4,512,512]{2,1,0:T(8,128)(2,1)} copy-done((bf16[4,512,512]{2,1,0:T(8,128)(2,1)}, bf16[4,512,512]{2,1,0:T(8,128)(2,1)S(1)}, u32[]{:S(2)}) %copy-start.10) | copy-done | bytes 2097176
  51.9 0.0 copy-done.5
  51.9 0.0 copy-done.7
  51.9 0.0 copy-done.8
  52.0 0.0 copy-start.6
  52.0 6.4 %fusion.20 = f32[4,512,1024]{2,1,0:T(8,128)} fusion(bf16[4,1024,512]{2,1,0:T(8,128)(2,1)S(1)} %copy-done.5, bf16[4,512,512]{2,1,0:T(8,128)(2,1)S(1)} %copy-done.7, bf16[4,512,512]{2,1,0:T(8,128)(2,1)S(1)} %convolution_convert_fusion, bf16[4,512,512]{2,1,0:T(8,128)(2,1)S(1)} %copy-done.8), kind=kOutput, calls=%fused_computation.34 | convolution fusion | flops 2161115136 | bytes 18874368 | tf_op jit(solution)/shard_map/erf,edf->erd/dot_general | solution.py:42
  58.4 0.0 copy-done.6
  58.4 7.2 %add_convert_fusion = bf16[4,512,1024]{2,1,0:T(8,128)(2,1)S(1)} fusion(f32[4,512,1024]{2,1,0:T(8,128)} %fusion.20, bf16[4,1024,512]{2,1,0:T(8,128)(2,1)S(1)} %copy-done.6, bf16[4,512,512]{2,1,0:T(8,128)(2,1)} %copy-done.10, bf16[4,512,512]{2,1,0:T(8,128)(2,1)} %param.18), kind=kOutput, calls=%fused_computation | convolution fusion | flops 2160066560 | bytes 20971520 | tf_op jit(solution)/shard_map/erf,edf->erd/dot_general | solution.py:42
  65.6 0.4 copy.33
  66.1 2.7 %fusion.22 = f32[8,128,1024]{2,1,0:T(8,128)} fusion(pred[8,256,128]{2,1,0:T(8,128)(4,1)S(1)} %fusion, bf16[8,256,1024]{2,1,0:T(8,128)(2,1)S(1)} %bitcast.41), kind=kOutput, calls=%fused_computation.35 | convolution fusion | flops 536870912 | bytes 8650752 | tf_op jit(solution)/shard_map/srt,srd->std/dot_general | solution.py:44
  68.8 0.0 copy-start.3
  68.8 0.1 reduce-scatter.2.cloned.1.call-update
  68.9 0.0 copy-done
  68.9 0.9 copy-done.3
  69.8 1.4 %fusion.12 = f32[128,1,8]{2,1,0:T(1,128)S(1)} fusion(bf16[128,8,1024]{2,1,0:T(8,128)(2,1)S(1)} %copy-done, bf16[128,1024,1]{1,0,2:T(8,128)(2,1)S(1)} %bitcast.49), kind=kOutput, calls=%fused_computation.24 | convolution fusion | flops 2097152 | bytes 2363392 | tf_op jit(solution)/shard_map/td,tkd->tk/dot_general | solution.py:31
  71.1 0.7 copy.42
  71.8 10.5 %convolution_bitcast_fusion.1 = f32[4,1024,512]{1,2,0:T(8,128)} fusion(bf16[4,512,1024]{2,1,0:T(8,128)(2,1)} %param.17, bf16[4,512,512]{2,1,0:T(8,128)(2,1)} %param.19, bf16[4,512,512]{2,1,0:T(8,128)(2,1)} %copy-done.10, bf16[4,512,512]{2,1,0:T(8,128)(2,1)} %param.18), kind=kOutput, calls=%fused_computation.21 | convolution fusion | flops 2161115136 | bytes 18874368 | tf_op jit(solution)/shard_map/erd,erf->edf/dot_general | solution.py:48
  82.3 0.0 copy-start.9
  82.3 8.8 %copy.38 = f32[4,1024,512]{2,1,0:T(8,128)} copy(f32[4,1024,512]{1,2,0:T(8,128)} %convolution_bitcast_fusion.1) | data formatting | bytes 16777216
  91.1 0.0 copy-done.9
  91.1 8.8 %convolution_bitcast_fusion = f32[4,1024,512]{1,2,0:T(8,128)} fusion(bf16[4,512,1024]{2,1,0:T(8,128)(2,1)} %param.17, bf16[4,512,512]{2,1,0:T(8,128)(2,1)} %copy-done.10, bf16[4,512,512]{2,1,0:T(8,128)(2,1)S(1)} %copy-done.9), kind=kOutput, calls=%fused_computation.20 | convolution fusion | flops 2155872256 | bytes 16777216 | tf_op jit(solution)/shard_map/erd,erf->edf/dot_general | solution.py:49
  99.9 8.7 %copy.39 = f32[4,1024,512]{2,1,0:T(8,128)} copy(f32[4,1024,512]{1,2,0:T(8,128)} %convolution_bitcast_fusion) | data formatting | bytes 16777216
  108.6 0.0 copy-start.1
  108.6 9.5 %fusion.10 = f32[4,512,1024]{2,1,0:T(8,128)} fusion(bf16[4,512,1024]{2,1,0:T(8,128)(2,1)} %bitcast.44, bf16[4,512,512]{2,1,0:T(8,128)(2,1)} %param.19, bf16[4,512,512]{2,1,0:T(8,128)(2,1)} %param.18), kind=kOutput, calls=%fused_computation.22 | convolution fusion | flops 2155872256 | bytes 16777216 | tf_op jit(solution)/shard_map/erf,erd->efd/dot_general | solution.py:47
  118.1 0.0 reduce-scatter.2.cloned.1.call-done
  118.1 1.8 %convert_bitcast_fusion = bf16[128,1024]{1,0:T(8,128)(2,1)} fusion(f32[1,128,1024]{2,1,0:T(8,128)} %reduce-scatter.2.cloned.1.call-done), kind=kLoop, calls=%fused_computation.26 | loop fusion | flops 131072 | bytes 786432 | tf_op jit(solution)/shard_map/convert_element_type | solution.py:46
  119.9 0.0 copy-done.1
  (2 shorter events, 0.0 us)
Async XLA Ops:
  7.2 61.7 %copy-start = (bf16[128,8,1024]{2,1,0:T(8,128)(2,1)S(1)}, bf16[128,8,1024]{2,1,0:T(8,128)(2,1)}, u32[]{:S(2)}) copy-start(bf16[128,8,1024]{2,1,0:T(8,128)(2,1)} %param.16) | copy-start | bytes 6291460
  7.2 34.5 %all-gather.4.cloned.1.call-start = ((), (), s32[]{:S(2)}) async-start(), calls=%async_computation.2 | async-start | bytes 2359296 | tf_op jit(solution)/shard_map/all_gather | solution.py:18
  8.0 110.1 %reduce-scatter.2.cloned.1.call-start = ((), (), s32[]{:S(2)}) async-start(), calls=%async_computation.1 | async-start | bytes 4718592 | tf_op jit(solution)/shard_map/reduce_scatter | solution.py:45
  44.6 3.5 %copy-start.4 = (bf16[4,512,1024]{2,1,0:T(8,128)(2,1)S(1)}, bf16[4,512,1024]{2,1,0:T(8,128)(2,1)}, u32[]{:S(2)}) copy-start(bf16[4,512,1024]{2,1,0:T(8,128)(2,1)} %param.22) | copy-start | bytes 12582916
  45.3 2.0 %copy-start.2 = (bf16[4,8,64,1024]{3,2,1,0:T(8,128)(2,1)}, bf16[4,8,64,1024]{3,2,1,0:T(8,128)(2,1)S(1)}, u32[]{:S(2)}) copy-start(bf16[4,8,64,1024]{3,2,1,0:T(8,128)(2,1)S(1)} %copy.32) | copy-start | bytes 12582916
  48.1 3.9 %copy-start.5 = (bf16[4,1024,512]{2,1,0:T(8,128)(2,1)S(1)}, bf16[4,1024,512]{2,1,0:T(8,128)(2,1)}, u32[]{:S(2)}) copy-start(bf16[4,1024,512]{2,1,0:T(8,128)(2,1)} %param.20) | copy-start | bytes 12582916
  48.1 3.9 %copy-start.7 = (bf16[4,512,512]{2,1,0:T(8,128)(2,1)S(1)}, bf16[4,512,512]{2,1,0:T(8,128)(2,1)}, u32[]{:S(2)}) copy-start(bf16[4,512,512]{2,1,0:T(8,128)(2,1)} %param.19) | copy-start | bytes 6291460
  48.1 3.9 %copy-start.8 = (bf16[4,512,512]{2,1,0:T(8,128)(2,1)S(1)}, bf16[4,512,512]{2,1,0:T(8,128)(2,1)}, u32[]{:S(2)}) copy-start(bf16[4,512,512]{2,1,0:T(8,128)(2,1)} %param.18) | copy-start | bytes 6291460
  50.6 1.3 %copy-start.10 = (bf16[4,512,512]{2,1,0:T(8,128)(2,1)}, bf16[4,512,512]{2,1,0:T(8,128)(2,1)S(1)}, u32[]{:S(2)}) copy-start(bf16[4,512,512]{2,1,0:T(8,128)(2,1)S(1)} %convolution_convert_fusion) | copy-start | bytes 6291460
  52.0 6.4 %copy-start.6 = (bf16[4,1024,512]{2,1,0:T(8,128)(2,1)S(1)}, bf16[4,1024,512]{2,1,0:T(8,128)(2,1)}, u32[]{:S(2)}) copy-start(bf16[4,1024,512]{2,1,0:T(8,128)(2,1)} %param.21) | copy-start | bytes 12582916
  68.8 0.9 copy-start.3
  82.3 8.8 %copy-start.9 = (bf16[4,512,512]{2,1,0:T(8,128)(2,1)S(1)}, bf16[4,512,512]{2,1,0:T(8,128)(2,1)}, u32[]{:S(2)}) copy-start(bf16[4,512,512]{2,1,0:T(8,128)(2,1)} %param.18) | copy-start | bytes 6291460
  108.6 11.3 %copy-start.1 = (bf16[128,8,1024]{2,1,0:T(8,128)(2,1)S(1)}, bf16[128,8,1024]{2,1,0:T(8,128)(2,1)}, u32[]{:S(2)}) copy-start(bf16[128,8,1024]{2,1,0:T(8,128)(2,1)} %param.16) | copy-start | bytes 6291460
Sparse Core Ops, SparseCore 0:
  9.6 24.1 all-gather.3
  69.0 34.2 reduce-scatter.1

commit v2 on v1

v2 whole, which is shorter than its diff:
```python
import functools

import jax
import jax.numpy as jnp
from jax import lax
from jax.experimental import pallas as pl
from jax.experimental.pallas import tpu as pltpu
from jax.sharding import PartitionSpec as P

MESH = pl.DeviceIdType.MESH
F32 = jnp.float32
BF16 = jnp.bfloat16
NT = (((1,), (1,)), ((), ()))
TN = (((0,), (0,)), ((), ()))
SUBS = 2


def exchange_kernel(n_dev, cap, counts, gates, idx, slot, gy_hbm, yr_hbm, h1_hbm, h3_hbm, wg_hbm, wu_hbm, wd_hbm,
                    gx_out, gg_out, d_hbm, dh_hbm, a_hbm,
                    gy_all, yr, h1, h3, wcat, wd, fs, d_buf, dh_buf, a_buf, meta, pt, rbuf, own, psend, pairin, rsend, rrecv,
                    loc_sem, out_sem, meta_ssem, meta_rsem, ag_ssem, ag_rsem, pair_ssem, pair_rsem, ring_ssem, ring_rsem):
    n_loc, ffn, model = wd.shape
    top_k, tok = idx.shape
    n_chip = n_dev // 2
    half = model // 2
    hrow = tok // 2
    me = lax.axis_index("ep")
    x = me // 2
    c = me % 2
    partner = x * 2 + (1 - c)

    def chip(d):
        return (x + d + n_chip) % n_chip

    def dev(i):
        return {"ep": i}

    def load(src, dst, s):
        cp = pltpu.make_async_copy(src, dst, loc_sem.at[s])
        cp.start()
        return cp

    ld_gy = load(gy_hbm, gy_all.at[me], 0)
    ld_yr = load(yr_hbm, yr, 1)
    ld_h1 = load(h1_hbm, h1, 2)
    ld_h3 = load(h3_hbm, h3, 3)
    ld_wd = load(wd_hbm, wd, 4)
    ld_wg = load(wg_hbm, wcat.at[:, :, pl.ds(0, ffn)], 5)
    ld_wu = load(wu_hbm, wcat.at[:, :, pl.ds(ffn, ffn)], 6)

    cnt = jnp.zeros(idx.shape, jnp.int32)
    for e in range(n_loc * n_dev):
        cnt = jnp.where(idx[...] == e, counts[0, e], cnt)
    keep = (slot[...] >= 0) & (slot[...] < cnt)
    meta[me, 0] = gates[...]
    meta[me, 1] = jnp.where(keep, idx[...] * cap + slot[...], -1).astype(F32)

    barrier = pltpu.get_barrier_semaphore()
    for r in range(1, n_dev):
        pl.semaphore_signal(barrier, inc=1, device_id=dev((me + r) % n_dev), device_id_type=MESH)
    pl.semaphore_wait(barrier, n_dev - 1)

    meta_cp = []
    for r in range(1, n_dev):
        cp = pltpu.make_async_remote_copy(src_ref=meta.at[me], dst_ref=meta.at[me], send_sem=meta_ssem.at[r - 1], recv_sem=meta_rsem.at[r - 1],
                                          device_id=dev((me + r) % n_dev), device_id_type=MESH)
        cp.start()
        meta_cp.append(cp)

    def gy_copy(block, lo, n, s, to):
        ref = gy_all.at[block, pl.ds(lo, n), :]
        return pltpu.make_async_remote_copy(src_ref=ref, dst_ref=ref, send_sem=ag_ssem.at[s], recv_sem=ag_rsem.at[s], device_id=dev(to), device_id_type=MESH)

    right = chip(1) * 2 + c
    left = chip(-1) * 2 + c
    far = chip(2) * 2 + c
    ld_gy.wait()
    to_r0 = gy_copy(me, 0, hrow, 0, right)
    to_l1 = gy_copy(me, hrow, hrow, 1, left)
    to_r1 = gy_copy(me, hrow, hrow, 2, right)
    to_l0 = gy_copy(me, 0, hrow, 3, left)
    to_p = gy_copy(me, 0, tok, 4, partner)
    for cp in (to_r0, to_l1, to_p, to_r1, to_l0):
        cp.start()
    fw_r = gy_copy(left, 0, hrow, 5, right)
    fw_l = gy_copy(right, hrow, hrow, 6, left)
    p_l0 = gy_copy(left, 0, hrow, 7, partner)
    p_r1 = gy_copy(right, hrow, hrow, 8, partner)
    p_l1 = gy_copy(left, hrow, hrow, 9, partner)
    p_r0 = gy_copy(right, 0, hrow, 10, partner)
    p_f0 = gy_copy(far, 0, hrow, 11, partner)
    p_f1 = gy_copy(far, hrow, hrow, 12, partner)

    ld_yr.wait()
    step = 16

    @pl.loop(0, tok // step)
    def _(i):
        t = pl.multiple_of(i * step, step)
        g = gy_all[me, pl.ds(t, step), :].astype(F32)
        y = yr[pl.ds(t, step), :, :].astype(F32)
        gg_out[pl.ds(t, step), :] = jnp.sum(y * g[:, None, :], axis=2)

    ld_h1.wait()
    ld_h3.wait()
    rstep = 32

    @pl.loop(0, n_loc * (h1.shape[1] // rstep))
    def _(i):
        e = i // (h1.shape[1] // rstep)
        r = pl.multiple_of((i % (h1.shape[1] // rstep)) * rstep, rstep)
        a = h1[e, pl.ds(r, rstep), :].astype(F32)
        b = h3[e, pl.ds(r, rstep), :].astype(F32)
        g = jax.nn.sigmoid(a)
        s = a * g
        a_buf[e, pl.ds(r, rstep), :] = (s * b).astype(BF16)
        fs[e, pl.ds(r, rstep), pl.ds(0, ffn)] = b * g * (1.0 + a * (1.0 - g))
        fs[e, pl.ds(r, rstep), pl.ds(ffn, ffn)] = s

    out_a = pltpu.make_async_copy(a_buf, a_hbm, out_sem.at[0])
    out_a.start()

    to_r0.wait_recv()
    fw_r.start()
    p_l0.start()
    to_l1.wait_recv()
    fw_l.start()
    p_r1.start()
    for cp in meta_cp:
        cp.wait_recv()
    to_p.wait_recv()
    ld_wd.wait()
    ld_wg.wait()
    ld_wu.wait()

    def build(h):
        rel = meta[h, 1] - (me * (n_loc * cap)).astype(F32)
        gate = meta[h, 0]
        rows = lax.broadcasted_iota(jnp.int32, (n_loc * cap, tok), 0).astype(F32)
        sel = jnp.zeros((n_loc * cap, tok), F32)
        gsel = jnp.zeros((n_loc * cap, tok), F32)
        for k in range(top_k):
            hit = rows == rel[k:k + 1, :]
            sel = jnp.where(hit, 1.0, sel)
            gsel = jnp.where(hit, gate[k:k + 1, :], gsel)
        grow = jnp.sum(gsel, axis=1, keepdims=True)
        pt[h] = sel.T.astype(BF16)
        picked = jnp.dot(sel.astype(BF16), gy_all[h], preferred_element_type=F32)
        rows_d = (grow * picked).astype(BF16)
        for e in range(n_loc):
            d_buf[e, pl.ds(pl.multiple_of(h * cap, cap), cap), :] = rows_d[e * cap:(e + 1) * cap]

    def pair_copy(q, s, lo):
        return pltpu.make_async_remote_copy(src_ref=psend.at[q, :, pl.ds(lo, half)], dst_ref=pairin.at[q, :, pl.ds(lo, half)],
                                            send_sem=pair_ssem.at[s], recv_sem=pair_rsem.at[s], device_id=dev(partner), device_id_type=MESH)

    def unit(dists):
        qs = [chip(d) for d in dists]
        ns = len(qs)

        for q in qs:
            @pl.loop(0, 2)
            def _(i):
                build(q * 2 + i)

        def rows_of(ref, e, q, cols=None):
            rows = pl.ds(pl.multiple_of(q * (2 * cap), 2 * cap), 2 * cap)
            return ref[e, rows, :]

        @pl.loop(0, n_loc)
        def _(e):
            d = jnp.concatenate([rows_of(d_buf, e, q) for q in qs], axis=0)
            da = lax.dot_general(d, wd[e], NT, preferred_element_type=F32).astype(BF16).astype(F32)
            da2 = jnp.concatenate([da, da], axis=1)
            for i, q in enumerate(qs):
                dh = (da2[i * 2 * cap:(i + 1) * 2 * cap] * rows_of(fs, e, q)).astype(BF16)
                dh_buf[e, pl.ds(pl.multiple_of(q * (2 * cap), 2 * cap), 2 * cap), :] = dh

        copies = []
        for hf in range(2):
            @pl.loop(0, n_loc)
            def _(e):
                dh = jnp.concatenate([rows_of(dh_buf, e, q) for q in qs], axis=0)
                r = lax.dot_general(dh, wcat[e, pl.ds(hf * half, half), :], NT, preferred_element_type=F32).astype(BF16)
                for i in range(ns):
                    for j in range(2):
                        rbuf[i, j, pl.ds(pl.multiple_of(e * cap, cap), cap), pl.ds(hf * half, half)] = r[(i * 2 + j) * cap:(i * 2 + j + 1) * cap]

            for i, q in enumerate(qs):
                psend[q, :, pl.ds(hf * half, half)] = jnp.dot(pt[q * 2 + 1 - c], rbuf[i, 1 - c, :, pl.ds(hf * half, half)], preferred_element_type=F32)
            for i, q in enumerate(qs):
                own[q, :, pl.ds(hf * half, half)] = jnp.dot(pt[q * 2 + c], rbuf[i, c, :, pl.ds(hf * half, half)], preferred_element_type=F32)
            for i, d in enumerate(dists):
                cp = pair_copy(qs[i], ((d + n_chip) % n_chip) * 2 + hf, hf * half)
                cp.start()
                copies.append(cp)
        return copies

    pair_cps = {}
    pair_cps[0] = unit((0,))

    to_r1.wait_recv()
    p_l1.start()
    to_l0.wait_recv()
    p_r0.start()
    for cp in (p_l0, p_r1, p_l1, p_r0):
        cp.wait_recv()
    near = unit((-1, 1))
    pair_cps[-1] = [near[0], near[2]]
    pair_cps[1] = [near[1], near[3]]

    fw_r.wait_recv()
    p_f0.start()
    fw_l.wait_recv()
    p_f1.start()

    sub = tok // SUBS

    def ring_copy(dr, st, s):
        k = (dr * 3 + st) * SUBS + s
        return pltpu.make_async_remote_copy(src_ref=rsend.at[k], dst_ref=rrecv.at[k], send_sem=ring_ssem.at[k], recv_sem=ring_rsem.at[k],
                                            device_id=dev(right if dr == 0 else left), device_id_type=MESH)

    ring = {(dr, st, s): ring_copy(dr, st, s) for dr in range(2) for st in range(3) for s in range(SUBS)}
    dest = {0: (-1, 2, 1, 0), 1: (1, 2, -1, 0)}

    def ring_step(st):
        for dr in range(2):
            pair_cps[dest[dr][st]][dr].wait_recv()
        for s in range(SUBS):
            for dr in range(2):
                q = chip(dest[dr][st])
                rows, cols = pl.ds(s * sub, sub), pl.ds(dr * half, half)
                v = own[q, rows, cols] + pairin[q, rows, cols]
                if st > 0:
                    ring[dr, st - 1, s].wait_recv()
                    v = v + rrecv[(dr * 3 + st - 1) * SUBS + s]
                if st < 3:
                    rsend[(dr * 3 + st) * SUBS + s] = v
                    ring[dr, st, s].start()
                else:
                    gx_out[rows, cols] = v.astype(BF16)

    ring_step(0)
    p_f0.wait_recv()
    p_f1.wait_recv()
    pair_cps[2] = unit((2,))
    out_d = pltpu.make_async_copy(d_buf, d_hbm, out_sem.at[1])
    out_dh = pltpu.make_async_copy(dh_buf, dh_hbm, out_sem.at[2])
    out_d.start()
    out_dh.start()
    ring_step(1)
    ring_step(2)
    ring_step(3)

    for cp in meta_cp + [to_r0, to_l1, to_r1, to_l0, to_p, fw_r, fw_l, p_l0, p_r1, p_l1, p_r0, p_f0, p_f1]:
        cp.wait_send()
    for cps in pair_cps.values():
        for cp in cps:
            cp.wait_send()
    for cp in ring.values():
        cp.wait_send()
    out_a.wait()
    out_d.wait()
    out_dh.wait()


def weight_kernel(x_ref, dh_ref, a_ref, d_ref, gwg, gwu, gwd):
    ffn = gwg.shape[2]
    r = lax.dot_general(x_ref[0], dh_ref[0], TN, preferred_element_type=F32)
    gwg[0] = r[:, :ffn]
    gwu[0] = r[:, ffn:]
    gwd[0] = lax.dot_general(a_ref[0], d_ref[0], TN, preferred_element_type=F32)


def solution(mesh):
    n_dev = mesh.shape["ep"]
    rows_spec = P(("dp", "ep"), None)
    cube_spec = P(("dp", "ep"), None, None)
    weight_spec = P("ep", None, None)

    def local_step(grad_y, gate_vals, topk_idx, slot_ids, pair_counts, y_routed, x_disp, h_gate, h_up, w_gate, w_up, w_down):
        n_loc, ffn, model = w_down.shape
        tok, top_k = topk_idx.shape
        rows = x_disp.shape[1]
        cap = rows // n_dev
        n_chip = n_dev // 2
        vm = pl.BlockSpec(memory_space=pltpu.VMEM)
        hbm = pl.BlockSpec(memory_space=pl.ANY)
        dma = pltpu.SemaphoreType.DMA
        gx, gg, d_rows, dh, act = pl.pallas_call(
            functools.partial(exchange_kernel, n_dev, cap),
            out_shape=(jax.ShapeDtypeStruct((tok, model), BF16), jax.ShapeDtypeStruct((tok, top_k), F32),
                       jax.ShapeDtypeStruct((n_loc, rows, model), BF16), jax.ShapeDtypeStruct((n_loc, rows, 2 * ffn), BF16),
                       jax.ShapeDtypeStruct((n_loc, rows, ffn), BF16)),
            in_specs=[pl.BlockSpec(memory_space=pltpu.SMEM), vm, vm, vm] + [hbm] * 7,
            out_specs=(vm, vm, hbm, hbm, hbm),
            scratch_shapes=[
                pltpu.VMEM((n_dev, tok, model), BF16),
                pltpu.VMEM((tok, top_k, model), BF16),
                pltpu.VMEM((n_loc, rows, ffn), BF16),
                pltpu.VMEM((n_loc, rows, ffn), BF16),
                pltpu.VMEM((n_loc, model, 2 * ffn), BF16),
                pltpu.VMEM((n_loc, ffn, model), BF16),
                pltpu.VMEM((n_loc, rows, 2 * ffn), F32),
                pltpu.VMEM((n_loc, rows, model), BF16),
                pltpu.VMEM((n_loc, rows, 2 * ffn), BF16),
                pltpu.VMEM((n_loc, rows, ffn), BF16),
                pltpu.VMEM((n_dev, 2, top_k, tok), F32),
                pltpu.VMEM((n_dev, tok, n_loc * cap), BF16),
                pltpu.VMEM((2, 2, n_loc * cap, model), BF16),
                pltpu.VMEM((n_chip, tok, model), F32),
                pltpu.VMEM((n_chip, tok, model), F32),
                pltpu.VMEM((n_chip, tok, model), F32),
                pltpu.VMEM((6 * SUBS, tok // SUBS, model // 2), F32),
                pltpu.VMEM((6 * SUBS, tok // SUBS, model // 2), F32),
                dma((7,)), dma((3,)), dma((n_dev - 1,)), dma((n_dev - 1,)), dma((13,)), dma((13,)),
                dma((2 * n_chip,)), dma((2 * n_chip,)), dma((6 * SUBS,)), dma((6 * SUBS,)),
            ],
            compiler_params=pltpu.CompilerParams(collective_id=0, has_side_effects=True, vmem_limit_bytes=62 * 1024 * 1024),
            name="exchange",
        )(pair_counts, gate_vals.T, topk_idx.T, slot_ids.T, grad_y, y_routed, h_gate, h_up, w_gate, w_up, w_down)
        js = 2
        gwg, gwu, gwd = pl.pallas_call(
            weight_kernel,
            grid=(n_loc, js),
            out_shape=(jax.ShapeDtypeStruct((n_loc, model, ffn), F32), jax.ShapeDtypeStruct((n_loc, model, ffn), F32),
                       jax.ShapeDtypeStruct((n_loc, ffn, model), F32)),
            in_specs=[pl.BlockSpec((1, rows, model // js), lambda e, j: (e, 0, j)), pl.BlockSpec((1, rows, 2 * ffn), lambda e, j: (e, 0, 0)),
                      pl.BlockSpec((1, rows, ffn // js), lambda e, j: (e, 0, j)), pl.BlockSpec((1, rows, model), lambda e, j: (e, 0, 0))],
            out_specs=(pl.BlockSpec((1, model // js, ffn), lambda e, j: (e, j, 0)), pl.BlockSpec((1, model // js, ffn), lambda e, j: (e, j, 0)),
                       pl.BlockSpec((1, ffn // js, model), lambda e, j: (e, j, 0))),
            compiler_params=pltpu.CompilerParams(dimension_semantics=("arbitrary", "arbitrary")),
            name="weights",
        )(x_disp, dh, act, d_rows)
        return gx, gg, gwg, gwu, gwd

    return jax.shard_map(local_step, mesh=mesh, in_specs=(rows_spec, rows_spec, rows_spec, rows_spec, rows_spec, cube_spec, cube_spec, cube_spec, cube_spec, weight_spec, weight_spec, weight_spec), out_specs=(rows_spec, rows_spec, cube_spec, cube_spec, cube_spec), check_vma=False)
```

time: 127 us -> 75.9 us (0.60)
  Pallas kernels: 0 us -> 72.3 us
  matrix products: 52 us -> 0 us
  blocking collectives: 24.4 us -> 0 us
  local copies, waits for them, and re-layouts: 24.3 us -> 2.21 us
  between operations: 14.2 us -> 0.65 us
  other arithmetic: 11 us -> 0 us
    pallas_call x0 -> x2, Pallas kernels: none -> 72.3 us  [the longest x1 52.9 us: local_step(): pl.pallas_call(functools.partial(exchange_kernel, n_dev, cap), out_shape=...]
    dot_general x9 -> x0, matrix products: 52 us -> none  [the longest x1 10.5 us: local_step(): jnp.einsum('erd,erf->edf', x_disp, dh1, preferred_element_type=jnp.float32)]
    all_gather x1 -> x0, blocking collectives: 24.4 us -> none  [local_step(): meta_all = lax.all_gather(meta, 'ep', axis=0)]
    unnamed x24 -> x4, local copies, waits for them, and re-layouts: 22.5 us -> 2.21 us
    reduce_sum x1 -> x0, other arithmetic: 3.98 us -> none  [local_step(): gate_row = jnp.sum(jnp.where(hit, gates[:, None], 0.0), axis=(2, 3))]
    reduce_or x1 -> x0, other arithmetic: 3.8 us -> none  [local_step(): sel = jnp.any(hit, axis=2)]
    convert_element_type x1 -> x0, other arithmetic: 1.78 us -> none  [local_step(): grad_x = gx.astype(jnp.bfloat16)]
    another operation x2 -> x0, other arithmetic: 1.4 us -> none  [local_step(): jnp.stack([gate_vals.T, jnp.where(slot_ids >= 0, topk_idx * cap + slot_id...]
  transfers between devices with their start and end apart: 2 -> 0, of which waited for: 0 -> 0; matrix products, arithmetic and copies ran while one was open for 45% -> 0% of each run, Pallas kernels for 0% -> 0%
where the time goes in v2:
time: 75.9 us; the launch traced here: 75.1 us
  Pallas kernels  72.3 us (95%)
  local copies, waits for them, and re-layouts  2.21 us (3%)
    pallas_call x1, Pallas kernels, local_step(): pl.pallas_call(functools.partial(exchange_kernel, n_dev, cap), out_shape=...  52.9 us
    pallas_call x1, Pallas kernels, local_step(): pl.pallas_call(weight_kernel, grid=(n_loc, js), out_shape=(jax.ShapeDtype...  19.4 us
    unnamed x4, local copies, waits for them, and re-layouts  2.21 us

profile of v2, /device:TPU:112, one launch (start us, length us, event | category | flops | bytes accessed | tf_op | source)
XLA Modules:
  0.0 75.1 jit_solution(18430938448103757285)
XLA Ops:
  0.6 52.9 %exchange.1 = (bf16[128,1024]{1,0:T(8,128)(2,1)}, f32[128,8]{1,0:T(8,128)}, bf16[4,512,1024]{2,1,0:T(8,128)(2,1)}, bf16[4,512,1024]{2,1,0:T(8,128)(2,1)}, bf16[4,512,512]{2,1,0:T(8,128)(2,1)}) custom-call(s32[1,32]{1,0:T(1,128)} %counts.1, f32[8,128]{1,0:T(8,128)} %bitcast.3, s32[8,128]{1,0:T(8,128)} %bitcast.4, s32[8,128]{1,0:T(8,128)} %bitcast.5, ...), custom_call_target="tpu_custom_call" | custom-call | tf_op jit(solution)/shard_map/exchange/pallas_call | solution.py:291
  53.5 1.5 %copy.17 = f32[128,8]{0,1:T(8,128)} copy(f32[128,8]{1,0:T(8,128)} %get-tuple-element.22) | data formatting | bytes 8192
  55.0 0.0 copy-start
  55.0 19.4 %weights.1 = (f32[4,1024,512]{2,1,0:T(8,128)}, f32[4,1024,512]{2,1,0:T(8,128)}, f32[4,512,1024]{2,1,0:T(8,128)}) custom-call(bf16[4,512,1024]{2,1,0:T(8,128)(2,1)} %x_ref.1, bf16[4,512,1024]{2,1,0:T(8,128)(2,1)} %get-tuple-element.15.dh_ref, bf16[4,512,512]{2,1,0:T(8,128)(2,1)} %get-tuple-element.16.a_ref, bf16[4,512,1024]{2,1,0:T(8,128)(2,1)} %get-tuple-element.17.d_ref), custom_call_target="tpu_custom_call" | custom-call | tf_op jit(solution)/shard_map/weights/pallas_call | solution.py:324
  74.4 0.0 copy-done
  74.4 0.7 copy.19
Async XLA Ops:
  55.0 19.4 %copy-start = (bf16[128,1024]{1,0:T(8,128)(2,1)S(1)}, bf16[128,1024]{1,0:T(8,128)(2,1)}, u32[]{:S(2)}) copy-start(bf16[128,1024]{1,0:T(8,128)(2,1)} %get-tuple-element.31) | copy-start | bytes 786436

commit v3 on v2

--- a/solution.py
+++ b/solution.py
@@ -15,10 +15,10 @@
 SUBS = 2
 
 
-def exchange_kernel(n_dev, cap, counts, gates, idx, slot, gy_hbm, yr_hbm, h1_hbm, h3_hbm, wg_hbm, wu_hbm, wd_hbm,
-                    gx_out, gg_out, d_hbm, dh_hbm, a_hbm,
-                    gy_all, yr, h1, h3, wcat, wd, fs, d_buf, dh_buf, a_buf, meta, pt, rbuf, own, psend, pairin, rsend, rrecv,
-                    loc_sem, out_sem, meta_ssem, meta_rsem, ag_ssem, ag_rsem, pair_ssem, pair_rsem, ring_ssem, ring_rsem):
+def exchange_kernel(n_dev, cap, counts, gates, idx, slot, gy_hbm, yr_hbm, h1_hbm, h3_hbm, wg_hbm, wu_hbm, wd_hbm, x_hbm,
+                    gx_out, gg_out, d_buf, dh_buf, a_buf, x_buf,
+                    gy_all, yr, h1, h3, wcat, wd, fs, gg_rows, meta, pt, rbuf, own, psend, pairin, rsend, rrecv,
+                    loc_sem, meta_ssem, meta_rsem, ag_ssem, ag_rsem, pair_ssem, pair_rsem, ring_ssem, ring_rsem):
     n_loc, ffn, model = wd.shape
     top_k, tok = idx.shape
     n_chip = n_dev // 2
@@ -99,7 +99,9 @@
         t = pl.multiple_of(i * step, step)
         g = gy_all[me, pl.ds(t, step), :].astype(F32)
         y = yr[pl.ds(t, step), :, :].astype(F32)
-        gg_out[pl.ds(t, step), :] = jnp.sum(y * g[:, None, :], axis=2)
+        gg_rows[pl.ds(t, step), :] = jnp.sum(y * g[:, None, :], axis=2)
+
+    gg_out[...] = gg_rows[...].T
 
     ld_h1.wait()
     ld_h3.wait()
@@ -117,8 +119,6 @@
         fs[e, pl.ds(r, rstep), pl.ds(0, ffn)] = b * g * (1.0 + a * (1.0 - g))
         fs[e, pl.ds(r, rstep), pl.ds(ffn, ffn)] = s
 
-    out_a = pltpu.make_async_copy(a_buf, a_hbm, out_sem.at[0])
-    out_a.start()
 
     to_r0.wait_recv()
     fw_r.start()
@@ -196,6 +196,7 @@
                 copies.append(cp)
         return copies
 
+    ld_x = load(x_hbm, x_buf, 7)
     pair_cps = {}
     pair_cps[0] = unit((0,))
 
@@ -245,10 +246,6 @@
     p_f0.wait_recv()
     p_f1.wait_recv()
     pair_cps[2] = unit((2,))
-    out_d = pltpu.make_async_copy(d_buf, d_hbm, out_sem.at[1])
-    out_dh = pltpu.make_async_copy(dh_buf, dh_hbm, out_sem.at[2])
-    out_d.start()
-    out_dh.start()
     ring_step(1)
     ring_step(2)
     ring_step(3)
@@ -260,17 +257,39 @@
             cp.wait_send()
     for cp in ring.values():
         cp.wait_send()
-    out_a.wait()
-    out_d.wait()
-    out_dh.wait()
-
-
-def weight_kernel(x_ref, dh_ref, a_ref, d_ref, gwg, gwu, gwd):
-    ffn = gwg.shape[2]
-    r = lax.dot_general(x_ref[0], dh_ref[0], TN, preferred_element_type=F32)
-    gwg[0] = r[:, :ffn]
-    gwu[0] = r[:, ffn:]
-    gwd[0] = lax.dot_general(a_ref[0], d_ref[0], TN, preferred_element_type=F32)
+    ld_x.wait()
+
+
+def weight_kernel(js, x_ref, dh_ref, a_ref, d_ref, gx_ref, gg_ref, gx_out, gg_out, gwg, gwu, gwd, gbuf, dbuf, sem):
+    n_loc, model, ffn = gwg.shape
+    xc, ac = model // js, ffn // js
+    gx_out[...] = gx_ref[...]
+    gg_out[...] = gg_ref[...]
+
+    def copies(i):
+        e, j, b = i // js, i % js, i % 2
+        rows, arows = pl.ds(pl.multiple_of(j * xc, xc), xc), pl.ds(pl.multiple_of(j * ac, ac), ac)
+        return (pltpu.make_async_copy(gbuf.at[b, :, pl.ds(0, ffn)], gwg.at[e, rows, :], sem.at[b, 0]),
+                pltpu.make_async_copy(gbuf.at[b, :, pl.ds(ffn, ffn)], gwu.at[e, rows, :], sem.at[b, 1]),
+                pltpu.make_async_copy(dbuf.at[b], gwd.at[e, arows, :], sem.at[b, 2]))
+
+    @pl.loop(0, n_loc * js)
+    def _(i):
+        e, j, b = i // js, i % js, i % 2
+
+        @pl.when(i >= 2)
+        def _():
+            for cp in copies(i - 2):
+                cp.wait()
+
+        gbuf[b] = lax.dot_general(x_ref[e, :, pl.ds(pl.multiple_of(j * xc, xc), xc)], dh_ref[e], TN, preferred_element_type=F32)
+        dbuf[b] = lax.dot_general(a_ref[e, :, pl.ds(pl.multiple_of(j * ac, ac), ac)], d_ref[e], TN, preferred_element_type=F32)
+        for cp in copies(i):
+            cp.start()
+
+    for i in range(n_loc * js - 2, n_loc * js):
+        for cp in copies(i):
+            cp.wait()
 
 
 def solution(mesh):
@@ -288,13 +307,12 @@
         vm = pl.BlockSpec(memory_space=pltpu.VMEM)
         hbm = pl.BlockSpec(memory_space=pl.ANY)
         dma = pltpu.SemaphoreType.DMA
-        gx, gg, d_rows, dh, act = pl.pallas_call(
+        gx, gg, d_rows, dh, act, x_rows = pl.pallas_call(
             functools.partial(exchange_kernel, n_dev, cap),
-            out_shape=(jax.ShapeDtypeStruct((tok, model), BF16), jax.ShapeDtypeStruct((tok, top_k), F32),
-                       jax.ShapeDtypeStruct((n_loc, rows, model), BF16), jax.ShapeDtypeStruct((n_loc, rows, 2 * ffn), BF16),
-                       jax.ShapeDtypeStruct((n_loc, rows, ffn), BF16)),
-            in_specs=[pl.BlockSpec(memory_space=pltpu.SMEM), vm, vm, vm] + [hbm] * 7,
-            out_specs=(vm, vm, hbm, hbm, hbm),
+            out_shape=(pltpu.VMEM((tok, model), BF16), pltpu.VMEM((top_k, tok), F32), pltpu.VMEM((n_loc, rows, model), BF16),
+                       pltpu.VMEM((n_loc, rows, 2 * ffn), BF16), pltpu.VMEM((n_loc, rows, ffn), BF16), pltpu.VMEM((n_loc, rows, model), BF16)),
+            in_specs=[pl.BlockSpec(memory_space=pltpu.SMEM), vm, vm, vm] + [hbm] * 8,
+            out_specs=(vm,) * 6,
             scratch_shapes=[
                 pltpu.VMEM((n_dev, tok, model), BF16),
                 pltpu.VMEM((tok, top_k, model), BF16),
@@ -303,9 +321,7 @@
                 pltpu.VMEM((n_loc, model, 2 * ffn), BF16),
                 pltpu.VMEM((n_loc, ffn, model), BF16),
                 pltpu.VMEM((n_loc, rows, 2 * ffn), F32),
-                pltpu.VMEM((n_loc, rows, model), BF16),
-                pltpu.VMEM((n_loc, rows, 2 * ffn), BF16),
-                pltpu.VMEM((n_loc, rows, ffn), BF16),
+                pltpu.VMEM((tok, top_k), F32),
                 pltpu.VMEM((n_dev, 2, top_k, tok), F32),
                 pltpu.VMEM((n_dev, tok, n_loc * cap), BF16),
                 pltpu.VMEM((2, 2, n_loc * cap, model), BF16),
@@ -314,25 +330,23 @@
                 pltpu.VMEM((n_chip, tok, model), F32),
                 pltpu.VMEM((6 * SUBS, tok // SUBS, model // 2), F32),
                 pltpu.VMEM((6 * SUBS, tok // SUBS, model // 2), F32),
-                dma((7,)), dma((3,)), dma((n_dev - 1,)), dma((n_dev - 1,)), dma((13,)), dma((13,)),
+                dma((8,)), dma((n_dev - 1,)), dma((n_dev - 1,)), dma((13,)), dma((13,)),
                 dma((2 * n_chip,)), dma((2 * n_chip,)), dma((6 * SUBS,)), dma((6 * SUBS,)),
             ],
-            compiler_params=pltpu.CompilerParams(collective_id=0, has_side_effects=True, vmem_limit_bytes=62 * 1024 * 1024),
+            compiler_params=pltpu.CompilerParams(collective_id=0, has_side_effects=True, vmem_limit_bytes=44 * 1024 * 1024),
             name="exchange",
-        )(pair_counts, gate_vals.T, topk_idx.T, slot_ids.T, grad_y, y_routed, h_gate, h_up, w_gate, w_up, w_down)
+        )(pair_counts, gate_vals.T, topk_idx.T, slot_ids.T, grad_y, y_routed, h_gate, h_up, w_gate, w_up, w_down, x_disp)
         js = 2
-        gwg, gwu, gwd = pl.pallas_call(
-            weight_kernel,
-            grid=(n_loc, js),
-            out_shape=(jax.ShapeDtypeStruct((n_loc, model, ffn), F32), jax.ShapeDtypeStruct((n_loc, model, ffn), F32),
-                       jax.ShapeDtypeStruct((n_loc, ffn, model), F32)),
-            in_specs=[pl.BlockSpec((1, rows, model // js), lambda e, j: (e, 0, j)), pl.BlockSpec((1, rows, 2 * ffn), lambda e, j: (e, 0, 0)),
-                      pl.BlockSpec((1, rows, ffn // js), lambda e, j: (e, 0, j)), pl.BlockSpec((1, rows, model), lambda e, j: (e, 0, 0))],
-            out_specs=(pl.BlockSpec((1, model // js, ffn), lambda e, j: (e, j, 0)), pl.BlockSpec((1, model // js, ffn), lambda e, j: (e, j, 0)),
-                       pl.BlockSpec((1, ffn // js, model), lambda e, j: (e, j, 0))),
-            compiler_params=pltpu.CompilerParams(dimension_semantics=("arbitrary", "arbitrary")),
+        gx, gg, gwg, gwu, gwd = pl.pallas_call(
+            functools.partial(weight_kernel, js),
+            out_shape=(jax.ShapeDtypeStruct((tok, model), BF16), jax.ShapeDtypeStruct((top_k, tok), F32), jax.ShapeDtypeStruct((n_loc, model, ffn), F32),
+                       jax.ShapeDtypeStruct((n_loc, model, ffn), F32), jax.ShapeDtypeStruct((n_loc, ffn, model), F32)),
+            in_specs=[vm] * 6,
+            out_specs=(vm, vm, hbm, hbm, hbm),
+            scratch_shapes=[pltpu.VMEM((2, model // js, 2 * ffn), F32), pltpu.VMEM((2, ffn // js, model), F32), dma((2, 3))],
+            compiler_params=pltpu.CompilerParams(vmem_limit_bytes=20 * 1024 * 1024),
             name="weights",
-        )(x_disp, dh, act, d_rows)
-        return gx, gg, gwg, gwu, gwd
+        )(x_rows, dh, act, d_rows, gx, gg)
+        return gx, gg.T, gwg, gwu, gwd
 
     return jax.shard_map(local_step, mesh=mesh, in_specs=(rows_spec, rows_spec, rows_spec, rows_spec, rows_spec, cube_spec, cube_spec, cube_spec, cube_spec, weight_spec, weight_spec, weight_spec), out_specs=(rows_spec, rows_spec, cube_spec, cube_spec, cube_spec), check_vma=False)

time: 75.9 us -> 65 us (0.86)
  Pallas kernels: 72.3 us -> 63.8 us
  local copies, waits for them, and re-layouts: 2.21 us -> 0 us
    pallas_call x1, Pallas kernels: 19.4 us -> 11.5 us  [local_step(): pl.pallas_call(functools.partial(weight_kernel, js), out_shape=(jax.Shape...]
    unnamed x4 -> x0, local copies, waits for them, and re-layouts: 2.21 us -> none
where the time goes in v3:
time: 65 us; the launch traced here: 64.4 us
  Pallas kernels  63.8 us (98%)
    pallas_call x1, Pallas kernels, local_step(): pl.pallas_call(functools.partial(exchange_kernel, n_dev, cap), out_shape=...  52.3 us
    pallas_call x1, Pallas kernels, local_step(): pl.pallas_call(functools.partial(weight_kernel, js), out_shape=(jax.Shape...  11.5 us

profile of v3, /device:TPU:112, one launch (start us, length us, event | category | flops | bytes accessed | tf_op | source)
XLA Modules:
  0.0 64.4 jit_solution(15985784649674664782)
XLA Ops:
  0.6 52.3 %exchange.1 = (bf16[128,1024]{1,0:T(8,128)(2,1)S(1)}, f32[8,128]{1,0:T(8,128)S(1)}, bf16[4,512,1024]{2,1,0:T(8,128)(2,1)S(1)}, bf16[4,512,1024]{2,1,0:T(8,128)(2...) custom-call(s32[1,32]{1,0:T(1,128)} %counts.1, f32[8,128]{1,0:T(8,128)} %bitcast.4, ...), custom_call_target="tpu_custom_call" | custom-call | tf_op jit(solution)/shard_map/exchange/pallas_call | solution.py:310
  52.9 11.5 %weights.1 = (bf16[128,1024]{1,0:T(8,128)(2,1)}, f32[8,128]{1,0:T(8,128)}, f32[4,1024,512]{2,1,0:T(8,128)}, f32[4,1024,512]{2,1,0:T(8,128)}, f32[4,512,1024]{2,1,0:T(8,128)}) custom-call(bf16[4,512,1024]{2,1,0:T(8,128)(2,1)S(1)} %get-tuple-element.16.x_ref, bf16[4,512,1024]{2,1,0:T(8,128)(2,1)S(1)} %get-tuple-element.17.dh_ref, ...), custom_call_target="tpu_custom_call" | custom-call | tf_op jit(solution)/shard_map/weights/pallas_call | solution.py:340

commit v4 on v3

--- a/solution.py
+++ b/solution.py
@@ -41,7 +41,6 @@
         return cp
 
     ld_gy = load(gy_hbm, gy_all.at[me], 0)
-    ld_yr = load(yr_hbm, yr, 1)
     ld_h1 = load(h1_hbm, h1, 2)
     ld_h3 = load(h3_hbm, h3, 3)
     ld_wd = load(wd_hbm, wd, 4)
@@ -91,18 +90,6 @@
     p_f0 = gy_copy(far, 0, hrow, 11, partner)
     p_f1 = gy_copy(far, hrow, hrow, 12, partner)
 
-    ld_yr.wait()
-    step = 16
-
-    @pl.loop(0, tok // step)
-    def _(i):
-        t = pl.multiple_of(i * step, step)
-        g = gy_all[me, pl.ds(t, step), :].astype(F32)
-        y = yr[pl.ds(t, step), :, :].astype(F32)
-        gg_rows[pl.ds(t, step), :] = jnp.sum(y * g[:, None, :], axis=2)
-
-    gg_out[...] = gg_rows[...].T
-
     ld_h1.wait()
     ld_h3.wait()
     rstep = 32
@@ -119,19 +106,6 @@
         fs[e, pl.ds(r, rstep), pl.ds(0, ffn)] = b * g * (1.0 + a * (1.0 - g))
         fs[e, pl.ds(r, rstep), pl.ds(ffn, ffn)] = s
 
-
-    to_r0.wait_recv()
-    fw_r.start()
-    p_l0.start()
-    to_l1.wait_recv()
-    fw_l.start()
-    p_r1.start()
-    for cp in meta_cp:
-        cp.wait_recv()
-    to_p.wait_recv()
-    ld_wd.wait()
-    ld_wg.wait()
-    ld_wu.wait()
 
     def build(h):
         rel = meta[h, 1] - (me * (n_loc * cap)).astype(F32)
@@ -154,19 +128,10 @@
         return pltpu.make_async_remote_copy(src_ref=psend.at[q, :, pl.ds(lo, half)], dst_ref=pairin.at[q, :, pl.ds(lo, half)],
                                             send_sem=pair_ssem.at[s], recv_sem=pair_rsem.at[s], device_id=dev(partner), device_id_type=MESH)
 
-    def unit(dists):
-        qs = [chip(d) for d in dists]
-        ns = len(qs)
-
-        for q in qs:
-            @pl.loop(0, 2)
-            def _(i):
-                build(q * 2 + i)
-
-        def rows_of(ref, e, q, cols=None):
-            rows = pl.ds(pl.multiple_of(q * (2 * cap), 2 * cap), 2 * cap)
-            return ref[e, rows, :]
-
+    def rows_of(ref, e, q):
+        return ref[e, pl.ds(pl.multiple_of(q * (2 * cap), 2 * cap), 2 * cap), :]
+
+    def hidden(qs):
         @pl.loop(0, n_loc)
         def _(e):
             d = jnp.concatenate([rows_of(d_buf, e, q) for q in qs], axis=0)
@@ -176,46 +141,29 @@
                 dh = (da2[i * 2 * cap:(i + 1) * 2 * cap] * rows_of(fs, e, q)).astype(BF16)
                 dh_buf[e, pl.ds(pl.multiple_of(q * (2 * cap), 2 * cap), 2 * cap), :] = dh
 
-        copies = []
-        for hf in range(2):
-            @pl.loop(0, n_loc)
-            def _(e):
-                dh = jnp.concatenate([rows_of(dh_buf, e, q) for q in qs], axis=0)
-                r = lax.dot_general(dh, wcat[e, pl.ds(hf * half, half), :], NT, preferred_element_type=F32).astype(BF16)
-                for i in range(ns):
-                    for j in range(2):
-                        rbuf[i, j, pl.ds(pl.multiple_of(e * cap, cap), cap), pl.ds(hf * half, half)] = r[(i * 2 + j) * cap:(i * 2 + j + 1) * cap]
-
-            for i, q in enumerate(qs):
-                psend[q, :, pl.ds(hf * half, half)] = jnp.dot(pt[q * 2 + 1 - c], rbuf[i, 1 - c, :, pl.ds(hf * half, half)], preferred_element_type=F32)
-            for i, q in enumerate(qs):
-                own[q, :, pl.ds(hf * half, half)] = jnp.dot(pt[q * 2 + c], rbuf[i, c, :, pl.ds(hf * half, half)], preferred_element_type=F32)
-            for i, d in enumerate(dists):
-                cp = pair_copy(qs[i], ((d + n_chip) % n_chip) * 2 + hf, hf * half)
-                cp.start()
-                copies.append(cp)
-        return copies
-
-    ld_x = load(x_hbm, x_buf, 7)
     pair_cps = {}
-    pair_cps[0] = unit((0,))
-
-    to_r1.wait_recv()
-    p_l1.start()
-    to_l0.wait_recv()
-    p_r0.start()
-    for cp in (p_l0, p_r1, p_l1, p_r0):
-        cp.wait_recv()
-    near = unit((-1, 1))
-    pair_cps[-1] = [near[0], near[2]]
-    pair_cps[1] = [near[1], near[3]]
-
-    fw_r.wait_recv()
-    p_f0.start()
-    fw_l.wait_recv()
-    p_f1.start()
-
-    sub = tok // SUBS
+
+    def back(dists, qs, hf):
+        cols = pl.ds(hf * half, half)
+
+        @pl.loop(0, n_loc)
+        def _(e):
+            dh = jnp.concatenate([rows_of(dh_buf, e, q) for q in qs], axis=0)
+            r = lax.dot_general(dh, wcat[e, cols, :], NT, preferred_element_type=F32).astype(BF16)
+            for i in range(len(qs)):
+                for j in range(2):
+                    rbuf[i, j, pl.ds(pl.multiple_of(e * cap, cap), cap), cols] = r[(i * 2 + j) * cap:(i * 2 + j + 1) * cap]
+
+        for i, q in enumerate(qs):
+            psend[q, :, cols] = jnp.dot(pt[q * 2 + 1 - c], rbuf[i, 1 - c, :, cols], preferred_element_type=F32)
+        for i, d in enumerate(dists):
+            cp = pair_copy(qs[i], ((d + n_chip) % n_chip) * 2 + hf, hf * half)
+            cp.start()
+            pair_cps[d, hf] = cp
+        for i, q in enumerate(qs):
+            own[q, :, cols] = jnp.dot(pt[q * 2 + c], rbuf[i, c, :, cols], preferred_element_type=F32)
+
+    width = half // SUBS
 
     def ring_copy(dr, st, s):
         k = (dr * 3 + st) * SUBS + s
@@ -224,15 +172,19 @@
 
     ring = {(dr, st, s): ring_copy(dr, st, s) for dr in range(2) for st in range(3) for s in range(SUBS)}
     dest = {0: (-1, 2, 1, 0), 1: (1, 2, -1, 0)}
-
-    def ring_step(st):
-        for dr in range(2):
-            pair_cps[dest[dr][st]][dr].wait_recv()
-        for s in range(SUBS):
+    waited = set()
+
+    def ring_step(st, subs=range(SUBS)):
+        for s in subs:
             for dr in range(2):
-                q = chip(dest[dr][st])
-                rows, cols = pl.ds(s * sub, sub), pl.ds(dr * half, half)
-                v = own[q, rows, cols] + pairin[q, rows, cols]
+                d = dest[dr][st]
+                cols = pl.ds((2 * s + dr) * width, width)
+                hf = ((2 * s + dr) * width) // half
+                if (d, hf) not in waited:
+                    waited.add((d, hf))
+                    pair_cps[d, hf].wait_recv()
+                q = chip(d)
+                v = own[q, :, cols] + pairin[q, :, cols]
                 if st > 0:
                     ring[dr, st - 1, s].wait_recv()
                     v = v + rrecv[(dr * 3 + st - 1) * SUBS + s]
@@ -240,21 +192,74 @@
                     rsend[(dr * 3 + st) * SUBS + s] = v
                     ring[dr, st, s].start()
                 else:
-                    gx_out[rows, cols] = v.astype(BF16)
-
+                    gx_out[:, cols] = v.astype(BF16)
+
+    for cp in meta_cp:
+        cp.wait_recv()
+    to_p.wait_recv()
+    build(x * 2)
+    build(x * 2 + 1)
+    to_r0.wait_recv()
+    fw_r.start()
+    p_l0.start()
+    to_l1.wait_recv()
+    fw_l.start()
+    p_r1.start()
+    to_r1.wait_recv()
+    p_l1.start()
+    to_l0.wait_recv()
+    p_r0.start()
+    build(left)
+    build(right)
+    p_l0.wait_recv()
+    p_l1.wait_recv()
+    build(chip(-1) * 2 + 1 - c)
+    p_r0.wait_recv()
+    p_r1.wait_recv()
+    build(chip(1) * 2 + 1 - c)
+    ld_wd.wait()
+    near = [chip(-1), chip(1)]
+    hidden(near)
+    fw_r.wait_recv()
+    p_f0.start()
+    fw_l.wait_recv()
+    p_f1.start()
+    ld_wg.wait()
+    ld_wu.wait()
+    ld_x = load(x_hbm, x_buf, 7)
+    ld_yr = load(yr_hbm, yr, 1)
+    back((-1, 1), near, 0)
+    back((-1, 1), near, 1)
     ring_step(0)
+    build(far)
     p_f0.wait_recv()
     p_f1.wait_recv()
-    pair_cps[2] = unit((2,))
+    build(chip(2) * 2 + 1 - c)
+    rest = [chip(2), x]
+    hidden(rest)
+    back((2, 0), rest, 0)
+    back((2, 0), rest, 1)
     ring_step(1)
+
+    ld_yr.wait()
+    step = 16
+
+    @pl.loop(0, tok // step)
+    def _(i):
+        t = pl.multiple_of(i * step, step)
+        g = gy_all[me, pl.ds(t, step), :].astype(F32)
+        y = yr[pl.ds(t, step), :, :].astype(F32)
+        gg_rows[pl.ds(t, step), :] = jnp.sum(y * g[:, None, :], axis=2)
+
+    gg_out[...] = gg_rows[...].T
+
     ring_step(2)
     ring_step(3)
 
     for cp in meta_cp + [to_r0, to_l1, to_r1, to_l0, to_p, fw_r, fw_l, p_l0, p_r1, p_l1, p_r0, p_f0, p_f1]:
         cp.wait_send()
-    for cps in pair_cps.values():
-        for cp in cps:
-            cp.wait_send()
+    for cp in pair_cps.values():
+        cp.wait_send()
     for cp in ring.values():
         cp.wait_send()
     ld_x.wait()
@@ -328,8 +333,8 @@
                 pltpu.VMEM((n_chip, tok, model), F32),
                 pltpu.VMEM((n_chip, tok, model), F32),
                 pltpu.VMEM((n_chip, tok, model), F32),
-                pltpu.VMEM((6 * SUBS, tok // SUBS, model // 2), F32),
-                pltpu.VMEM((6 * SUBS, tok // SUBS, model // 2), F32),
+                pltpu.VMEM((6 * SUBS, tok, model // 2 // SUBS), F32),
+                pltpu.VMEM((6 * SUBS, tok, model // 2 // SUBS), F32),
                 dma((8,)), dma((n_dev - 1,)), dma((n_dev - 1,)), dma((13,)), dma((13,)),
                 dma((2 * n_chip,)), dma((2 * n_chip,)), dma((6 * SUBS,)), dma((6 * SUBS,)),
             ],

time: 65 us -> 58.3 us (0.90)
  Pallas kernels: 63.8 us -> 57.5 us
    pallas_call x1, Pallas kernels: 52.3 us -> 46 us  [local_step(): pl.pallas_call(functools.partial(exchange_kernel, n_dev, cap), out_shape=...]
where the time goes in v4:
time: 58.3 us; the launch traced here: 58.2 us
  Pallas kernels  57.5 us (99%)
  between operations  0.64 us (1%)
    pallas_call x1, Pallas kernels, local_step(): pl.pallas_call(functools.partial(exchange_kernel, n_dev, cap), out_shape=...  46 us
    pallas_call x1, Pallas kernels, local_step(): pl.pallas_call(functools.partial(weight_kernel, js), out_shape=(jax.Shape...  11.5 us

profile of v4, /device:TPU:112, one launch (start us, length us, event | category | flops | bytes accessed | tf_op | source)
XLA Modules:
  0.0 58.2 jit_solution(2147497078431018501)
XLA Ops:
  0.6 46.0 %exchange.1 = (bf16[128,1024]{1,0:T(8,128)(2,1)S(1)}, f32[8,128]{1,0:T(8,128)S(1)}, bf16[4,512,1024]{2,1,0:T(8,128)(2,1)S(1)}, bf16[4,512,1024]{2,1,0:T(8,128)(2...) custom-call(s32[1,32]{1,0:T(1,128)} %counts.1, f32[8,128]{1,0:T(8,128)} %bitcast.4, ...), custom_call_target="tpu_custom_call" | custom-call | tf_op jit(solution)/shard_map/exchange/pallas_call | solution.py:315
  46.7 11.5 %weights.1 = (bf16[128,1024]{1,0:T(8,128)(2,1)}, f32[8,128]{1,0:T(8,128)}, f32[4,1024,512]{2,1,0:T(8,128)}, f32[4,1024,512]{2,1,0:T(8,128)}, f32[4,512,1024]{2,1,0:T(8,128)}) custom-call(bf16[4,512,1024]{2,1,0:T(8,128)(2,1)S(1)} %get-tuple-element.16.x_ref, bf16[4,512,1024]{2,1,0:T(8,128)(2,1)S(1)} %get-tuple-element.17.dh_ref, ...), custom_call_target="tpu_custom_call" | custom-call | tf_op jit(solution)/shard_map/weights/pallas_call | solution.py:345

commit v5 on v4

--- a/solution.py
+++ b/solution.py
@@ -12,12 +12,12 @@
 BF16 = jnp.bfloat16
 NT = (((1,), (1,)), ((), ()))
 TN = (((0,), (0,)), ((), ()))
-SUBS = 2
-
-
-def exchange_kernel(n_dev, cap, counts, gates, idx, slot, gy_hbm, yr_hbm, h1_hbm, h3_hbm, wg_hbm, wu_hbm, wd_hbm, x_hbm,
-                    gx_out, gg_out, d_buf, dh_buf, a_buf, x_buf,
-                    gy_all, yr, h1, h3, wcat, wd, fs, gg_rows, meta, pt, rbuf, own, psend, pairin, rsend, rrecv,
+SUBS = 4
+
+
+def exchange_kernel(n_dev, cap, counts_hbm, gates_hbm, idx_hbm, slot_hbm, gy_hbm, yr_hbm, h1_hbm, h3_hbm, wg_hbm, wu_hbm, wd_hbm, x_hbm,
+                    base_out, tail_r, tail_l, gg_out, d_buf, dh_buf, a_buf, x_buf,
+                    counts, idx, slot, gy_all, yr, h1, h3, wcat, wd, fs, gg_rows, meta, pt, rbuf, own, psend, pairin, rsend, rrecv,
                     loc_sem, meta_ssem, meta_rsem, ag_ssem, ag_rsem, pair_ssem, pair_rsem, ring_ssem, ring_rsem):
     n_loc, ffn, model = wd.shape
     top_k, tok = idx.shape
@@ -40,6 +40,7 @@
         cp.start()
         return cp
 
+    ld_small = (load(counts_hbm, counts, 8), load(idx_hbm, idx, 9), load(slot_hbm, slot, 10), load(gates_hbm, meta.at[me, 0], 11))
     ld_gy = load(gy_hbm, gy_all.at[me], 0)
     ld_h1 = load(h1_hbm, h1, 2)
     ld_h3 = load(h3_hbm, h3, 3)
@@ -47,16 +48,17 @@
     ld_wg = load(wg_hbm, wcat.at[:, :, pl.ds(0, ffn)], 5)
     ld_wu = load(wu_hbm, wcat.at[:, :, pl.ds(ffn, ffn)], 6)
 
+    barrier = pltpu.get_barrier_semaphore()
+    for r in range(1, n_dev):
+        pl.semaphore_signal(barrier, inc=1, device_id=dev((me + r) % n_dev), device_id_type=MESH)
+
+    for cp in ld_small:
+        cp.wait()
     cnt = jnp.zeros(idx.shape, jnp.int32)
     for e in range(n_loc * n_dev):
         cnt = jnp.where(idx[...] == e, counts[0, e], cnt)
     keep = (slot[...] >= 0) & (slot[...] < cnt)
-    meta[me, 0] = gates[...]
     meta[me, 1] = jnp.where(keep, idx[...] * cap + slot[...], -1).astype(F32)
-
-    barrier = pltpu.get_barrier_semaphore()
-    for r in range(1, n_dev):
-        pl.semaphore_signal(barrier, inc=1, device_id=dev((me + r) % n_dev), device_id_type=MESH)
     pl.semaphore_wait(barrier, n_dev - 1)
 
     meta_cp = []
@@ -125,7 +127,7 @@
             d_buf[e, pl.ds(pl.multiple_of(h * cap, cap), cap), :] = rows_d[e * cap:(e + 1) * cap]
 
     def pair_copy(q, s, lo):
-        return pltpu.make_async_remote_copy(src_ref=psend.at[q, :, pl.ds(lo, half)], dst_ref=pairin.at[q, :, pl.ds(lo, half)],
+        return pltpu.make_async_remote_copy(src_ref=psend.at[q, lo], dst_ref=pairin.at[q, lo],
                                             send_sem=pair_ssem.at[s], recv_sem=pair_rsem.at[s], device_id=dev(partner), device_id_type=MESH)
 
     def rows_of(ref, e, q):
@@ -143,8 +145,10 @@
 
     pair_cps = {}
 
+    chunk = model // SUBS
+
     def back(dists, qs, hf):
-        cols = pl.ds(hf * half, half)
+        cols = pl.ds(hf * chunk, chunk)
 
         @pl.loop(0, n_loc)
         def _(e):
@@ -152,47 +156,48 @@
             r = lax.dot_general(dh, wcat[e, cols, :], NT, preferred_element_type=F32).astype(BF16)
             for i in range(len(qs)):
                 for j in range(2):
-                    rbuf[i, j, pl.ds(pl.multiple_of(e * cap, cap), cap), cols] = r[(i * 2 + j) * cap:(i * 2 + j + 1) * cap]
+                    rbuf[i, j, pl.ds(pl.multiple_of(e * cap, cap), cap), :] = r[(i * 2 + j) * cap:(i * 2 + j + 1) * cap]
 
         for i, q in enumerate(qs):
-            psend[q, :, cols] = jnp.dot(pt[q * 2 + 1 - c], rbuf[i, 1 - c, :, cols], preferred_element_type=F32)
+            psend[q, hf] = jnp.dot(pt[q * 2 + 1 - c], rbuf[i, 1 - c], preferred_element_type=F32)
         for i, d in enumerate(dists):
-            cp = pair_copy(qs[i], ((d + n_chip) % n_chip) * 2 + hf, hf * half)
+            cp = pair_copy(qs[i], ((d + n_chip) % n_chip) * SUBS + hf, hf)
             cp.start()
             pair_cps[d, hf] = cp
         for i, q in enumerate(qs):
-            own[q, :, cols] = jnp.dot(pt[q * 2 + c], rbuf[i, c, :, cols], preferred_element_type=F32)
+            own[q, hf] = jnp.dot(pt[q * 2 + c], rbuf[i, c], preferred_element_type=F32)
 
     width = half // SUBS
 
     def ring_copy(dr, st, s):
-        k = (dr * 3 + st) * SUBS + s
+        k = (dr * 2 + st) * SUBS + s
         return pltpu.make_async_remote_copy(src_ref=rsend.at[k], dst_ref=rrecv.at[k], send_sem=ring_ssem.at[k], recv_sem=ring_rsem.at[k],
                                             device_id=dev(right if dr == 0 else left), device_id_type=MESH)
 
-    ring = {(dr, st, s): ring_copy(dr, st, s) for dr in range(2) for st in range(3) for s in range(SUBS)}
-    dest = {0: (-1, 2, 1, 0), 1: (1, 2, -1, 0)}
+    ring = {(dr, st, s): ring_copy(dr, st, s) for dr in range(2) for st in range(2) for s in range(SUBS)}
+    dest = {0: (-1, 2, 1), 1: (1, 2, -1)}
+    tails = (tail_r, tail_l)
     waited = set()
 
-    def ring_step(st, subs=range(SUBS)):
-        for s in subs:
-            for dr in range(2):
-                d = dest[dr][st]
-                cols = pl.ds((2 * s + dr) * width, width)
-                hf = ((2 * s + dr) * width) // half
-                if (d, hf) not in waited:
-                    waited.add((d, hf))
-                    pair_cps[d, hf].wait_recv()
-                q = chip(d)
-                v = own[q, :, cols] + pairin[q, :, cols]
-                if st > 0:
-                    ring[dr, st - 1, s].wait_recv()
-                    v = v + rrecv[(dr * 3 + st - 1) * SUBS + s]
-                if st < 3:
-                    rsend[(dr * 3 + st) * SUBS + s] = v
-                    ring[dr, st, s].start()
-                else:
-                    gx_out[:, cols] = v.astype(BF16)
+    def pair_sum(d, s, dr):
+        if (d, s) not in waited:
+            waited.add((d, s))
+            pair_cps[d, s].wait_recv()
+        q = chip(d)
+        cols = pl.ds(dr * width, width)
+        return own[q, s, :, cols] + pairin[q, s, :, cols]
+
+    def ring_step(st, s):
+        for dr in range(2):
+            v = pair_sum(dest[dr][st], s, dr)
+            if st > 0:
+                ring[dr, st - 1, s].wait_recv()
+                v = v + rrecv[(dr * 2 + st - 1) * SUBS + s]
+            if st < 2:
+                rsend[(dr * 2 + st) * SUBS + s] = v
+                ring[dr, st, s].start()
+            else:
+                tails[dr][s] = v
 
     for cp in meta_cp:
         cp.wait_recv()
@@ -229,8 +234,10 @@
     ld_x = load(x_hbm, x_buf, 7)
     ld_yr = load(yr_hbm, yr, 1)
     back((-1, 1), near, 0)
-    back((-1, 1), near, 1)
-    ring_step(0)
+    for s in range(1, SUBS):
+        back((-1, 1), near, s)
+        ring_step(0, s - 1)
+    ring_step(0, SUBS - 1)
     build(far)
     p_f0.wait_recv()
     p_f1.wait_recv()
@@ -238,8 +245,10 @@
     rest = [chip(2), x]
     hidden(rest)
     back((2, 0), rest, 0)
-    back((2, 0), rest, 1)
-    ring_step(1)
+    for s in range(1, SUBS):
+        back((2, 0), rest, s)
+        ring_step(1, s - 1)
+    ring_step(1, SUBS - 1)
 
     ld_yr.wait()
     step = 16
@@ -253,8 +262,11 @@
 
     gg_out[...] = gg_rows[...].T
 
-    ring_step(2)
-    ring_step(3)
+    for s in range(SUBS):
+        for dr in range(2):
+            base_out[s, :, pl.ds(dr * width, width)] = pair_sum(0, s, dr)
+    for s in range(SUBS):
+        ring_step(2, s)
 
     for cp in meta_cp + [to_r0, to_l1, to_r1, to_l0, to_p, fw_r, fw_l, p_l0, p_r1, p_l1, p_r0, p_f0, p_f1]:
         cp.wait_send()
@@ -265,10 +277,9 @@
     ld_x.wait()
 
 
-def weight_kernel(js, x_ref, dh_ref, a_ref, d_ref, gx_ref, gg_ref, gx_out, gg_out, gwg, gwu, gwd, gbuf, dbuf, sem):
+def weight_kernel(js, x_ref, dh_ref, a_ref, d_ref, gg_ref, gg_out, gwg, gwu, gwd, gbuf, dbuf, sem):
     n_loc, model, ffn = gwg.shape
     xc, ac = model // js, ffn // js
-    gx_out[...] = gx_ref[...]
     gg_out[...] = gg_ref[...]
 
     def copies(i):
@@ -295,6 +306,13 @@
     for i in range(n_loc * js - 2, n_loc * js):
         for cp in copies(i):
             cp.wait()
+
+
+def finish_kernel(base, from_l, from_r, gx_out):
+    width = from_l.shape[2]
+    for s in range(SUBS):
+        for dr, ref in enumerate((from_l, from_r)):
+            gx_out[:, pl.ds((2 * s + dr) * width, width)] = (base[s, :, pl.ds(dr * width, width)] + ref[s]).astype(BF16)
 
 
 def solution(mesh):
@@ -312,13 +330,18 @@
         vm = pl.BlockSpec(memory_space=pltpu.VMEM)
         hbm = pl.BlockSpec(memory_space=pl.ANY)
         dma = pltpu.SemaphoreType.DMA
-        gx, gg, d_rows, dh, act, x_rows = pl.pallas_call(
+        vs = pltpu.VMEM
+        tail = vs((SUBS, tok, model // 2 // SUBS), F32)
+        base, tail_r, tail_l, gg, d_rows, dh, act, x_rows = pl.pallas_call(
             functools.partial(exchange_kernel, n_dev, cap),
-            out_shape=(pltpu.VMEM((tok, model), BF16), pltpu.VMEM((top_k, tok), F32), pltpu.VMEM((n_loc, rows, model), BF16),
+            out_shape=(vs((SUBS, tok, model // SUBS), F32), tail, tail, pltpu.VMEM((top_k, tok), F32), pltpu.VMEM((n_loc, rows, model), BF16),
                        pltpu.VMEM((n_loc, rows, 2 * ffn), BF16), pltpu.VMEM((n_loc, rows, ffn), BF16), pltpu.VMEM((n_loc, rows, model), BF16)),
-            in_specs=[pl.BlockSpec(memory_space=pltpu.SMEM), vm, vm, vm] + [hbm] * 8,
-            out_specs=(vm,) * 6,
+            in_specs=[hbm] * 12,
+            out_specs=(vm,) * 8,
             scratch_shapes=[
+                pltpu.SMEM(pair_counts.shape, jnp.int32),
+                pltpu.VMEM((top_k, tok), jnp.int32),
+                pltpu.VMEM((top_k, tok), jnp.int32),
                 pltpu.VMEM((n_dev, tok, model), BF16),
                 pltpu.VMEM((tok, top_k, model), BF16),
                 pltpu.VMEM((n_loc, rows, ffn), BF16),
@@ -329,29 +352,41 @@
                 pltpu.VMEM((tok, top_k), F32),
                 pltpu.VMEM((n_dev, 2, top_k, tok), F32),
                 pltpu.VMEM((n_dev, tok, n_loc * cap), BF16),
-                pltpu.VMEM((2, 2, n_loc * cap, model), BF16),
-                pltpu.VMEM((n_chip, tok, model), F32),
-                pltpu.VMEM((n_chip, tok, model), F32),
-                pltpu.VMEM((n_chip, tok, model), F32),
-                pltpu.VMEM((6 * SUBS, tok, model // 2 // SUBS), F32),
-                pltpu.VMEM((6 * SUBS, tok, model // 2 // SUBS), F32),
-                dma((8,)), dma((n_dev - 1,)), dma((n_dev - 1,)), dma((13,)), dma((13,)),
-                dma((2 * n_chip,)), dma((2 * n_chip,)), dma((6 * SUBS,)), dma((6 * SUBS,)),
+                pltpu.VMEM((2, 2, n_loc * cap, model // SUBS), BF16),
+                pltpu.VMEM((n_chip, SUBS, tok, model // SUBS), F32),
+                pltpu.VMEM((n_chip, SUBS, tok, model // SUBS), F32),
+                pltpu.VMEM((n_chip, SUBS, tok, model // SUBS), F32),
+                pltpu.VMEM((4 * SUBS, tok, model // 2 // SUBS), F32),
+                pltpu.VMEM((4 * SUBS, tok, model // 2 // SUBS), F32),
+                dma((12,)), dma((n_dev - 1,)), dma((n_dev - 1,)), dma((13,)), dma((13,)),
+                dma((SUBS * n_chip,)), dma((SUBS * n_chip,)), dma((4 * SUBS,)), dma((4 * SUBS,)),
             ],
             compiler_params=pltpu.CompilerParams(collective_id=0, has_side_effects=True, vmem_limit_bytes=44 * 1024 * 1024),
             name="exchange",
         )(pair_counts, gate_vals.T, topk_idx.T, slot_ids.T, grad_y, y_routed, h_gate, h_up, w_gate, w_up, w_down, x_disp)
         js = 2
-        gx, gg, gwg, gwu, gwd = pl.pallas_call(
+        ring_r = [(i, ((i // 2 + 1) % n_chip) * 2 + i % 2) for i in range(n_dev)]
+        from_l = lax.ppermute(tail_r, "ep", ring_r)
+        from_r = lax.ppermute(tail_l, "ep", [(b, a) for a, b in ring_r])
+        gg, gwg, gwu, gwd = pl.pallas_call(
             functools.partial(weight_kernel, js),
-            out_shape=(jax.ShapeDtypeStruct((tok, model), BF16), jax.ShapeDtypeStruct((top_k, tok), F32), jax.ShapeDtypeStruct((n_loc, model, ffn), F32),
+            out_shape=(jax.ShapeDtypeStruct((top_k, tok), F32), jax.ShapeDtypeStruct((n_loc, model, ffn), F32),
                        jax.ShapeDtypeStruct((n_loc, model, ffn), F32), jax.ShapeDtypeStruct((n_loc, ffn, model), F32)),
-            in_specs=[vm] * 6,
-            out_specs=(vm, vm, hbm, hbm, hbm),
+            in_specs=[vm] * 5,
+            out_specs=(vm, hbm, hbm, hbm),
             scratch_shapes=[pltpu.VMEM((2, model // js, 2 * ffn), F32), pltpu.VMEM((2, ffn // js, model), F32), dma((2, 3))],
             compiler_params=pltpu.CompilerParams(vmem_limit_bytes=20 * 1024 * 1024),
+            cost_estimate=pl.CostEstimate(flops=6 * n_loc * rows * model * ffn, bytes_accessed=12 * n_loc * model * ffn, transcendentals=0),
             name="weights",
-        )(x_rows, dh, act, d_rows, gx, gg)
+        )(x_rows, dh, act, d_rows, gg)
+        gx = pl.pallas_call(
+            finish_kernel,
+            out_shape=jax.ShapeDtypeStruct((tok, model), BF16),
+            in_specs=[vm] * 3,
+            out_specs=vm,
+            compiler_params=pltpu.CompilerParams(vmem_limit_bytes=4 * 1024 * 1024),
+            name="finish",
+        )(base, from_l, from_r)
         return gx, gg.T, gwg, gwu, gwd
 
     return jax.shard_map(local_step, mesh=mesh, in_specs=(rows_spec, rows_spec, rows_spec, rows_spec, rows_spec, cube_spec, cube_spec, cube_spec, cube_spec, weight_spec, weight_spec, weight_spec), out_specs=(rows_spec, rows_spec, cube_spec, cube_spec, cube_spec), check_vma=False)

time: 58.3 us -> 57.4 us (0.985)
  Pallas kernels: 57.5 us -> 53.3 us
  starting transfers between devices: 0 us -> 3.31 us
    pallas_call x1, Pallas kernels: 46 us -> 41.3 us  [local_step(): pl.pallas_call(functools.partial(exchange_kernel, n_dev, cap), out_shape=...]
    ppermute x0 -> x2, starting transfers between devices: none -> 3.31 us  [the longest x1 2.95 us: local_step(): from_r = lax.ppermute(tail_l, 'ep', [(b, a) for a, b in ring_r])]
    pallas_call x0 -> x1, Pallas kernels: none -> 0.79 us  [local_step(): pl.pallas_call(finish_kernel, out_shape=jax.ShapeDtypeStruct((tok, model)...]
  transfers between devices with their start and end apart: 0 -> 2, of which waited for: 0 -> 0; matrix products, arithmetic and copies ran while one was open for 0% -> 0% of each run, Pallas kernels for 0% -> 19%
where the time goes in v5:
time: 57.4 us; the launch traced here: 57.3 us
  Pallas kernels  53.3 us (93%)
  starting transfers between devices  3.31 us (6%)
  between operations  0.67 us (1%)
    pallas_call x1, Pallas kernels, local_step(): pl.pallas_call(functools.partial(exchange_kernel, n_dev, cap), out_shape=...  41.3 us
    pallas_call x1, Pallas kernels, local_step(): pl.pallas_call(functools.partial(weight_kernel, js), out_shape=(jax.Shape...  11.2 us
    ppermute x1, starting transfers between devices, local_step(): from_r = lax.ppermute(tail_l, 'ep', [(b, a) for a, b in ring_r])  2.95 us
  transfers between devices with their start and end apart: 2, of which 0 were waited for; matrix products, arithmetic and copies ran while one was open for 0% of the time, Pallas kernels for 19%

profile of v5, /device:TPU:112, one launch (start us, length us, event | category | flops | bytes accessed | tf_op | source)
XLA Modules:
  0.0 57.3 jit_solution(6229037713341816786)
XLA Ops:
  0.6 41.3 %exchange.1 = (f32[4,128,256]{2,1,0:T(8,128)S(1)}, f32[4,128,128]{2,1,0:T(8,128)S(1)}, f32[4,128,128]{2,1,0:T(8,128)S(1)}, f32[8,128]{1,0:T(8,128)S(1)}, bf16[4,...) custom-call(s32[1,32]{1,0:T(1,128)} %counts_hbm.1, ...), custom_call_target="tpu_custom_call" | custom-call | tf_op jit(solution)/shard_map/exchange/pallas_call | solution.py:335
  42.0 0.4 collective-permute-start
  42.4 2.9 %collective-permute-start.1 = (f32[4,128,128]{2,1,0:T(8,128)S(1)}, f32[4,128,128]{2,1,0:T(8,128)S(1)}, u32[]{:S(2)}, u32[]{:S(2)}) collective-permute-start(f32[4,128,128]{2,1,0:T(8,128)S(1)} %get-tuple-element.19), channel_id=1, source_target_pairs={{2,0},{3,1},{4,2},{5,3},{6,4},{7,5},{0,6},{1,7},{10,8},{11,9},{12,... | collective-permute-start | bytes 786440 | tf_op jit(solution)/shard_map/ppermute | solution.py:370
  45.3 11.2 %weights.1 = (f32[8,128]{1,0:T(8,128)}, f32[4,1024,512]{2,1,0:T(8,128)}, f32[4,1024,512]{2,1,0:T(8,128)}, f32[4,512,1024]{2,1,0:T(8,128)}) custom-call(bf16[4,512,1024]{2,1,0:T(8,128)(2,1)S(1)} %get-tuple-element.20.x_ref, bf16[4,512,1024]{2,1,0:T(8,128)(2,1)S(1)} %get-tuple-element.21.dh_ref, bf16[4,512,512]{2,1,0:T(8,128)(2,1)S(1)} %get-tuple-element.22.a_ref, ...), custom_call_target="tpu_custom_call" | custom-call | flops 6442450944 | bytes 25165824 | tf_op jit(solution)/shard_map/weights/pallas_call | solution.py:371
  56.5 0.0 collective-permute-done.from_l
  56.5 0.0 collective-permute-done.1.from_r
  56.5 0.8 %finish.1 = bf16[128,1024]{1,0:T(8,128)(2,1)} custom-call(f32[4,128,256]{2,1,0:T(8,128)S(1)} %get-tuple-element.17.base, f32[4,128,128]{2,1,0:T(8,128)S(1)} %collective-permute-done.from_l, f32[4,128,128]{2,1,0:T(8,128)S(1)} %collective-permute-done.1.from_r), custom_call_target="tpu_custom_call" | custom-call | tf_op jit(solution)/shard_map/finish/pallas_call | solution.py:382
Async XLA Ops:
  42.0 14.5 %collective-permute-start = (f32[4,128,128]{2,1,0:T(8,128)S(1)}, f32[4,128,128]{2,1,0:T(8,128)S(1)}, u32[]{:S(2)}, u32[]{:S(2)}) collective-permute-start(f32[4,128,128]{2,1,0:T(8,128)S(1)} %get-tuple-element.18), channel_id=1, source_target_pairs={{0,2},{1,3},{2,4},{3,5},{4,6},{5,7},{6,0},{7,1},{8,10},{9,11},{10,... | collective-permute-start | bytes 786440 | tf_op jit(solution)/shard_map/ppermute | solution.py:369
  42.4 14.1 %collective-permute-start.1 = (f32[4,128,128]{2,1,0:T(8,128)S(1)}, f32[4,128,128]{2,1,0:T(8,128)S(1)}, u32[]{:S(2)}, u32[]{:S(2)}) collective-permute-start(f32[4,128,128]{2,1,0:T(8,128)S(1)} %get-tuple-element.19), channel_id=1, source_target_pairs={{2,0},{3,1},{4,2},{5,3},{6,4},{7,5},{0,6},{1,7},{10,8},{11,9},{12,... | collective-permute-start | bytes 786440 | tf_op jit(solution)/shard_map/ppermute | solution.py:370

commit v6 on v5

--- a/solution.py
+++ b/solution.py
@@ -13,6 +13,33 @@
 NT = (((1,), (1,)), ((), ()))
 TN = (((0,), (0,)), ((), ()))
 SUBS = 4
+BUFS = 4
+
+
+class Once:
+    def __init__(self, cp, log, remote):
+        self.cp, self.log, self.remote, self.got = cp, log, remote, False
+
+    def start(self):
+        self.cp.start()
+        self.log.append(self)
+
+    def wait(self):
+        if not self.got:
+            self.got = True
+            self.cp.wait()
+
+    def wait_recv(self):
+        if not self.got:
+            self.got = True
+            self.cp.wait_recv()
+
+    def finish(self):
+        if self.remote:
+            self.wait_recv()
+            self.cp.wait_send()
+        else:
+            self.wait()
 
 
 def exchange_kernel(n_dev, cap, counts_hbm, gates_hbm, idx_hbm, slot_hbm, gy_hbm, yr_hbm, h1_hbm, h3_hbm, wg_hbm, wu_hbm, wd_hbm, x_hbm,
@@ -24,6 +51,7 @@
     n_chip = n_dev // 2
     half = model // 2
     hrow = tok // 2
+    log = []
     me = lax.axis_index("ep")
     x = me // 2
     c = me % 2
@@ -36,7 +64,7 @@
         return {"ep": i}
 
     def load(src, dst, s):
-        cp = pltpu.make_async_copy(src, dst, loc_sem.at[s])
+        cp = Once(pltpu.make_async_copy(src, dst, loc_sem.at[s]), log, False)
         cp.start()
         return cp
 
@@ -52,37 +80,18 @@
     for r in range(1, n_dev):
         pl.semaphore_signal(barrier, inc=1, device_id=dev((me + r) % n_dev), device_id_type=MESH)
 
-    for cp in ld_small:
-        cp.wait()
-    cnt = jnp.zeros(idx.shape, jnp.int32)
-    for e in range(n_loc * n_dev):
-        cnt = jnp.where(idx[...] == e, counts[0, e], cnt)
-    keep = (slot[...] >= 0) & (slot[...] < cnt)
-    meta[me, 1] = jnp.where(keep, idx[...] * cap + slot[...], -1).astype(F32)
-    pl.semaphore_wait(barrier, n_dev - 1)
-
-    meta_cp = []
-    for r in range(1, n_dev):
-        cp = pltpu.make_async_remote_copy(src_ref=meta.at[me], dst_ref=meta.at[me], send_sem=meta_ssem.at[r - 1], recv_sem=meta_rsem.at[r - 1],
-                                          device_id=dev((me + r) % n_dev), device_id_type=MESH)
-        cp.start()
-        meta_cp.append(cp)
-
     def gy_copy(block, lo, n, s, to):
         ref = gy_all.at[block, pl.ds(lo, n), :]
-        return pltpu.make_async_remote_copy(src_ref=ref, dst_ref=ref, send_sem=ag_ssem.at[s], recv_sem=ag_rsem.at[s], device_id=dev(to), device_id_type=MESH)
+        return Once(pltpu.make_async_remote_copy(src_ref=ref, dst_ref=ref, send_sem=ag_ssem.at[s], recv_sem=ag_rsem.at[s], device_id=dev(to), device_id_type=MESH), log, True)
 
     right = chip(1) * 2 + c
     left = chip(-1) * 2 + c
     far = chip(2) * 2 + c
-    ld_gy.wait()
     to_r0 = gy_copy(me, 0, hrow, 0, right)
     to_l1 = gy_copy(me, hrow, hrow, 1, left)
     to_r1 = gy_copy(me, hrow, hrow, 2, right)
     to_l0 = gy_copy(me, 0, hrow, 3, left)
     to_p = gy_copy(me, 0, tok, 4, partner)
-    for cp in (to_r0, to_l1, to_p, to_r1, to_l0):
-        cp.start()
     fw_r = gy_copy(left, 0, hrow, 5, right)
     fw_l = gy_copy(right, hrow, hrow, 6, left)
     p_l0 = gy_copy(left, 0, hrow, 7, partner)
@@ -91,6 +100,37 @@
     p_r0 = gy_copy(right, 0, hrow, 10, partner)
     p_f0 = gy_copy(far, 0, hrow, 11, partner)
     p_f1 = gy_copy(far, hrow, hrow, 12, partner)
+
+    pl.semaphore_wait(barrier, n_dev - 1)
+    ld_gy.wait()
+    for cp in (to_r0, to_l1, to_p):
+        cp.start()
+
+    for cp in ld_small:
+        cp.wait()
+    cnt = jnp.zeros(idx.shape, jnp.int32)
+    for e in range(n_loc * n_dev):
+        cnt = jnp.where(idx[...] == e, counts[0, e], cnt)
+    keep = (slot[...] >= 0) & (slot[...] < cnt)
+    meta[me, 1] = jnp.where(keep, idx[...] * cap + slot[...], -1).astype(F32)
+
+    meta_cp = {}
+    for d in range(n_chip):
+        for k in range(2):
+            if d == 0 and k == 0:
+                continue
+            s = d * 2 + k - 1
+            cp = Once(pltpu.make_async_remote_copy(src_ref=meta.at[me], dst_ref=meta.at[me], send_sem=meta_ssem.at[s], recv_sem=meta_rsem.at[s],
+                                                   device_id=dev(chip(d) * 2 + (c if k == 0 else 1 - c)), device_id_type=MESH), log, True)
+            cp.start()
+            meta_cp[d, k] = cp
+    to_r1.start()
+    to_l0.start()
+
+    def meta_wait(d):
+        for k in range(2):
+            if (d, k) != (0, 0):
+                meta_cp[(n_chip - d) % n_chip, k].wait_recv()
 
     ld_h1.wait()
     ld_h3.wait()
@@ -127,8 +167,8 @@
             d_buf[e, pl.ds(pl.multiple_of(h * cap, cap), cap), :] = rows_d[e * cap:(e + 1) * cap]
 
     def pair_copy(q, s, lo):
-        return pltpu.make_async_remote_copy(src_ref=psend.at[q, lo], dst_ref=pairin.at[q, lo],
-                                            send_sem=pair_ssem.at[s], recv_sem=pair_rsem.at[s], device_id=dev(partner), device_id_type=MESH)
+        return Once(pltpu.make_async_remote_copy(src_ref=psend.at[q, lo], dst_ref=pairin.at[q, lo],
+                                                 send_sem=pair_ssem.at[s], recv_sem=pair_rsem.at[s], device_id=dev(partner), device_id_type=MESH), log, True)
 
     def rows_of(ref, e, q):
         return ref[e, pl.ds(pl.multiple_of(q * (2 * cap), 2 * cap), 2 * cap), :]
@@ -171,18 +211,15 @@
 
     def ring_copy(dr, st, s):
         k = (dr * 2 + st) * SUBS + s
-        return pltpu.make_async_remote_copy(src_ref=rsend.at[k], dst_ref=rrecv.at[k], send_sem=ring_ssem.at[k], recv_sem=ring_rsem.at[k],
-                                            device_id=dev(right if dr == 0 else left), device_id_type=MESH)
+        return Once(pltpu.make_async_remote_copy(src_ref=rsend.at[k], dst_ref=rrecv.at[k], send_sem=ring_ssem.at[k], recv_sem=ring_rsem.at[k],
+                                                 device_id=dev(right if dr == 0 else left), device_id_type=MESH), log, True)
 
     ring = {(dr, st, s): ring_copy(dr, st, s) for dr in range(2) for st in range(2) for s in range(SUBS)}
     dest = {0: (-1, 2, 1), 1: (1, 2, -1)}
     tails = (tail_r, tail_l)
-    waited = set()
 
     def pair_sum(d, s, dr):
-        if (d, s) not in waited:
-            waited.add((d, s))
-            pair_cps[d, s].wait_recv()
+        pair_cps[d, s].wait_recv()
         q = chip(d)
         cols = pl.ds(dr * width, width)
         return own[q, s, :, cols] + pairin[q, s, :, cols]
@@ -199,8 +236,11 @@
             else:
                 tails[dr][s] = v
 
-    for cp in meta_cp:
-        cp.wait_recv()
+    def finish():
+        for cp in log:
+            cp.finish()
+
+    meta_wait(0)
     to_p.wait_recv()
     build(x * 2)
     build(x * 2 + 1)
@@ -210,45 +250,54 @@
     to_l1.wait_recv()
     fw_l.start()
     p_r1.start()
+    ld_wd.wait()
+    hidden([x])
+    ld_wg.wait()
+    ld_wu.wait()
+    back((0,), [x], 0)
     to_r1.wait_recv()
     p_l1.start()
     to_l0.wait_recv()
     p_r0.start()
+    ld_x = load(x_hbm, x_buf, 7)
+    ld_yr = load(yr_hbm, yr, 1)
+    meta_wait(-1)
+    meta_wait(1)
     build(left)
     build(right)
+    back((0,), [x], 1)
     p_l0.wait_recv()
     p_l1.wait_recv()
     build(chip(-1) * 2 + 1 - c)
     p_r0.wait_recv()
     p_r1.wait_recv()
     build(chip(1) * 2 + 1 - c)
-    ld_wd.wait()
     near = [chip(-1), chip(1)]
     hidden(near)
+    back((-1, 1), near, 0)
+    back((-1, 1), near, 1)
     fw_r.wait_recv()
     p_f0.start()
     fw_l.wait_recv()
     p_f1.start()
-    ld_wg.wait()
-    ld_wu.wait()
-    ld_x = load(x_hbm, x_buf, 7)
-    ld_yr = load(yr_hbm, yr, 1)
-    back((-1, 1), near, 0)
-    for s in range(1, SUBS):
+    ring_step(0, 0)
+    for s in range(2, SUBS):
         back((-1, 1), near, s)
         ring_step(0, s - 1)
+    meta_wait(2)
+    build(far)
     ring_step(0, SUBS - 1)
-    build(far)
     p_f0.wait_recv()
     p_f1.wait_recv()
     build(chip(2) * 2 + 1 - c)
-    rest = [chip(2), x]
-    hidden(rest)
-    back((2, 0), rest, 0)
+    hidden([chip(2)])
+    back((2,), [chip(2)], 0)
     for s in range(1, SUBS):
-        back((2, 0), rest, s)
+        back((2,), [chip(2)], s)
         ring_step(1, s - 1)
     ring_step(1, SUBS - 1)
+    for s in range(2, SUBS):
+        back((0,), [x], s)
 
     ld_yr.wait()
     step = 16
@@ -268,13 +317,7 @@
     for s in range(SUBS):
         ring_step(2, s)
 
-    for cp in meta_cp + [to_r0, to_l1, to_r1, to_l0, to_p, fw_r, fw_l, p_l0, p_r1, p_l1, p_r0, p_f0, p_f1]:
-        cp.wait_send()
-    for cp in pair_cps.values():
-        cp.wait_send()
-    for cp in ring.values():
-        cp.wait_send()
-    ld_x.wait()
+    finish()
 
 
 def weight_kernel(js, x_ref, dh_ref, a_ref, d_ref, gg_ref, gg_out, gwg, gwu, gwd, gbuf, dbuf, sem):
@@ -283,7 +326,7 @@
     gg_out[...] = gg_ref[...]
 
     def copies(i):
-        e, j, b = i // js, i % js, i % 2
+        e, j, b = i // js, i % js, i % BUFS
         rows, arows = pl.ds(pl.multiple_of(j * xc, xc), xc), pl.ds(pl.multiple_of(j * ac, ac), ac)
         return (pltpu.make_async_copy(gbuf.at[b, :, pl.ds(0, ffn)], gwg.at[e, rows, :], sem.at[b, 0]),
                 pltpu.make_async_copy(gbuf.at[b, :, pl.ds(ffn, ffn)], gwu.at[e, rows, :], sem.at[b, 1]),
@@ -291,11 +334,11 @@
 
     @pl.loop(0, n_loc * js)
     def _(i):
-        e, j, b = i // js, i % js, i % 2
-
-        @pl.when(i >= 2)
+        e, j, b = i // js, i % js, i % BUFS
+
+        @pl.when(i >= BUFS)
         def _():
-            for cp in copies(i - 2):
+            for cp in copies(i - BUFS):
                 cp.wait()
 
         gbuf[b] = lax.dot_general(x_ref[e, :, pl.ds(pl.multiple_of(j * xc, xc), xc)], dh_ref[e], TN, preferred_element_type=F32)
@@ -303,7 +346,7 @@
         for cp in copies(i):
             cp.start()
 
-    for i in range(n_loc * js - 2, n_loc * js):
+    for i in range(n_loc * js - BUFS, n_loc * js):
         for cp in copies(i):
             cp.wait()
 
@@ -364,7 +407,7 @@
             compiler_params=pltpu.CompilerParams(collective_id=0, has_side_effects=True, vmem_limit_bytes=44 * 1024 * 1024),
             name="exchange",
         )(pair_counts, gate_vals.T, topk_idx.T, slot_ids.T, grad_y, y_routed, h_gate, h_up, w_gate, w_up, w_down, x_disp)
-        js = 2
+        js = 4
         ring_r = [(i, ((i // 2 + 1) % n_chip) * 2 + i % 2) for i in range(n_dev)]
         from_l = lax.ppermute(tail_r, "ep", ring_r)
         from_r = lax.ppermute(tail_l, "ep", [(b, a) for a, b in ring_r])
@@ -374,7 +417,7 @@
                        jax.ShapeDtypeStruct((n_loc, model, ffn), F32), jax.ShapeDtypeStruct((n_loc, ffn, model), F32)),
             in_specs=[vm] * 5,
             out_specs=(vm, hbm, hbm, hbm),
-            scratch_shapes=[pltpu.VMEM((2, model // js, 2 * ffn), F32), pltpu.VMEM((2, ffn // js, model), F32), dma((2, 3))],
+            scratch_shapes=[pltpu.VMEM((BUFS, model // js, 2 * ffn), F32), pltpu.VMEM((BUFS, ffn // js, model), F32), dma((BUFS, 3))],
             compiler_params=pltpu.CompilerParams(vmem_limit_bytes=20 * 1024 * 1024),
             cost_estimate=pl.CostEstimate(flops=6 * n_loc * rows * model * ffn, bytes_accessed=12 * n_loc * model * ffn, transcendentals=0),
             name="weights",

time: 57.4 us -> 58.7 us (1.023)
  Pallas kernels: 53.3 us -> 54.7 us
    pallas_call x1, Pallas kernels: 41.3 us -> 42.3 us  [local_step(): pl.pallas_call(functools.partial(exchange_kernel, n_dev, cap), out_shape=...]
  transfers between devices with their start and end apart: 2 -> 2, of which waited for: 0 -> 0; matrix products, arithmetic and copies ran while one was open for 0% -> 0% of each run, Pallas kernels for 19% -> 20%
where the time goes in v6:
time: 58.7 us
  Pallas kernels  54.7 us (93%)
  starting transfers between devices  3.31 us (6%)
  between operations  0.67 us (1%)
    pallas_call x1, Pallas kernels, local_step(): pl.pallas_call(functools.partial(exchange_kernel, n_dev, cap), out_shape=...  42.3 us
    pallas_call x1, Pallas kernels, local_step(): pl.pallas_call(functools.partial(weight_kernel, js), out_shape=(jax.Shape...  11.5 us
    ppermute x1, starting transfers between devices, local_step(): from_r = lax.ppermute(tail_l, 'ep', [(b, a) for a, b in ring_r])  2.63 us
  transfers between devices with their start and end apart: 2, of which 0 were waited for; matrix products, arithmetic and copies ran while one was open for 0% of the time, Pallas kernels for 20%

profile of v6, /device:TPU:112, one launch (start us, length us, event | category | flops | bytes accessed | tf_op | source)
XLA Modules:
  0.0 58.7 jit_solution(12114528745503809427)
XLA Ops:
  0.6 42.3 %exchange.1 = (f32[4,128,256]{2,1,0:T(8,128)S(1)}, f32[4,128,128]{2,1,0:T(8,128)S(1)}, f32[4,128,128]{2,1,0:T(8,128)S(1)}, f32[8,128]{1,0:T(8,128)S(1)}, bf16[4,...) custom-call(s32[1,32]{1,0:T(1,128)} %counts_hbm.1, ...), custom_call_target="tpu_custom_call" | custom-call | tf_op jit(solution)/shard_map/exchange/pallas_call | solution.py:378
  43.0 0.7 %collective-permute-start = (f32[4,128,128]{2,1,0:T(8,128)S(1)}, f32[4,128,128]{2,1,0:T(8,128)S(1)}, u32[]{:S(2)}, u32[]{:S(2)}) collective-permute-start(f32[4,128,128]{2,1,0:T(8,128)S(1)} %get-tuple-element.18), channel_id=1, source_target_pairs={{0,2},{1,3},{2,4},{3,5},{4,6},{5,7},{6,0},{7,1},{8,10},{9,11},{10,... | collective-permute-start | bytes 786440 | tf_op jit(solution)/shard_map/ppermute | solution.py:412
  43.7 2.6 %collective-permute-start.1 = (f32[4,128,128]{2,1,0:T(8,128)S(1)}, f32[4,128,128]{2,1,0:T(8,128)S(1)}, u32[]{:S(2)}, u32[]{:S(2)}) collective-permute-start(f32[4,128,128]{2,1,0:T(8,128)S(1)} %get-tuple-element.19), channel_id=1, source_target_pairs={{2,0},{3,1},{4,2},{5,3},{6,4},{7,5},{0,6},{1,7},{10,8},{11,9},{12,... | collective-permute-start | bytes 786440 | tf_op jit(solution)/shard_map/ppermute | solution.py:413
  46.3 11.5 %weights.1 = (f32[8,128]{1,0:T(8,128)}, f32[4,1024,512]{2,1,0:T(8,128)}, f32[4,1024,512]{2,1,0:T(8,128)}, f32[4,512,1024]{2,1,0:T(8,128)}) custom-call(bf16[4,512,1024]{2,1,0:T(8,128)(2,1)S(1)} %get-tuple-element.20.x_ref, bf16[4,512,1024]{2,1,0:T(8,128)(2,1)S(1)} %get-tuple-element.21.dh_ref, bf16[4,512,512]{2,1,0:T(8,128)(2,1)S(1)} %get-tuple-element.22.a_ref, ...), custom_call_target="tpu_custom_call" | custom-call | flops 6442450944 | bytes 25165824 | tf_op jit(solution)/shard_map/weights/pallas_call | solution.py:414
  57.8 0.0 collective-permute-done.from_l
  57.9 0.0 collective-permute-done.1.from_r
  57.9 0.8 %finish.1 = bf16[128,1024]{1,0:T(8,128)(2,1)} custom-call(f32[4,128,256]{2,1,0:T(8,128)S(1)} %get-tuple-element.17.base, f32[4,128,128]{2,1,0:T(8,128)S(1)} %collective-permute-done.from_l, f32[4,128,128]{2,1,0:T(8,128)S(1)} %collective-permute-done.1.from_r), custom_call_target="tpu_custom_call" | custom-call | tf_op jit(solution)/shard_map/finish/pallas_call | solution.py:425
Async XLA Ops:
  43.0 14.9 %collective-permute-start = (f32[4,128,128]{2,1,0:T(8,128)S(1)}, f32[4,128,128]{2,1,0:T(8,128)S(1)}, u32[]{:S(2)}, u32[]{:S(2)}) collective-permute-start(f32[4,128,128]{2,1,0:T(8,128)S(1)} %get-tuple-element.18), channel_id=1, source_target_pairs={{0,2},{1,3},{2,4},{3,5},{4,6},{5,7},{6,0},{7,1},{8,10},{9,11},{10,... | collective-permute-start | bytes 786440 | tf_op jit(solution)/shard_map/ppermute | solution.py:412
  43.7 14.2 %collective-permute-start.1 = (f32[4,128,128]{2,1,0:T(8,128)S(1)}, f32[4,128,128]{2,1,0:T(8,128)S(1)}, u32[]{:S(2)}, u32[]{:S(2)}) collective-permute-start(f32[4,128,128]{2,1,0:T(8,128)S(1)} %get-tuple-element.19), channel_id=1, source_target_pairs={{2,0},{3,1},{4,2},{5,3},{6,4},{7,5},{0,6},{1,7},{10,8},{11,9},{12,... | collective-permute-start | bytes 786440 | tf_op jit(solution)/shard_map/ppermute | solution.py:413

commit v7 on v6

--- a/solution.py
+++ b/solution.py
@@ -13,7 +13,7 @@
 NT = (((1,), (1,)), ((), ()))
 TN = (((0,), (0,)), ((), ()))
 SUBS = 4
-BUFS = 4
+BUFS = 3
 
 
 class Once:
@@ -174,8 +174,7 @@
         return ref[e, pl.ds(pl.multiple_of(q * (2 * cap), 2 * cap), 2 * cap), :]
 
     def hidden(qs):
-        @pl.loop(0, n_loc)
-        def _(e):
+        for e in range(n_loc):
             d = jnp.concatenate([rows_of(d_buf, e, q) for q in qs], axis=0)
             da = lax.dot_general(d, wd[e], NT, preferred_element_type=F32).astype(BF16).astype(F32)
             da2 = jnp.concatenate([da, da], axis=1)
@@ -190,13 +189,12 @@
     def back(dists, qs, hf):
         cols = pl.ds(hf * chunk, chunk)
 
-        @pl.loop(0, n_loc)
-        def _(e):
+        for e in range(n_loc):
             dh = jnp.concatenate([rows_of(dh_buf, e, q) for q in qs], axis=0)
             r = lax.dot_general(dh, wcat[e, cols, :], NT, preferred_element_type=F32).astype(BF16)
             for i in range(len(qs)):
                 for j in range(2):
-                    rbuf[i, j, pl.ds(pl.multiple_of(e * cap, cap), cap), :] = r[(i * 2 + j) * cap:(i * 2 + j + 1) * cap]
+                    rbuf[i, j, pl.ds(e * cap, cap), :] = r[(i * 2 + j) * cap:(i * 2 + j + 1) * cap]
 
         for i, q in enumerate(qs):
             psend[q, hf] = jnp.dot(pt[q * 2 + 1 - c], rbuf[i, 1 - c], preferred_element_type=F32)
@@ -327,26 +325,22 @@
 
     def copies(i):
         e, j, b = i // js, i % js, i % BUFS
-        rows, arows = pl.ds(pl.multiple_of(j * xc, xc), xc), pl.ds(pl.multiple_of(j * ac, ac), ac)
+        rows, arows = pl.ds(j * xc, xc), pl.ds(j * ac, ac)
         return (pltpu.make_async_copy(gbuf.at[b, :, pl.ds(0, ffn)], gwg.at[e, rows, :], sem.at[b, 0]),
                 pltpu.make_async_copy(gbuf.at[b, :, pl.ds(ffn, ffn)], gwu.at[e, rows, :], sem.at[b, 1]),
                 pltpu.make_async_copy(dbuf.at[b], gwd.at[e, arows, :], sem.at[b, 2]))
 
-    @pl.loop(0, n_loc * js)
-    def _(i):
+    steps = n_loc * js
+    for i in range(steps):
         e, j, b = i // js, i % js, i % BUFS
-
-        @pl.when(i >= BUFS)
-        def _():
+        if i >= BUFS:
             for cp in copies(i - BUFS):
                 cp.wait()
-
-        gbuf[b] = lax.dot_general(x_ref[e, :, pl.ds(pl.multiple_of(j * xc, xc), xc)], dh_ref[e], TN, preferred_element_type=F32)
-        dbuf[b] = lax.dot_general(a_ref[e, :, pl.ds(pl.multiple_of(j * ac, ac), ac)], d_ref[e], TN, preferred_element_type=F32)
+        gbuf[b] = lax.dot_general(x_ref[e, :, pl.ds(j * xc, xc)], dh_ref[e], TN, preferred_element_type=F32)
+        dbuf[b] = lax.dot_general(a_ref[e, :, pl.ds(j * ac, ac)], d_ref[e], TN, preferred_element_type=F32)
         for cp in copies(i):
             cp.start()
-
-    for i in range(n_loc * js - BUFS, n_loc * js):
+    for i in range(steps - BUFS, steps):
         for cp in copies(i):
             cp.wait()
 
@@ -407,7 +401,7 @@
             compiler_params=pltpu.CompilerParams(collective_id=0, has_side_effects=True, vmem_limit_bytes=44 * 1024 * 1024),
             name="exchange",
         )(pair_counts, gate_vals.T, topk_idx.T, slot_ids.T, grad_y, y_routed, h_gate, h_up, w_gate, w_up, w_down, x_disp)
-        js = 4
+        js = 2
         ring_r = [(i, ((i // 2 + 1) % n_chip) * 2 + i % 2) for i in range(n_dev)]
         from_l = lax.ppermute(tail_r, "ep", ring_r)
         from_r = lax.ppermute(tail_l, "ep", [(b, a) for a, b in ring_r])
@@ -418,7 +412,7 @@
             in_specs=[vm] * 5,
             out_specs=(vm, hbm, hbm, hbm),
             scratch_shapes=[pltpu.VMEM((BUFS, model // js, 2 * ffn), F32), pltpu.VMEM((BUFS, ffn // js, model), F32), dma((BUFS, 3))],
-            compiler_params=pltpu.CompilerParams(vmem_limit_bytes=20 * 1024 * 1024),
+            compiler_params=pltpu.CompilerParams(vmem_limit_bytes=24 * 1024 * 1024),
             cost_estimate=pl.CostEstimate(flops=6 * n_loc * rows * model * ffn, bytes_accessed=12 * n_loc * model * ffn, transcendentals=0),
             name="weights",
         )(x_rows, dh, act, d_rows, gg)

time: 58.7 us -> 50.7 us (0.86)
  Pallas kernels: 54.7 us -> 46.6 us
    pallas_call x1, Pallas kernels: 42.3 us -> 36 us  [local_step(): pl.pallas_call(functools.partial(exchange_kernel, n_dev, cap), out_shape=...]
    pallas_call x1, Pallas kernels: 11.5 us -> 9.8 us  [local_step(): pl.pallas_call(functools.partial(weight_kernel, js), out_shape=(jax.Shape...]
    ppermute x1, starting transfers between devices: 0.69 us -> 0.1 us  [local_step(): from_l = lax.ppermute(tail_r, 'ep', ring_r)]
  transfers between devices with their start and end apart: 2 -> 2, of which waited for: 0 -> 0; matrix products, arithmetic and copies ran while one was open for 0% -> 0% of each run, Pallas kernels for 20% -> 19%
where the time goes in v7:
time: 50.7 us; the launch traced here: 50.6 us
  Pallas kernels  46.6 us (92%)
  starting transfers between devices  3.31 us (7%)
  between operations  0.68 us (1%)
    pallas_call x1, Pallas kernels, local_step(): pl.pallas_call(functools.partial(exchange_kernel, n_dev, cap), out_shape=...  36 us
    pallas_call x1, Pallas kernels, local_step(): pl.pallas_call(functools.partial(weight_kernel, js), out_shape=(jax.Shape...  9.8 us
    ppermute x1, starting transfers between devices, local_step(): from_r = lax.ppermute(tail_l, 'ep', [(b, a) for a, b in ring_r])  3.21 us
  transfers between devices with their start and end apart: 2, of which 0 were waited for; matrix products, arithmetic and copies ran while one was open for 0% of the time, Pallas kernels for 19%

profile of v7, /device:TPU:112, one launch (start us, length us, event | category | flops | bytes accessed | tf_op | source)
XLA Modules:
  0.0 50.6 jit_solution(18200319586668420830)
XLA Ops:
  0.6 36.0 %exchange.1 = (f32[4,128,256]{2,1,0:T(8,128)S(1)}, f32[4,128,128]{2,1,0:T(8,128)S(1)}, f32[4,128,128]{2,1,0:T(8,128)S(1)}, f32[8,128]{1,0:T(8,128)S(1)}, bf16[4,...) custom-call(s32[1,32]{1,0:T(1,128)} %counts_hbm.1, ...), custom_call_target="tpu_custom_call" | custom-call | tf_op jit(solution)/shard_map/exchange/pallas_call | solution.py:372
  36.7 0.1 collective-permute-start
  36.8 3.2 %collective-permute-start.1 = (f32[4,128,128]{2,1,0:T(8,128)S(1)}, f32[4,128,128]{2,1,0:T(8,128)S(1)}, u32[]{:S(2)}, u32[]{:S(2)}) collective-permute-start(f32[4,128,128]{2,1,0:T(8,128)S(1)} %get-tuple-element.19), channel_id=1, source_target_pairs={{2,0},{3,1},{4,2},{5,3},{6,4},{7,5},{0,6},{1,7},{10,8},{11,9},{12,... | collective-permute-start | bytes 786440 | tf_op jit(solution)/shard_map/ppermute | solution.py:407
  40.0 9.8 %weights.1 = (f32[8,128]{1,0:T(8,128)}, f32[4,1024,512]{2,1,0:T(8,128)}, f32[4,1024,512]{2,1,0:T(8,128)}, f32[4,512,1024]{2,1,0:T(8,128)}) custom-call(bf16[4,512,1024]{2,1,0:T(8,128)(2,1)S(1)} %get-tuple-element.20.x_ref, bf16[4,512,1024]{2,1,0:T(8,128)(2,1)S(1)} %get-tuple-element.21.dh_ref, bf16[4,512,512]{2,1,0:T(8,128)(2,1)S(1)} %get-tuple-element.22.a_ref, ...), custom_call_target="tpu_custom_call" | custom-call | flops 6442450944 | bytes 25165824 | tf_op jit(solution)/shard_map/weights/pallas_call | solution.py:408
  49.8 0.0 collective-permute-done.from_l
  49.8 0.0 collective-permute-done.1.from_r
  49.8 0.8 %finish.1 = bf16[128,1024]{1,0:T(8,128)(2,1)} custom-call(f32[4,128,256]{2,1,0:T(8,128)S(1)} %get-tuple-element.17.base, f32[4,128,128]{2,1,0:T(8,128)S(1)} %collective-permute-done.from_l, f32[4,128,128]{2,1,0:T(8,128)S(1)} %collective-permute-done.1.from_r), custom_call_target="tpu_custom_call" | custom-call | tf_op jit(solution)/shard_map/finish/pallas_call | solution.py:419
Async XLA Ops:
  36.7 13.1 %collective-permute-start = (f32[4,128,128]{2,1,0:T(8,128)S(1)}, f32[4,128,128]{2,1,0:T(8,128)S(1)}, u32[]{:S(2)}, u32[]{:S(2)}) collective-permute-start(f32[4,128,128]{2,1,0:T(8,128)S(1)} %get-tuple-element.18), channel_id=1, source_target_pairs={{0,2},{1,3},{2,4},{3,5},{4,6},{5,7},{6,0},{7,1},{8,10},{9,11},{10,... | collective-permute-start | bytes 786440 | tf_op jit(solution)/shard_map/ppermute | solution.py:406
  36.8 13.0 %collective-permute-start.1 = (f32[4,128,128]{2,1,0:T(8,128)S(1)}, f32[4,128,128]{2,1,0:T(8,128)S(1)}, u32[]{:S(2)}, u32[]{:S(2)}) collective-permute-start(f32[4,128,128]{2,1,0:T(8,128)S(1)} %get-tuple-element.19), channel_id=1, source_target_pairs={{2,0},{3,1},{4,2},{5,3},{6,4},{7,5},{0,6},{1,7},{10,8},{11,9},{12,... | collective-permute-start | bytes 786440 | tf_op jit(solution)/shard_map/ppermute | solution.py:407

commit v8 on v7

--- a/solution.py
+++ b/solution.py
@@ -68,17 +68,14 @@
         cp.start()
         return cp
 
+    ld_gy = load(gy_hbm, gy_all.at[me], 0)
     ld_small = (load(counts_hbm, counts, 8), load(idx_hbm, idx, 9), load(slot_hbm, slot, 10), load(gates_hbm, meta.at[me, 0], 11))
-    ld_gy = load(gy_hbm, gy_all.at[me], 0)
-    ld_h1 = load(h1_hbm, h1, 2)
-    ld_h3 = load(h3_hbm, h3, 3)
-    ld_wd = load(wd_hbm, wd, 4)
-    ld_wg = load(wg_hbm, wcat.at[:, :, pl.ds(0, ffn)], 5)
-    ld_wu = load(wu_hbm, wcat.at[:, :, pl.ds(ffn, ffn)], 6)
-
     barrier = pltpu.get_barrier_semaphore()
     for r in range(1, n_dev):
         pl.semaphore_signal(barrier, inc=1, device_id=dev((me + r) % n_dev), device_id_type=MESH)
+
+    ld_h1 = load(h1_hbm, h1, 2)
+    ld_h3 = load(h3_hbm, h3, 3)
 
     def gy_copy(block, lo, n, s, to):
         ref = gy_all.at[block, pl.ds(lo, n), :]
@@ -105,6 +102,9 @@
     ld_gy.wait()
     for cp in (to_r0, to_l1, to_p):
         cp.start()
+    ld_wd = load(wd_hbm, wd, 4)
+    ld_wg = load(wg_hbm, wcat.at[:, :, pl.ds(0, ffn)], 5)
+    ld_wu = load(wu_hbm, wcat.at[:, :, pl.ds(ffn, ffn)], 6)
 
     for cp in ld_small:
         cp.wait()
@@ -257,8 +257,6 @@
     p_l1.start()
     to_l0.wait_recv()
     p_r0.start()
-    ld_x = load(x_hbm, x_buf, 7)
-    ld_yr = load(yr_hbm, yr, 1)
     meta_wait(-1)
     meta_wait(1)
     build(left)
@@ -274,17 +272,19 @@
     hidden(near)
     back((-1, 1), near, 0)
     back((-1, 1), near, 1)
+    ring_step(0, 0)
     fw_r.wait_recv()
     p_f0.start()
     fw_l.wait_recv()
     p_f1.start()
-    ring_step(0, 0)
     for s in range(2, SUBS):
         back((-1, 1), near, s)
         ring_step(0, s - 1)
     meta_wait(2)
     build(far)
     ring_step(0, SUBS - 1)
+    ld_x = load(x_hbm, x_buf, 7)
+    ld_yr = load(yr_hbm, yr, 1)
     p_f0.wait_recv()
     p_f1.wait_recv()
     build(chip(2) * 2 + 1 - c)
@@ -330,16 +330,28 @@
                 pltpu.make_async_copy(gbuf.at[b, :, pl.ds(ffn, ffn)], gwu.at[e, rows, :], sem.at[b, 1]),
                 pltpu.make_async_copy(dbuf.at[b], gwd.at[e, arows, :], sem.at[b, 2]))
 
-    steps = n_loc * js
-    for i in range(steps):
+    def gate_up(i):
         e, j, b = i // js, i % js, i % BUFS
         if i >= BUFS:
-            for cp in copies(i - BUFS):
+            for cp in copies(i - BUFS)[:2]:
                 cp.wait()
         gbuf[b] = lax.dot_general(x_ref[e, :, pl.ds(j * xc, xc)], dh_ref[e], TN, preferred_element_type=F32)
+        for cp in copies(i)[:2]:
+            cp.start()
+
+    def down(i):
+        e, j, b = i // js, i % js, i % BUFS
+        if i >= BUFS:
+            copies(i - BUFS)[2].wait()
         dbuf[b] = lax.dot_general(a_ref[e, :, pl.ds(j * ac, ac)], d_ref[e], TN, preferred_element_type=F32)
-        for cp in copies(i):
-            cp.start()
+        copies(i)[2].start()
+
+    steps = n_loc * js
+    for i in range(steps - 1):
+        down(i)
+        gate_up(i)
+    gate_up(steps - 1)
+    down(steps - 1)
     for i in range(steps - BUFS, steps):
         for cp in copies(i):
             cp.wait()

time: 50.7 us -> 51.4 us (1.014)
  Pallas kernels: 46.6 us -> 47.4 us
    pallas_call x1, Pallas kernels: 9.8 us -> 10.5 us  [local_step(): pl.pallas_call(functools.partial(weight_kernel, js), out_shape=(jax.Shape...]
  transfers between devices with their start and end apart: 2 -> 2, of which waited for: 0 -> 0; matrix products, arithmetic and copies ran while one was open for 0% -> 0% of each run, Pallas kernels for 19% -> 20%
where the time goes in v8:
time: 51.4 us
  Pallas kernels  47.4 us (92%)
  starting transfers between devices  3.31 us (6%)
  between operations  0.68 us (1%)
    pallas_call x1, Pallas kernels, local_step(): pl.pallas_call(functools.partial(exchange_kernel, n_dev, cap), out_shape=...  36.1 us
    pallas_call x1, Pallas kernels, local_step(): pl.pallas_call(functools.partial(weight_kernel, js), out_shape=(jax.Shape...  10.5 us
    ppermute x1, starting transfers between devices, local_step(): from_r = lax.ppermute(tail_l, 'ep', [(b, a) for a, b in ring_r])  3.21 us
  transfers between devices with their start and end apart: 2, of which 0 were waited for; matrix products, arithmetic and copies ran while one was open for 0% of the time, Pallas kernels for 20%

profile of v8, /device:TPU:112, one launch (start us, length us, event | category | flops | bytes accessed | tf_op | source)
XLA Modules:
  0.0 51.4 jit_solution(12757806605417938166)
XLA Ops:
  0.6 36.1 %exchange.1 = (f32[4,128,256]{2,1,0:T(8,128)S(1)}, f32[4,128,128]{2,1,0:T(8,128)S(1)}, f32[4,128,128]{2,1,0:T(8,128)S(1)}, f32[8,128]{1,0:T(8,128)S(1)}, bf16[4,...) custom-call(s32[1,32]{1,0:T(1,128)} %counts_hbm.1, ...), custom_call_target="tpu_custom_call" | custom-call | tf_op jit(solution)/shard_map/exchange/pallas_call | solution.py:384
  36.7 0.1 collective-permute-start
  36.8 3.2 %collective-permute-start.1 = (f32[4,128,128]{2,1,0:T(8,128)S(1)}, f32[4,128,128]{2,1,0:T(8,128)S(1)}, u32[]{:S(2)}, u32[]{:S(2)}) collective-permute-start(f32[4,128,128]{2,1,0:T(8,128)S(1)} %get-tuple-element.19), channel_id=1, source_target_pairs={{2,0},{3,1},{4,2},{5,3},{6,4},{7,5},{0,6},{1,7},{10,8},{11,9},{12,... | collective-permute-start | bytes 786440 | tf_op jit(solution)/shard_map/ppermute | solution.py:419
  40.0 10.5 %weights.1 = (f32[8,128]{1,0:T(8,128)}, f32[4,1024,512]{2,1,0:T(8,128)}, f32[4,1024,512]{2,1,0:T(8,128)}, f32[4,512,1024]{2,1,0:T(8,128)}) custom-call(bf16[4,512,1024]{2,1,0:T(8,128)(2,1)S(1)} %get-tuple-element.20.x_ref, bf16[4,512,1024]{2,1,0:T(8,128)(2,1)S(1)} %get-tuple-element.21.dh_ref, bf16[4,512,512]{2,1,0:T(8,128)(2,1)S(1)} %get-tuple-element.22.a_ref, ...), custom_call_target="tpu_custom_call" | custom-call | flops 6442450944 | bytes 25165824 | tf_op jit(solution)/shard_map/weights/pallas_call | solution.py:420
  50.6 0.0 collective-permute-done.from_l
  50.6 0.0 collective-permute-done.1.from_r
  50.6 0.8 %finish.1 = bf16[128,1024]{1,0:T(8,128)(2,1)} custom-call(f32[4,128,256]{2,1,0:T(8,128)S(1)} %get-tuple-element.17.base, f32[4,128,128]{2,1,0:T(8,128)S(1)} %collective-permute-done.from_l, f32[4,128,128]{2,1,0:T(8,128)S(1)} %collective-permute-done.1.from_r), custom_call_target="tpu_custom_call" | custom-call | tf_op jit(solution)/shard_map/finish/pallas_call | solution.py:431
Async XLA Ops:
  36.7 13.8 %collective-permute-start = (f32[4,128,128]{2,1,0:T(8,128)S(1)}, f32[4,128,128]{2,1,0:T(8,128)S(1)}, u32[]{:S(2)}, u32[]{:S(2)}) collective-permute-start(f32[4,128,128]{2,1,0:T(8,128)S(1)} %get-tuple-element.18), channel_id=1, source_target_pairs={{0,2},{1,3},{2,4},{3,5},{4,6},{5,7},{6,0},{7,1},{8,10},{9,11},{10,... | collective-permute-start | bytes 786440 | tf_op jit(solution)/shard_map/ppermute | solution.py:418
  36.8 13.8 %collective-permute-start.1 = (f32[4,128,128]{2,1,0:T(8,128)S(1)}, f32[4,128,128]{2,1,0:T(8,128)S(1)}, u32[]{:S(2)}, u32[]{:S(2)}) collective-permute-start(f32[4,128,128]{2,1,0:T(8,128)S(1)} %get-tuple-element.19), channel_id=1, source_target_pairs={{2,0},{3,1},{4,2},{5,3},{6,4},{7,5},{0,6},{1,7},{10,8},{11,9},{12,... | collective-permute-start | bytes 786440 | tf_op jit(solution)/shard_map/ppermute | solution.py:419

commit v9 on v7

--- a/solution.py
+++ b/solution.py
@@ -43,8 +43,8 @@
 
 
 def exchange_kernel(n_dev, cap, counts_hbm, gates_hbm, idx_hbm, slot_hbm, gy_hbm, yr_hbm, h1_hbm, h3_hbm, wg_hbm, wu_hbm, wd_hbm, x_hbm,
-                    base_out, tail_r, tail_l, gg_out, d_buf, dh_buf, a_buf, x_buf,
-                    counts, idx, slot, gy_all, yr, h1, h3, wcat, wd, fs, gg_rows, meta, pt, rbuf, own, psend, pairin, rsend, rrecv,
+                    base_out, tail_r, tail_l, gg_out, d_buf, dh_buf, a_buf, x_buf, pre_g, pre_d,
+                    counts, idx, slot, gy_all, yr, h1, h3, wcat, wd, fs, gg_rows, meta, pmat, grow, pt, rbuf, own, psend, pairin, rsend, rrecv,
                     loc_sem, meta_ssem, meta_rsem, ag_ssem, ag_rsem, pair_ssem, pair_rsem, ring_ssem, ring_rsem):
     n_loc, ffn, model = wd.shape
     top_k, tok = idx.shape
@@ -68,8 +68,8 @@
         cp.start()
         return cp
 
+    ld_gy = load(gy_hbm, gy_all.at[me], 0)
     ld_small = (load(counts_hbm, counts, 8), load(idx_hbm, idx, 9), load(slot_hbm, slot, 10), load(gates_hbm, meta.at[me, 0], 11))
-    ld_gy = load(gy_hbm, gy_all.at[me], 0)
     ld_h1 = load(h1_hbm, h1, 2)
     ld_h3 = load(h3_hbm, h3, 3)
     ld_wd = load(wd_hbm, wd, 4)
@@ -149,7 +149,7 @@
         fs[e, pl.ds(r, rstep), pl.ds(ffn, ffn)] = s
 
 
-    def build(h):
+    def prep(h):
         rel = meta[h, 1] - (me * (n_loc * cap)).astype(F32)
         gate = meta[h, 0]
         rows = lax.broadcasted_iota(jnp.int32, (n_loc * cap, tok), 0).astype(F32)
@@ -159,10 +159,13 @@
             hit = rows == rel[k:k + 1, :]
             sel = jnp.where(hit, 1.0, sel)
             gsel = jnp.where(hit, gate[k:k + 1, :], gsel)
-        grow = jnp.sum(gsel, axis=1, keepdims=True)
+        grow[h] = jnp.sum(gsel, axis=1, keepdims=True)
+        pmat[h] = sel.astype(BF16)
         pt[h] = sel.T.astype(BF16)
-        picked = jnp.dot(sel.astype(BF16), gy_all[h], preferred_element_type=F32)
-        rows_d = (grow * picked).astype(BF16)
+
+    def build(h):
+        picked = jnp.dot(pmat[h], gy_all[h], preferred_element_type=F32)
+        rows_d = (grow[h] * picked).astype(BF16)
         for e in range(n_loc):
             d_buf[e, pl.ds(pl.multiple_of(h * cap, cap), cap), :] = rows_d[e * cap:(e + 1) * cap]
 
@@ -239,17 +242,23 @@
             cp.finish()
 
     meta_wait(0)
+    prep(x * 2)
+    prep(x * 2 + 1)
     to_p.wait_recv()
     build(x * 2)
     build(x * 2 + 1)
+    ld_wd.wait()
+    hidden([x])
     to_r0.wait_recv()
     fw_r.start()
     p_l0.start()
     to_l1.wait_recv()
     fw_l.start()
     p_r1.start()
-    ld_wd.wait()
-    hidden([x])
+    for d in (-1, 1):
+        meta_wait(d)
+        for i in range(2):
+            prep(chip(d) * 2 + i)
     ld_wg.wait()
     ld_wu.wait()
     back((0,), [x], 0)
@@ -257,13 +266,11 @@
     p_l1.start()
     to_l0.wait_recv()
     p_r0.start()
-    ld_x = load(x_hbm, x_buf, 7)
-    ld_yr = load(yr_hbm, yr, 1)
-    meta_wait(-1)
-    meta_wait(1)
     build(left)
     build(right)
-    back((0,), [x], 1)
+    meta_wait(2)
+    prep(chip(2) * 2)
+    prep(chip(2) * 2 + 1)
     p_l0.wait_recv()
     p_l1.wait_recv()
     build(chip(-1) * 2 + 1 - c)
@@ -274,17 +281,18 @@
     hidden(near)
     back((-1, 1), near, 0)
     back((-1, 1), near, 1)
+    ring_step(0, 0)
     fw_r.wait_recv()
     p_f0.start()
     fw_l.wait_recv()
     p_f1.start()
-    ring_step(0, 0)
     for s in range(2, SUBS):
         back((-1, 1), near, s)
         ring_step(0, s - 1)
-    meta_wait(2)
     build(far)
     ring_step(0, SUBS - 1)
+    ld_x = load(x_hbm, x_buf, 7)
+    ld_yr = load(yr_hbm, yr, 1)
     p_f0.wait_recv()
     p_f1.wait_recv()
     build(chip(2) * 2 + 1 - c)
@@ -294,7 +302,7 @@
         back((2,), [chip(2)], s)
         ring_step(1, s - 1)
     ring_step(1, SUBS - 1)
-    for s in range(2, SUBS):
+    for s in range(1, SUBS):
         back((0,), [x], s)
 
     ld_yr.wait()
@@ -312,13 +320,16 @@
     for s in range(SUBS):
         for dr in range(2):
             base_out[s, :, pl.ds(dr * width, width)] = pair_sum(0, s, dr)
+    ld_x.wait()
+    pre_g[...] = lax.dot_general(x_buf[0, :, pl.ds(0, pre_g.shape[0])], dh_buf[0], TN, preferred_element_type=F32)
+    pre_d[...] = lax.dot_general(a_buf[0, :, pl.ds(0, pre_d.shape[0])], d_buf[0], TN, preferred_element_type=F32)
     for s in range(SUBS):
         ring_step(2, s)
 
     finish()
 
 
-def weight_kernel(js, x_ref, dh_ref, a_ref, d_ref, gg_ref, gg_out, gwg, gwu, gwd, gbuf, dbuf, sem):
+def weight_kernel(js, x_ref, dh_ref, a_ref, d_ref, gg_ref, pre_g, pre_d, gg_out, gwg, gwu, gwd, gbuf, dbuf, sem):
     n_loc, model, ffn = gwg.shape
     xc, ac = model // js, ffn // js
     gg_out[...] = gg_ref[...]
@@ -326,9 +337,10 @@
     def copies(i):
         e, j, b = i // js, i % js, i % BUFS
         rows, arows = pl.ds(j * xc, xc), pl.ds(j * ac, ac)
-        return (pltpu.make_async_copy(gbuf.at[b, :, pl.ds(0, ffn)], gwg.at[e, rows, :], sem.at[b, 0]),
-                pltpu.make_async_copy(gbuf.at[b, :, pl.ds(ffn, ffn)], gwu.at[e, rows, :], sem.at[b, 1]),
-                pltpu.make_async_copy(dbuf.at[b], gwd.at[e, arows, :], sem.at[b, 2]))
+        g, d = (pre_g, pre_d) if i == 0 else (gbuf.at[b], dbuf.at[b])
+        return (pltpu.make_async_copy(g.at[:, pl.ds(0, ffn)], gwg.at[e, rows, :], sem.at[b, 0]),
+                pltpu.make_async_copy(g.at[:, pl.ds(ffn, ffn)], gwu.at[e, rows, :], sem.at[b, 1]),
+                pltpu.make_async_copy(d, gwd.at[e, arows, :], sem.at[b, 2]))
 
     steps = n_loc * js
     for i in range(steps):
@@ -336,8 +348,9 @@
         if i >= BUFS:
             for cp in copies(i - BUFS):
                 cp.wait()
-        gbuf[b] = lax.dot_general(x_ref[e, :, pl.ds(j * xc, xc)], dh_ref[e], TN, preferred_element_type=F32)
-        dbuf[b] = lax.dot_general(a_ref[e, :, pl.ds(j * ac, ac)], d_ref[e], TN, preferred_element_type=F32)
+        if i > 0:
+            gbuf[b] = lax.dot_general(x_ref[e, :, pl.ds(j * xc, xc)], dh_ref[e], TN, preferred_element_type=F32)
+            dbuf[b] = lax.dot_general(a_ref[e, :, pl.ds(j * ac, ac)], d_ref[e], TN, preferred_element_type=F32)
         for cp in copies(i):
             cp.start()
     for i in range(steps - BUFS, steps):
@@ -369,12 +382,14 @@
         dma = pltpu.SemaphoreType.DMA
         vs = pltpu.VMEM
         tail = vs((SUBS, tok, model // 2 // SUBS), F32)
-        base, tail_r, tail_l, gg, d_rows, dh, act, x_rows = pl.pallas_call(
+        js = 2
+        base, tail_r, tail_l, gg, d_rows, dh, act, x_rows, pre_g, pre_d = pl.pallas_call(
             functools.partial(exchange_kernel, n_dev, cap),
             out_shape=(vs((SUBS, tok, model // SUBS), F32), tail, tail, pltpu.VMEM((top_k, tok), F32), pltpu.VMEM((n_loc, rows, model), BF16),
-                       pltpu.VMEM((n_loc, rows, 2 * ffn), BF16), pltpu.VMEM((n_loc, rows, ffn), BF16), pltpu.VMEM((n_loc, rows, model), BF16)),
+                       pltpu.VMEM((n_loc, rows, 2 * ffn), BF16), pltpu.VMEM((n_loc, rows, ffn), BF16), pltpu.VMEM((n_loc, rows, model), BF16),
+                       vs((model // js, 2 * ffn), F32), vs((ffn // js, model), F32)),
             in_specs=[hbm] * 12,
-            out_specs=(vm,) * 8,
+            out_specs=(vm,) * 10,
             scratch_shapes=[
                 pltpu.SMEM(pair_counts.shape, jnp.int32),
                 pltpu.VMEM((top_k, tok), jnp.int32),
@@ -388,6 +403,8 @@
                 pltpu.VMEM((n_loc, rows, 2 * ffn), F32),
                 pltpu.VMEM((tok, top_k), F32),
                 pltpu.VMEM((n_dev, 2, top_k, tok), F32),
+                pltpu.VMEM((n_dev, n_loc * cap, tok), BF16),
+                pltpu.VMEM((n_dev, n_loc * cap, 1), F32),
                 pltpu.VMEM((n_dev, tok, n_loc * cap), BF16),
                 pltpu.VMEM((2, 2, n_loc * cap, model // SUBS), BF16),
                 pltpu.VMEM((n_chip, SUBS, tok, model // SUBS), F32),
@@ -398,10 +415,9 @@
                 dma((12,)), dma((n_dev - 1,)), dma((n_dev - 1,)), dma((13,)), dma((13,)),
                 dma((SUBS * n_chip,)), dma((SUBS * n_chip,)), dma((4 * SUBS,)), dma((4 * SUBS,)),
             ],
-            compiler_params=pltpu.CompilerParams(collective_id=0, has_side_effects=True, vmem_limit_bytes=44 * 1024 * 1024),
+            compiler_params=pltpu.CompilerParams(collective_id=0, has_side_effects=True, vmem_limit_bytes=43 * 1024 * 1024),
             name="exchange",
         )(pair_counts, gate_vals.T, topk_idx.T, slot_ids.T, grad_y, y_routed, h_gate, h_up, w_gate, w_up, w_down, x_disp)
-        js = 2
         ring_r = [(i, ((i // 2 + 1) % n_chip) * 2 + i % 2) for i in range(n_dev)]
         from_l = lax.ppermute(tail_r, "ep", ring_r)
         from_r = lax.ppermute(tail_l, "ep", [(b, a) for a, b in ring_r])
@@ -409,13 +425,13 @@
             functools.partial(weight_kernel, js),
             out_shape=(jax.ShapeDtypeStruct((top_k, tok), F32), jax.ShapeDtypeStruct((n_loc, model, ffn), F32),
                        jax.ShapeDtypeStruct((n_loc, model, ffn), F32), jax.ShapeDtypeStruct((n_loc, ffn, model), F32)),
-            in_specs=[vm] * 5,
+            in_specs=[vm] * 7,
             out_specs=(vm, hbm, hbm, hbm),
             scratch_shapes=[pltpu.VMEM((BUFS, model // js, 2 * ffn), F32), pltpu.VMEM((BUFS, ffn // js, model), F32), dma((BUFS, 3))],
-            compiler_params=pltpu.CompilerParams(vmem_limit_bytes=24 * 1024 * 1024),
+            compiler_params=pltpu.CompilerParams(vmem_limit_bytes=20 * 1024 * 1024),
             cost_estimate=pl.CostEstimate(flops=6 * n_loc * rows * model * ffn, bytes_accessed=12 * n_loc * model * ffn, transcendentals=0),
             name="weights",
-        )(x_rows, dh, act, d_rows, gg)
+        )(x_rows, dh, act, d_rows, gg, pre_g, pre_d)
         gx = pl.pallas_call(
             finish_kernel,
             out_shape=jax.ShapeDtypeStruct((tok, model), BF16),

time: 50.7 us -> 50.1 us (0.988)
    ppermute x1, starting transfers between devices: 0.1 us -> 1.13 us  [local_step(): from_l = lax.ppermute(tail_r, 'ep', ring_r)]
    ppermute x1, starting transfers between devices: 3.21 us -> 2.18 us  [local_step(): from_r = lax.ppermute(tail_l, 'ep', [(b, a) for a, b in ring_r])]
    pallas_call x1, Pallas kernels: 36 us -> 35.5 us  [local_step(): pl.pallas_call(functools.partial(exchange_kernel, n_dev, cap), out_shape=...]
where the time goes in v9:
time: 50.1 us
  Pallas kernels  46.1 us (92%)
  starting transfers between devices  3.31 us (7%)
  between operations  0.67 us (1%)
    pallas_call x1, Pallas kernels, local_step(): pl.pallas_call(functools.partial(exchange_kernel, n_dev, cap), out_shape=...  35.5 us
    pallas_call x1, Pallas kernels, local_step(): pl.pallas_call(functools.partial(weight_kernel, js), out_shape=(jax.Shape...  9.76 us
    ppermute x1, starting transfers between devices, local_step(): from_r = lax.ppermute(tail_l, 'ep', [(b, a) for a, b in ring_r])  2.18 us
    ppermute x1, starting transfers between devices, local_step(): from_l = lax.ppermute(tail_r, 'ep', ring_r)  1.13 us
  transfers between devices with their start and end apart: 2, of which 0 were waited for; matrix products, arithmetic and copies ran while one was open for 0% of the time, Pallas kernels for 19%

profile of v9, /device:TPU:112, one launch (start us, length us, event | category | flops | bytes accessed | tf_op | source)
XLA Modules:
  0.0 50.1 jit_solution(395577266659114957)
XLA Ops:
  0.6 35.5 %exchange.1 = (f32[4,128,256]{2,1,0:T(8,128)S(1)}, f32[4,128,128]{2,1,0:T(8,128)S(1)}, f32[4,128,128]{2,1,0:T(8,128)S(1)}, f32[8,128]{1,0:T(8,128)S(1)}, bf16[4,...) custom-call(s32[1,32]{1,0:T(1,128)} %counts_hbm.1, ...), custom_call_target="tpu_custom_call" | custom-call | tf_op jit(solution)/shard_map/exchange/pallas_call | solution.py:386
  36.2 1.1 %collective-permute-start = (f32[4,128,128]{2,1,0:T(8,128)S(1)}, f32[4,128,128]{2,1,0:T(8,128)S(1)}, u32[]{:S(2)}, u32[]{:S(2)}) collective-permute-start(f32[4,128,128]{2,1,0:T(8,128)S(1)} %get-tuple-element.20), channel_id=1, source_target_pairs={{0,2},{1,3},{2,4},{3,5},{4,6},{5,7},{6,0},{7,1},{8,10},{9,11},{10,... | collective-permute-start | bytes 786440 | tf_op jit(solution)/shard_map/ppermute | solution.py:422
  37.3 2.2 %collective-permute-start.1 = (f32[4,128,128]{2,1,0:T(8,128)S(1)}, f32[4,128,128]{2,1,0:T(8,128)S(1)}, u32[]{:S(2)}, u32[]{:S(2)}) collective-permute-start(f32[4,128,128]{2,1,0:T(8,128)S(1)} %get-tuple-element.21), channel_id=1, source_target_pairs={{2,0},{3,1},{4,2},{5,3},{6,4},{7,5},{0,6},{1,7},{10,8},{11,9},{12,... | collective-permute-start | bytes 786440 | tf_op jit(solution)/shard_map/ppermute | solution.py:423
  39.5 9.8 %weights.1 = (f32[8,128]{1,0:T(8,128)}, f32[4,1024,512]{2,1,0:T(8,128)}, f32[4,1024,512]{2,1,0:T(8,128)}, f32[4,512,1024]{2,1,0:T(8,128)}) custom-call(bf16[4,512,1024]{2,1,0:T(8,128)(2,1)S(1)} %get-tuple-element.22.x_ref, bf16[4,512,1024]{2,1,0:T(8,128)(2,1)S(1)} %get-tuple-element.23.dh_ref, bf16[4,512,512]{2,1,0:T(8,128)(2,1)S(1)} %get-tuple-element.24.a_ref, ...), custom_call_target="tpu_custom_call" | custom-call | flops 6442450944 | bytes 25165824 | tf_op jit(solution)/shard_map/weights/pallas_call | solution.py:424
  49.2 0.0 collective-permute-done.from_l
  49.3 0.0 collective-permute-done.1.from_r
  49.3 0.8 %finish.1 = bf16[128,1024]{1,0:T(8,128)(2,1)} custom-call(f32[4,128,256]{2,1,0:T(8,128)S(1)} %get-tuple-element.19.base, f32[4,128,128]{2,1,0:T(8,128)S(1)} %collective-permute-done.from_l, f32[4,128,128]{2,1,0:T(8,128)S(1)} %collective-permute-done.1.from_r), custom_call_target="tpu_custom_call" | custom-call | tf_op jit(solution)/shard_map/finish/pallas_call | solution.py:435
Async XLA Ops:
  36.2 13.1 %collective-permute-start = (f32[4,128,128]{2,1,0:T(8,128)S(1)}, f32[4,128,128]{2,1,0:T(8,128)S(1)}, u32[]{:S(2)}, u32[]{:S(2)}) collective-permute-start(f32[4,128,128]{2,1,0:T(8,128)S(1)} %get-tuple-element.20), channel_id=1, source_target_pairs={{0,2},{1,3},{2,4},{3,5},{4,6},{5,7},{6,0},{7,1},{8,10},{9,11},{10,... | collective-permute-start | bytes 786440 | tf_op jit(solution)/shard_map/ppermute | solution.py:422
  37.3 12.0 %collective-permute-start.1 = (f32[4,128,128]{2,1,0:T(8,128)S(1)}, f32[4,128,128]{2,1,0:T(8,128)S(1)}, u32[]{:S(2)}, u32[]{:S(2)}) collective-permute-start(f32[4,128,128]{2,1,0:T(8,128)S(1)} %get-tuple-element.21), channel_id=1, source_target_pairs={{2,0},{3,1},{4,2},{5,3},{6,4},{7,5},{0,6},{1,7},{10,8},{11,9},{12,... | collective-permute-start | bytes 786440 | tf_op jit(solution)/shard_map/ppermute | solution.py:423

commit v10 on v9

--- a/solution.py
+++ b/solution.py
@@ -43,7 +43,7 @@
 
 
 def exchange_kernel(n_dev, cap, counts_hbm, gates_hbm, idx_hbm, slot_hbm, gy_hbm, yr_hbm, h1_hbm, h3_hbm, wg_hbm, wu_hbm, wd_hbm, x_hbm,
-                    base_out, tail_r, tail_l, gg_out, d_buf, dh_buf, a_buf, x_buf, pre_g, pre_d,
+                    base_out, tail_r, tail_l, gg_out, d_buf, dh_buf, a_buf, x_buf,
                     counts, idx, slot, gy_all, yr, h1, h3, wcat, wd, fs, gg_rows, meta, pmat, grow, pt, rbuf, own, psend, pairin, rsend, rrecv,
                     loc_sem, meta_ssem, meta_rsem, ag_ssem, ag_rsem, pair_ssem, pair_rsem, ring_ssem, ring_rsem):
     n_loc, ffn, model = wd.shape
@@ -261,7 +261,8 @@
             prep(chip(d) * 2 + i)
     ld_wg.wait()
     ld_wu.wait()
-    back((0,), [x], 0)
+    for s in range(3):
+        back((0,), [x], s)
     to_r1.wait_recv()
     p_l1.start()
     to_l0.wait_recv()
@@ -302,8 +303,7 @@
         back((2,), [chip(2)], s)
         ring_step(1, s - 1)
     ring_step(1, SUBS - 1)
-    for s in range(1, SUBS):
-        back((0,), [x], s)
+    back((0,), [x], 3)
 
     ld_yr.wait()
     step = 16
@@ -320,16 +320,13 @@
     for s in range(SUBS):
         for dr in range(2):
             base_out[s, :, pl.ds(dr * width, width)] = pair_sum(0, s, dr)
-    ld_x.wait()
-    pre_g[...] = lax.dot_general(x_buf[0, :, pl.ds(0, pre_g.shape[0])], dh_buf[0], TN, preferred_element_type=F32)
-    pre_d[...] = lax.dot_general(a_buf[0, :, pl.ds(0, pre_d.shape[0])], d_buf[0], TN, preferred_element_type=F32)
     for s in range(SUBS):
         ring_step(2, s)
 
     finish()
 
 
-def weight_kernel(js, x_ref, dh_ref, a_ref, d_ref, gg_ref, pre_g, pre_d, gg_out, gwg, gwu, gwd, gbuf, dbuf, sem):
+def weight_kernel(js, x_ref, dh_ref, a_ref, d_ref, gg_ref, gg_out, gwg, gwu, gwd, gbuf, dbuf, sem):
     n_loc, model, ffn = gwg.shape
     xc, ac = model // js, ffn // js
     gg_out[...] = gg_ref[...]
@@ -337,10 +334,9 @@
     def copies(i):
         e, j, b = i // js, i % js, i % BUFS
         rows, arows = pl.ds(j * xc, xc), pl.ds(j * ac, ac)
-        g, d = (pre_g, pre_d) if i == 0 else (gbuf.at[b], dbuf.at[b])
-        return (pltpu.make_async_copy(g.at[:, pl.ds(0, ffn)], gwg.at[e, rows, :], sem.at[b, 0]),
-                pltpu.make_async_copy(g.at[:, pl.ds(ffn, ffn)], gwu.at[e, rows, :], sem.at[b, 1]),
-                pltpu.make_async_copy(d, gwd.at[e, arows, :], sem.at[b, 2]))
+        return (pltpu.make_async_copy(gbuf.at[b, :, pl.ds(0, ffn)], gwg.at[e, rows, :], sem.at[b, 0]),
+                pltpu.make_async_copy(gbuf.at[b, :, pl.ds(ffn, ffn)], gwu.at[e, rows, :], sem.at[b, 1]),
+                pltpu.make_async_copy(dbuf.at[b], gwd.at[e, arows, :], sem.at[b, 2]))
 
     steps = n_loc * js
     for i in range(steps):
@@ -348,9 +344,8 @@
         if i >= BUFS:
             for cp in copies(i - BUFS):
                 cp.wait()
-        if i > 0:
-            gbuf[b] = lax.dot_general(x_ref[e, :, pl.ds(j * xc, xc)], dh_ref[e], TN, preferred_element_type=F32)
-            dbuf[b] = lax.dot_general(a_ref[e, :, pl.ds(j * ac, ac)], d_ref[e], TN, preferred_element_type=F32)
+        gbuf[b] = lax.dot_general(x_ref[e, :, pl.ds(j * xc, xc)], dh_ref[e], TN, preferred_element_type=F32)
+        dbuf[b] = lax.dot_general(a_ref[e, :, pl.ds(j * ac, ac)], d_ref[e], TN, preferred_element_type=F32)
         for cp in copies(i):
             cp.start()
     for i in range(steps - BUFS, steps):
@@ -383,13 +378,12 @@
         vs = pltpu.VMEM
         tail = vs((SUBS, tok, model // 2 // SUBS), F32)
         js = 2
-        base, tail_r, tail_l, gg, d_rows, dh, act, x_rows, pre_g, pre_d = pl.pallas_call(
+        base, tail_r, tail_l, gg, d_rows, dh, act, x_rows = pl.pallas_call(
             functools.partial(exchange_kernel, n_dev, cap),
             out_shape=(vs((SUBS, tok, model // SUBS), F32), tail, tail, pltpu.VMEM((top_k, tok), F32), pltpu.VMEM((n_loc, rows, model), BF16),
-                       pltpu.VMEM((n_loc, rows, 2 * ffn), BF16), pltpu.VMEM((n_loc, rows, ffn), BF16), pltpu.VMEM((n_loc, rows, model), BF16),
-                       vs((model // js, 2 * ffn), F32), vs((ffn // js, model), F32)),
+                       pltpu.VMEM((n_loc, rows, 2 * ffn), BF16), pltpu.VMEM((n_loc, rows, ffn), BF16), pltpu.VMEM((n_loc, rows, model), BF16)),
             in_specs=[hbm] * 12,
-            out_specs=(vm,) * 10,
+            out_specs=(vm,) * 8,
             scratch_shapes=[
                 pltpu.SMEM(pair_counts.shape, jnp.int32),
                 pltpu.VMEM((top_k, tok), jnp.int32),
@@ -415,7 +409,7 @@
                 dma((12,)), dma((n_dev - 1,)), dma((n_dev - 1,)), dma((13,)), dma((13,)),
                 dma((SUBS * n_chip,)), dma((SUBS * n_chip,)), dma((4 * SUBS,)), dma((4 * SUBS,)),
             ],
-            compiler_params=pltpu.CompilerParams(collective_id=0, has_side_effects=True, vmem_limit_bytes=43 * 1024 * 1024),
+            compiler_params=pltpu.CompilerParams(collective_id=0, has_side_effects=True, vmem_limit_bytes=44 * 1024 * 1024),
             name="exchange",
         )(pair_counts, gate_vals.T, topk_idx.T, slot_ids.T, grad_y, y_routed, h_gate, h_up, w_gate, w_up, w_down, x_disp)
         ring_r = [(i, ((i // 2 + 1) % n_chip) * 2 + i % 2) for i in range(n_dev)]
@@ -425,13 +419,13 @@
             functools.partial(weight_kernel, js),
             out_shape=(jax.ShapeDtypeStruct((top_k, tok), F32), jax.ShapeDtypeStruct((n_loc, model, ffn), F32),
                        jax.ShapeDtypeStruct((n_loc, model, ffn), F32), jax.ShapeDtypeStruct((n_loc, ffn, model), F32)),
-            in_specs=[vm] * 7,
+            in_specs=[vm] * 5,
             out_specs=(vm, hbm, hbm, hbm),
             scratch_shapes=[pltpu.VMEM((BUFS, model // js, 2 * ffn), F32), pltpu.VMEM((BUFS, ffn // js, model), F32), dma((BUFS, 3))],
-            compiler_params=pltpu.CompilerParams(vmem_limit_bytes=20 * 1024 * 1024),
+            compiler_params=pltpu.CompilerParams(vmem_limit_bytes=24 * 1024 * 1024),
             cost_estimate=pl.CostEstimate(flops=6 * n_loc * rows * model * ffn, bytes_accessed=12 * n_loc * model * ffn, transcendentals=0),
             name="weights",
-        )(x_rows, dh, act, d_rows, gg, pre_g, pre_d)
+        )(x_rows, dh, act, d_rows, gg)
         gx = pl.pallas_call(
             finish_kernel,
             out_shape=jax.ShapeDtypeStruct((tok, model), BF16),

time: 50.1 us -> 50.4 us (level)
    ppermute x1, starting transfers between devices: 1.13 us -> 0.1 us  [local_step(): from_l = lax.ppermute(tail_r, 'ep', ring_r)]
    ppermute x1, starting transfers between devices: 2.18 us -> 3.21 us  [local_step(): from_r = lax.ppermute(tail_l, 'ep', [(b, a) for a, b in ring_r])]
where the time goes in v10:
time: 50.4 us
  Pallas kernels  46.4 us (92%)
  starting transfers between devices  3.31 us (7%)
  between operations  0.68 us (1%)
    pallas_call x1, Pallas kernels, local_step(): pl.pallas_call(functools.partial(exchange_kernel, n_dev, cap), out_shape=...  35.8 us
    pallas_call x1, Pallas kernels, local_step(): pl.pallas_call(functools.partial(weight_kernel, js), out_shape=(jax.Shape...  9.81 us
    ppermute x1, starting transfers between devices, local_step(): from_r = lax.ppermute(tail_l, 'ep', [(b, a) for a, b in ring_r])  3.21 us
  transfers between devices with their start and end apart: 2, of which 0 were waited for; matrix products, arithmetic and copies ran while one was open for 0% of the time, Pallas kernels for 19%

profile of v10, /device:TPU:112, one launch (start us, length us, event | category | flops | bytes accessed | tf_op | source)
XLA Modules:
  0.0 50.4 jit_solution(2302881850039788311)
XLA Ops:
  0.6 35.8 %exchange.1 = (f32[4,128,256]{2,1,0:T(8,128)S(1)}, f32[4,128,128]{2,1,0:T(8,128)S(1)}, f32[4,128,128]{2,1,0:T(8,128)S(1)}, f32[8,128]{1,0:T(8,128)S(1)}, bf16[4,...) custom-call(s32[1,32]{1,0:T(1,128)} %counts_hbm.1, ...), custom_call_target="tpu_custom_call" | custom-call | tf_op jit(solution)/shard_map/exchange/pallas_call | solution.py:381
  36.4 0.1 collective-permute-start
  36.5 3.2 %collective-permute-start.1 = (f32[4,128,128]{2,1,0:T(8,128)S(1)}, f32[4,128,128]{2,1,0:T(8,128)S(1)}, u32[]{:S(2)}, u32[]{:S(2)}) collective-permute-start(f32[4,128,128]{2,1,0:T(8,128)S(1)} %get-tuple-element.19), channel_id=1, source_target_pairs={{2,0},{3,1},{4,2},{5,3},{6,4},{7,5},{0,6},{1,7},{10,8},{11,9},{12,... | collective-permute-start | bytes 786440 | tf_op jit(solution)/shard_map/ppermute | solution.py:417
  39.7 9.8 %weights.1 = (f32[8,128]{1,0:T(8,128)}, f32[4,1024,512]{2,1,0:T(8,128)}, f32[4,1024,512]{2,1,0:T(8,128)}, f32[4,512,1024]{2,1,0:T(8,128)}) custom-call(bf16[4,512,1024]{2,1,0:T(8,128)(2,1)S(1)} %get-tuple-element.20.x_ref, bf16[4,512,1024]{2,1,0:T(8,128)(2,1)S(1)} %get-tuple-element.21.dh_ref, bf16[4,512,512]{2,1,0:T(8,128)(2,1)S(1)} %get-tuple-element.22.a_ref, ...), custom_call_target="tpu_custom_call" | custom-call | flops 6442450944 | bytes 25165824 | tf_op jit(solution)/shard_map/weights/pallas_call | solution.py:418
  49.5 0.0 collective-permute-done.from_l
  49.6 0.0 collective-permute-done.1.from_r
  49.6 0.8 %finish.1 = bf16[128,1024]{1,0:T(8,128)(2,1)} custom-call(f32[4,128,256]{2,1,0:T(8,128)S(1)} %get-tuple-element.17.base, f32[4,128,128]{2,1,0:T(8,128)S(1)} %collective-permute-done.from_l, f32[4,128,128]{2,1,0:T(8,128)S(1)} %collective-permute-done.1.from_r), custom_call_target="tpu_custom_call" | custom-call | tf_op jit(solution)/shard_map/finish/pallas_call | solution.py:429
Async XLA Ops:
  36.4 13.1 %collective-permute-start = (f32[4,128,128]{2,1,0:T(8,128)S(1)}, f32[4,128,128]{2,1,0:T(8,128)S(1)}, u32[]{:S(2)}, u32[]{:S(2)}) collective-permute-start(f32[4,128,128]{2,1,0:T(8,128)S(1)} %get-tuple-element.18), channel_id=1, source_target_pairs={{0,2},{1,3},{2,4},{3,5},{4,6},{5,7},{6,0},{7,1},{8,10},{9,11},{10,... | collective-permute-start | bytes 786440 | tf_op jit(solution)/shard_map/ppermute | solution.py:416
  36.5 13.0 %collective-permute-start.1 = (f32[4,128,128]{2,1,0:T(8,128)S(1)}, f32[4,128,128]{2,1,0:T(8,128)S(1)}, u32[]{:S(2)}, u32[]{:S(2)}) collective-permute-start(f32[4,128,128]{2,1,0:T(8,128)S(1)} %get-tuple-element.19), channel_id=1, source_target_pairs={{2,0},{3,1},{4,2},{5,3},{6,4},{7,5},{0,6},{1,7},{10,8},{11,9},{12,... | collective-permute-start | bytes 786440 | tf_op jit(solution)/shard_map/ppermute | solution.py:417

commit v11 on v10

--- a/solution.py
+++ b/solution.py
@@ -43,7 +43,7 @@
 
 
 def exchange_kernel(n_dev, cap, counts_hbm, gates_hbm, idx_hbm, slot_hbm, gy_hbm, yr_hbm, h1_hbm, h3_hbm, wg_hbm, wu_hbm, wd_hbm, x_hbm,
-                    base_out, tail_r, tail_l, gg_out, d_buf, dh_buf, a_buf, x_buf,
+                    base_out, tail, gg_out, d_buf, dh_buf, a_buf, x_buf,
                     counts, idx, slot, gy_all, yr, h1, h3, wcat, wd, fs, gg_rows, meta, pmat, grow, pt, rbuf, own, psend, pairin, rsend, rrecv,
                     loc_sem, meta_ssem, meta_rsem, ag_ssem, ag_rsem, pair_ssem, pair_rsem, ring_ssem, ring_rsem):
     n_loc, ffn, model = wd.shape
@@ -185,11 +185,12 @@
                 dh = (da2[i * 2 * cap:(i + 1) * 2 * cap] * rows_of(fs, e, q)).astype(BF16)
                 dh_buf[e, pl.ds(pl.multiple_of(q * (2 * cap), 2 * cap), 2 * cap), :] = dh
 
+    sgn = 1 - 2 * c
     pair_cps = {}
 
     chunk = model // SUBS
 
-    def back(dists, qs, hf):
+    def back(roles, qs, hf):
         cols = pl.ds(hf * chunk, chunk)
 
         for e in range(n_loc):
@@ -201,41 +202,36 @@
 
         for i, q in enumerate(qs):
             psend[q, hf] = jnp.dot(pt[q * 2 + 1 - c], rbuf[i, 1 - c], preferred_element_type=F32)
-        for i, d in enumerate(dists):
-            cp = pair_copy(qs[i], ((d + n_chip) % n_chip) * SUBS + hf, hf)
+        for i, role in enumerate(roles):
+            cp = pair_copy(qs[i], role * SUBS + hf, hf)
             cp.start()
-            pair_cps[d, hf] = cp
+            pair_cps[role, hf] = cp
         for i, q in enumerate(qs):
             own[q, hf] = jnp.dot(pt[q * 2 + c], rbuf[i, c], preferred_element_type=F32)
 
-    width = half // SUBS
-
-    def ring_copy(dr, st, s):
-        k = (dr * 2 + st) * SUBS + s
+    def ring_copy(st, s):
+        k = st * SUBS + s
         return Once(pltpu.make_async_remote_copy(src_ref=rsend.at[k], dst_ref=rrecv.at[k], send_sem=ring_ssem.at[k], recv_sem=ring_rsem.at[k],
-                                                 device_id=dev(right if dr == 0 else left), device_id_type=MESH), log, True)
-
-    ring = {(dr, st, s): ring_copy(dr, st, s) for dr in range(2) for st in range(2) for s in range(SUBS)}
-    dest = {0: (-1, 2, 1), 1: (1, 2, -1)}
-    tails = (tail_r, tail_l)
-
-    def pair_sum(d, s, dr):
-        pair_cps[d, s].wait_recv()
-        q = chip(d)
-        cols = pl.ds(dr * width, width)
-        return own[q, s, :, cols] + pairin[q, s, :, cols]
+                                                 device_id=dev(chip(sgn) * 2 + c), device_id_type=MESH), log, True)
+
+    ring = {(st, s): ring_copy(st, s) for st in range(2) for s in range(SUBS)}
+    stops = ((0, chip(-sgn)), (2, chip(2)), (1, chip(sgn)))
+
+    def pair_sum(role, s, q):
+        pair_cps[role, s].wait_recv()
+        return own[q, s] + pairin[q, s]
 
     def ring_step(st, s):
-        for dr in range(2):
-            v = pair_sum(dest[dr][st], s, dr)
-            if st > 0:
-                ring[dr, st - 1, s].wait_recv()
-                v = v + rrecv[(dr * 2 + st - 1) * SUBS + s]
-            if st < 2:
-                rsend[(dr * 2 + st) * SUBS + s] = v
-                ring[dr, st, s].start()
-            else:
-                tails[dr][s] = v
+        role, q = stops[st]
+        v = pair_sum(role, s, q)
+        if st > 0:
+            ring[st - 1, s].wait_recv()
+            v = v + rrecv[(st - 1) * SUBS + s]
+        if st < 2:
+            rsend[st * SUBS + s] = v
+            ring[st, s].start()
+        else:
+            tail[s] = v
 
     def finish():
         for cp in log:
@@ -262,7 +258,7 @@
     ld_wg.wait()
     ld_wu.wait()
     for s in range(3):
-        back((0,), [x], s)
+        back((3,), [x], s)
     to_r1.wait_recv()
     p_l1.start()
     to_l0.wait_recv()
@@ -278,17 +274,17 @@
     p_r0.wait_recv()
     p_r1.wait_recv()
     build(chip(1) * 2 + 1 - c)
-    near = [chip(-1), chip(1)]
+    near = [chip(sgn), chip(-sgn)]
     hidden(near)
-    back((-1, 1), near, 0)
-    back((-1, 1), near, 1)
+    back((0, 1), near, 0)
+    back((0, 1), near, 1)
     ring_step(0, 0)
     fw_r.wait_recv()
     p_f0.start()
     fw_l.wait_recv()
     p_f1.start()
     for s in range(2, SUBS):
-        back((-1, 1), near, s)
+        back((0, 1), near, s)
         ring_step(0, s - 1)
     build(far)
     ring_step(0, SUBS - 1)
@@ -303,7 +299,7 @@
         back((2,), [chip(2)], s)
         ring_step(1, s - 1)
     ring_step(1, SUBS - 1)
-    back((0,), [x], 3)
+    back((3,), [x], 3)
 
     ld_yr.wait()
     step = 16
@@ -318,8 +314,7 @@
     gg_out[...] = gg_rows[...].T
 
     for s in range(SUBS):
-        for dr in range(2):
-            base_out[s, :, pl.ds(dr * width, width)] = pair_sum(0, s, dr)
+        base_out[s] = pair_sum(3, s, x)
     for s in range(SUBS):
         ring_step(2, s)
 
@@ -334,8 +329,8 @@
     def copies(i):
         e, j, b = i // js, i % js, i % BUFS
         rows, arows = pl.ds(j * xc, xc), pl.ds(j * ac, ac)
-        return (pltpu.make_async_copy(gbuf.at[b, :, pl.ds(0, ffn)], gwg.at[e, rows, :], sem.at[b, 0]),
-                pltpu.make_async_copy(gbuf.at[b, :, pl.ds(ffn, ffn)], gwu.at[e, rows, :], sem.at[b, 1]),
+        return (pltpu.make_async_copy(gbuf.at[b, 0], gwg.at[e, rows, :], sem.at[b, 0]),
+                pltpu.make_async_copy(gbuf.at[b, 1], gwu.at[e, rows, :], sem.at[b, 1]),
                 pltpu.make_async_copy(dbuf.at[b], gwd.at[e, arows, :], sem.at[b, 2]))
 
     steps = n_loc * js
@@ -344,7 +339,9 @@
         if i >= BUFS:
             for cp in copies(i - BUFS):
                 cp.wait()
-        gbuf[b] = lax.dot_general(x_ref[e, :, pl.ds(j * xc, xc)], dh_ref[e], TN, preferred_element_type=F32)
+        r = lax.dot_general(x_ref[e, :, pl.ds(j * xc, xc)], dh_ref[e], TN, preferred_element_type=F32)
+        gbuf[b, 0] = r[:, :ffn]
+        gbuf[b, 1] = r[:, ffn:]
         dbuf[b] = lax.dot_general(a_ref[e, :, pl.ds(j * ac, ac)], d_ref[e], TN, preferred_element_type=F32)
         for cp in copies(i):
             cp.start()
@@ -353,11 +350,10 @@
             cp.wait()
 
 
-def finish_kernel(base, from_l, from_r, gx_out):
-    width = from_l.shape[2]
+def finish_kernel(base, got, gx_out):
+    chunk = got.shape[2]
     for s in range(SUBS):
-        for dr, ref in enumerate((from_l, from_r)):
-            gx_out[:, pl.ds((2 * s + dr) * width, width)] = (base[s, :, pl.ds(dr * width, width)] + ref[s]).astype(BF16)
+        gx_out[:, pl.ds(s * chunk, chunk)] = (base[s] + got[s]).astype(BF16)
 
 
 def solution(mesh):
@@ -376,14 +372,14 @@
         hbm = pl.BlockSpec(memory_space=pl.ANY)
         dma = pltpu.SemaphoreType.DMA
         vs = pltpu.VMEM
-        tail = vs((SUBS, tok, model // 2 // SUBS), F32)
+        tail = vs((SUBS, tok, model // SUBS), F32)
         js = 2
-        base, tail_r, tail_l, gg, d_rows, dh, act, x_rows = pl.pallas_call(
+        base, last, gg, d_rows, dh, act, x_rows = pl.pallas_call(
             functools.partial(exchange_kernel, n_dev, cap),
-            out_shape=(vs((SUBS, tok, model // SUBS), F32), tail, tail, pltpu.VMEM((top_k, tok), F32), pltpu.VMEM((n_loc, rows, model), BF16),
+            out_shape=(tail, tail, pltpu.VMEM((top_k, tok), F32), pltpu.VMEM((n_loc, rows, model), BF16),
                        pltpu.VMEM((n_loc, rows, 2 * ffn), BF16), pltpu.VMEM((n_loc, rows, ffn), BF16), pltpu.VMEM((n_loc, rows, model), BF16)),
             in_specs=[hbm] * 12,
-            out_specs=(vm,) * 8,
+            out_specs=(vm,) * 7,
             scratch_shapes=[
                 pltpu.SMEM(pair_counts.shape, jnp.int32),
                 pltpu.VMEM((top_k, tok), jnp.int32),
@@ -404,24 +400,23 @@
                 pltpu.VMEM((n_chip, SUBS, tok, model // SUBS), F32),
                 pltpu.VMEM((n_chip, SUBS, tok, model // SUBS), F32),
                 pltpu.VMEM((n_chip, SUBS, tok, model // SUBS), F32),
-                pltpu.VMEM((4 * SUBS, tok, model // 2 // SUBS), F32),
-                pltpu.VMEM((4 * SUBS, tok, model // 2 // SUBS), F32),
+                pltpu.VMEM((2 * SUBS, tok, model // SUBS), F32),
+                pltpu.VMEM((2 * SUBS, tok, model // SUBS), F32),
                 dma((12,)), dma((n_dev - 1,)), dma((n_dev - 1,)), dma((13,)), dma((13,)),
-                dma((SUBS * n_chip,)), dma((SUBS * n_chip,)), dma((4 * SUBS,)), dma((4 * SUBS,)),
+                dma((SUBS * n_chip,)), dma((SUBS * n_chip,)), dma((2 * SUBS,)), dma((2 * SUBS,)),
             ],
             compiler_params=pltpu.CompilerParams(collective_id=0, has_side_effects=True, vmem_limit_bytes=44 * 1024 * 1024),
             name="exchange",
         )(pair_counts, gate_vals.T, topk_idx.T, slot_ids.T, grad_y, y_routed, h_gate, h_up, w_gate, w_up, w_down, x_disp)
-        ring_r = [(i, ((i // 2 + 1) % n_chip) * 2 + i % 2) for i in range(n_dev)]
-        from_l = lax.ppermute(tail_r, "ep", ring_r)
-        from_r = lax.ppermute(tail_l, "ep", [(b, a) for a, b in ring_r])
+        hops = [(i, ((i // 2 + 1 - 2 * (i % 2)) % n_chip) * 2 + i % 2) for i in range(n_dev)]
+        got = lax.ppermute(last, "ep", hops)
         gg, gwg, gwu, gwd = pl.pallas_call(
             functools.partial(weight_kernel, js),
             out_shape=(jax.ShapeDtypeStruct((top_k, tok), F32), jax.ShapeDtypeStruct((n_loc, model, ffn), F32),
                        jax.ShapeDtypeStruct((n_loc, model, ffn), F32), jax.ShapeDtypeStruct((n_loc, ffn, model), F32)),
             in_specs=[vm] * 5,
             out_specs=(vm, hbm, hbm, hbm),
-            scratch_shapes=[pltpu.VMEM((BUFS, model // js, 2 * ffn), F32), pltpu.VMEM((BUFS, ffn // js, model), F32), dma((BUFS, 3))],
+            scratch_shapes=[pltpu.VMEM((BUFS, 2, model // js, ffn), F32), pltpu.VMEM((BUFS, ffn // js, model), F32), dma((BUFS, 3))],
             compiler_params=pltpu.CompilerParams(vmem_limit_bytes=24 * 1024 * 1024),
             cost_estimate=pl.CostEstimate(flops=6 * n_loc * rows * model * ffn, bytes_accessed=12 * n_loc * model * ffn, transcendentals=0),
             name="weights",
@@ -429,11 +424,11 @@
         gx = pl.pallas_call(
             finish_kernel,
             out_shape=jax.ShapeDtypeStruct((tok, model), BF16),
-            in_specs=[vm] * 3,
+            in_specs=[vm] * 2,
             out_specs=vm,
             compiler_params=pltpu.CompilerParams(vmem_limit_bytes=4 * 1024 * 1024),
             name="finish",
-        )(base, from_l, from_r)
+        )(base, got)
         return gx, gg.T, gwg, gwu, gwd
 
     return jax.shard_map(local_step, mesh=mesh, in_specs=(rows_spec, rows_spec, rows_spec, rows_spec, rows_spec, cube_spec, cube_spec, cube_spec, cube_spec, weight_spec, weight_spec, weight_spec), out_specs=(rows_spec, rows_spec, cube_spec, cube_spec, cube_spec), check_vma=False)

time: 50.4 us -> 47.8 us (0.948)
  starting transfers between devices: 3.31 us -> 0.1 us
  waiting for transfers between devices: 0.01 us -> 0.55 us
    ppermute x2 -> x1, starting transfers between devices: 3.31 us -> 0.1 us  [local_step(): got = lax.ppermute(last, 'ep', hops)]
    ppermute x2 -> x1, waiting for transfers between devices: 0.01 us -> 0.55 us  [local_step(): got = lax.ppermute(last, 'ep', hops)]
  transfers between devices with their start and end apart: 2 -> 1, of which waited for: 0 -> 1; matrix products, arithmetic and copies ran while one was open for 0% -> 0% of each run, Pallas kernels for 19% -> 21%
where the time goes in v11:
time: 47.8 us; the launch traced here: 47.7 us
  Pallas kernels  46.4 us (97%)
  between operations  0.66 us (1%)
  waiting for transfers between devices  0.55 us (1%)
    pallas_call x1, Pallas kernels, local_step(): pl.pallas_call(functools.partial(exchange_kernel, n_dev, cap), out_shape=...  35.8 us
    pallas_call x1, Pallas kernels, local_step(): pl.pallas_call(functools.partial(weight_kernel, js), out_shape=(jax.Shape...  9.81 us
  transfers between devices with their start and end apart: 1, of which 1 were waited for; matrix products, arithmetic and copies ran while one was open for 0% of the time, Pallas kernels for 21%

profile of v11, /device:TPU:112, one launch (start us, length us, event | category | flops | bytes accessed | tf_op | source)
XLA Modules:
  0.0 47.7 jit_solution(74306623053290031)
XLA Ops:
  0.6 35.8 %exchange.1 = (f32[4,128,256]{2,1,0:T(8,128)S(1)}, f32[4,128,256]{2,1,0:T(8,128)S(1)}, f32[8,128]{1,0:T(8,128)S(1)}, bf16[4,512,1024]{2,1,0:T(8,128)(2,1)S(1)}, ...) custom-call(s32[1,32]{1,0:T(1,128)} %counts_hbm.1, ...), custom_call_target="tpu_custom_call" | custom-call | tf_op jit(solution)/shard_map/exchange/pallas_call | solution.py:377
  36.4 0.1 collective-permute-start
  36.6 9.8 %weights.1 = (f32[8,128]{1,0:T(8,128)}, f32[4,1024,512]{2,1,0:T(8,128)}, f32[4,1024,512]{2,1,0:T(8,128)}, f32[4,512,1024]{2,1,0:T(8,128)}) custom-call(bf16[4,512,1024]{2,1,0:T(8,128)(2,1)S(1)} %get-tuple-element.18.x_ref, bf16[4,512,1024]{2,1,0:T(8,128)(2,1)S(1)} %get-tuple-element.19.dh_ref, bf16[4,512,512]{2,1,0:T(8,128)(2,1)S(1)} %get-tuple-element.20.a_ref, ...), custom_call_target="tpu_custom_call" | custom-call | flops 6442450944 | bytes 25165824 | tf_op jit(solution)/shard_map/weights/pallas_call | solution.py:413
  46.4 0.6 %collective-permute-done.got = f32[4,128,256]{2,1,0:T(8,128)S(1)} collective-permute-done((f32[4,128,256]{2,1,0:T(8,128)S(1)}, f32[4,128,256]{2,1,0:T(8,128)S(1)}, u32[]{:S(2)}, u32[]{:S(2)}) %collective-permute-start) | collective-permute-done | bytes 524320 | tf_op jit(solution)/shard_map/ppermute | solution.py:412
  46.9 0.8 %finish.1 = bf16[128,1024]{1,0:T(8,128)(2,1)} custom-call(f32[4,128,256]{2,1,0:T(8,128)S(1)} %get-tuple-element.16.base, f32[4,128,256]{2,1,0:T(8,128)S(1)} %collective-permute-done.got), custom_call_target="tpu_custom_call" | custom-call | tf_op jit(solution)/shard_map/finish/pallas_call | solution.py:424
Async XLA Ops:
  36.4 10.5 %collective-permute-start = (f32[4,128,256]{2,1,0:T(8,128)S(1)}, f32[4,128,256]{2,1,0:T(8,128)S(1)}, u32[]{:S(2)}, u32[]{:S(2)}) collective-permute-start(f32[4,128,256]{2,1,0:T(8,128)S(1)} %get-tuple-element.17), channel_id=1, source_target_pairs={{0,2},{1,7},{2,4},{3,1},{4,6},{5,3},{6,0},{7,5},{8,10},{9,15},{10,... | collective-permute-start | bytes 1572872 | tf_op jit(solution)/shard_map/ppermute | solution.py:412

commit v12 on v11

--- a/solution.py
+++ b/solution.py
@@ -13,7 +13,7 @@
 NT = (((1,), (1,)), ((), ()))
 TN = (((0,), (0,)), ((), ()))
 SUBS = 4
-BUFS = 3
+BUFS = 6
 
 
 class Once:
@@ -200,10 +200,9 @@
                 for j in range(2):
                     rbuf[i, j, pl.ds(e * cap, cap), :] = r[(i * 2 + j) * cap:(i * 2 + j + 1) * cap]
 
-        for i, q in enumerate(qs):
+        for i, (role, q) in enumerate(zip(roles, qs)):
             psend[q, hf] = jnp.dot(pt[q * 2 + 1 - c], rbuf[i, 1 - c], preferred_element_type=F32)
-        for i, role in enumerate(roles):
-            cp = pair_copy(qs[i], role * SUBS + hf, hf)
+            cp = pair_copy(q, role * SUBS + hf, hf)
             cp.start()
             pair_cps[role, hf] = cp
         for i, q in enumerate(qs):
@@ -373,7 +372,7 @@
         dma = pltpu.SemaphoreType.DMA
         vs = pltpu.VMEM
         tail = vs((SUBS, tok, model // SUBS), F32)
-        js = 2
+        js = 4
         base, last, gg, d_rows, dh, act, x_rows = pl.pallas_call(
             functools.partial(exchange_kernel, n_dev, cap),
             out_shape=(tail, tail, pltpu.VMEM((top_k, tok), F32), pltpu.VMEM((n_loc, rows, model), BF16),

time: 47.8 us -> 48.8 us (1.021)
  Pallas kernels: 46.4 us -> 47.5 us
  waiting for transfers between devices: 0.55 us -> 0.01 us
    pallas_call x1, Pallas kernels: 9.81 us -> 10.5 us  [local_step(): pl.pallas_call(functools.partial(weight_kernel, js), out_shape=(jax.Shape...]
    ppermute x1, waiting for transfers between devices: 0.55 us -> 0.01 us  [local_step(): got = lax.ppermute(last, 'ep', hops)]
  transfers between devices with their start and end apart: 1 -> 1, of which waited for: 1 -> 0; matrix products, arithmetic and copies ran while one was open for 0% -> 0% of each run, Pallas kernels for 21% -> 22%
where the time goes in v12:
time: 48.8 us; the launch traced here: 48.2 us
  Pallas kernels  47.5 us (97%)
  between operations  0.67 us (1%)
    pallas_call x1, Pallas kernels, local_step(): pl.pallas_call(functools.partial(exchange_kernel, n_dev, cap), out_shape=...  36.2 us
    pallas_call x1, Pallas kernels, local_step(): pl.pallas_call(functools.partial(weight_kernel, js), out_shape=(jax.Shape...  10.5 us
  transfers between devices with their start and end apart: 1, of which 0 were waited for; matrix products, arithmetic and copies ran while one was open for 0% of the time, Pallas kernels for 22%

profile of v12, /device:TPU:112, one launch (start us, length us, event | category | flops | bytes accessed | tf_op | source)
XLA Modules:
  0.0 48.2 jit_solution(16011956047712110270)
XLA Ops:
  0.6 36.2 %exchange.1 = (f32[4,128,256]{2,1,0:T(8,128)S(1)}, f32[4,128,256]{2,1,0:T(8,128)S(1)}, f32[8,128]{1,0:T(8,128)S(1)}, bf16[4,512,1024]{2,1,0:T(8,128)(2,1)S(1)}, ...) custom-call(s32[1,32]{1,0:T(1,128)} %counts_hbm.1, ...), custom_call_target="tpu_custom_call" | custom-call | tf_op jit(solution)/shard_map/exchange/pallas_call | solution.py:376
  36.9 0.1 collective-permute-start
  37.0 10.5 %weights.1 = (f32[8,128]{1,0:T(8,128)}, f32[4,1024,512]{2,1,0:T(8,128)}, f32[4,1024,512]{2,1,0:T(8,128)}, f32[4,512,1024]{2,1,0:T(8,128)}) custom-call(bf16[4,512,1024]{2,1,0:T(8,128)(2,1)S(1)} %get-tuple-element.18.x_ref, bf16[4,512,1024]{2,1,0:T(8,128)(2,1)S(1)} %get-tuple-element.19.dh_ref, bf16[4,512,512]{2,1,0:T(8,128)(2,1)S(1)} %get-tuple-element.20.a_ref, ...), custom_call_target="tpu_custom_call" | custom-call | flops 6442450944 | bytes 25165824 | tf_op jit(solution)/shard_map/weights/pallas_call | solution.py:412
  47.4 0.0 collective-permute-done.got
  47.4 0.8 %finish.1 = bf16[128,1024]{1,0:T(8,128)(2,1)} custom-call(f32[4,128,256]{2,1,0:T(8,128)S(1)} %get-tuple-element.16.base, f32[4,128,256]{2,1,0:T(8,128)S(1)} %collective-permute-done.got), custom_call_target="tpu_custom_call" | custom-call | tf_op jit(solution)/shard_map/finish/pallas_call | solution.py:423
Async XLA Ops:
  36.9 10.6 %collective-permute-start = (f32[4,128,256]{2,1,0:T(8,128)S(1)}, f32[4,128,256]{2,1,0:T(8,128)S(1)}, u32[]{:S(2)}, u32[]{:S(2)}) collective-permute-start(f32[4,128,256]{2,1,0:T(8,128)S(1)} %get-tuple-element.17), channel_id=1, source_target_pairs={{0,2},{1,7},{2,4},{3,1},{4,6},{5,3},{6,0},{7,5},{8,10},{9,15},{10,... | collective-permute-start | bytes 1572872 | tf_op jit(solution)/shard_map/ppermute | solution.py:411

commit v13 on v11

--- a/solution.py
+++ b/solution.py
@@ -257,8 +257,7 @@
             prep(chip(d) * 2 + i)
     ld_wg.wait()
     ld_wu.wait()
-    for s in range(3):
-        back((3,), [x], s)
+    back((3,), [x], 0)
     to_r1.wait_recv()
     p_l1.start()
     to_l0.wait_recv()
@@ -299,7 +298,8 @@
         back((2,), [chip(2)], s)
         ring_step(1, s - 1)
     ring_step(1, SUBS - 1)
-    back((3,), [x], 3)
+    for s in range(1, SUBS):
+        back((3,), [x], s)
 
     ld_yr.wait()
     step = 16

time: 47.8 us -> 47.5 us (level)
  Pallas kernels: 46.4 us -> 45.8 us
    pallas_call x1, Pallas kernels: 35.8 us -> 35.2 us  [local_step(): pl.pallas_call(functools.partial(exchange_kernel, n_dev, cap), out_shape=...]
where the time goes in v13:
time: 47.5 us; the launch traced here: 47.1 us
  Pallas kernels  45.8 us (96%)
  between operations  0.65 us (1%)
  waiting for transfers between devices  0.55 us (1%)
    pallas_call x1, Pallas kernels, local_step(): pl.pallas_call(functools.partial(exchange_kernel, n_dev, cap), out_shape=...  35.2 us
    pallas_call x1, Pallas kernels, local_step(): pl.pallas_call(functools.partial(weight_kernel, js), out_shape=(jax.Shape...  9.8 us
  transfers between devices with their start and end apart: 1, of which 1 were waited for; matrix products, arithmetic and copies ran while one was open for 0% of the time, Pallas kernels for 21%

profile of v13, /device:TPU:112, one launch (start us, length us, event | category | flops | bytes accessed | tf_op | source)
XLA Modules:
  0.0 47.1 jit_solution(10118225791711926493)
XLA Ops:
  0.6 35.2 %exchange.1 = (f32[4,128,256]{2,1,0:T(8,128)S(1)}, f32[4,128,256]{2,1,0:T(8,128)S(1)}, f32[8,128]{1,0:T(8,128)S(1)}, bf16[4,512,1024]{2,1,0:T(8,128)(2,1)S(1)}, ...) custom-call(s32[1,32]{1,0:T(1,128)} %counts_hbm.1, ...), custom_call_target="tpu_custom_call" | custom-call | tf_op jit(solution)/shard_map/exchange/pallas_call | solution.py:377
  35.8 0.1 collective-permute-start
  35.9 9.8 %weights.1 = (f32[8,128]{1,0:T(8,128)}, f32[4,1024,512]{2,1,0:T(8,128)}, f32[4,1024,512]{2,1,0:T(8,128)}, f32[4,512,1024]{2,1,0:T(8,128)}) custom-call(bf16[4,512,1024]{2,1,0:T(8,128)(2,1)S(1)} %get-tuple-element.18.x_ref, bf16[4,512,1024]{2,1,0:T(8,128)(2,1)S(1)} %get-tuple-element.19.dh_ref, bf16[4,512,512]{2,1,0:T(8,128)(2,1)S(1)} %get-tuple-element.20.a_ref, ...), custom_call_target="tpu_custom_call" | custom-call | flops 6442450944 | bytes 25165824 | tf_op jit(solution)/shard_map/weights/pallas_call | solution.py:413
  45.7 0.6 %collective-permute-done.got = f32[4,128,256]{2,1,0:T(8,128)S(1)} collective-permute-done((f32[4,128,256]{2,1,0:T(8,128)S(1)}, f32[4,128,256]{2,1,0:T(8,128)S(1)}, u32[]{:S(2)}, u32[]{:S(2)}) %collective-permute-start) | collective-permute-done | bytes 524320 | tf_op jit(solution)/shard_map/ppermute | solution.py:412
  46.3 0.8 %finish.1 = bf16[128,1024]{1,0:T(8,128)(2,1)} custom-call(f32[4,128,256]{2,1,0:T(8,128)S(1)} %get-tuple-element.16.base, f32[4,128,256]{2,1,0:T(8,128)S(1)} %collective-permute-done.got), custom_call_target="tpu_custom_call" | custom-call | tf_op jit(solution)/shard_map/finish/pallas_call | solution.py:424
Async XLA Ops:
  35.8 10.5 %collective-permute-start = (f32[4,128,256]{2,1,0:T(8,128)S(1)}, f32[4,128,256]{2,1,0:T(8,128)S(1)}, u32[]{:S(2)}, u32[]{:S(2)}) collective-permute-start(f32[4,128,256]{2,1,0:T(8,128)S(1)} %get-tuple-element.17), channel_id=1, source_target_pairs={{0,2},{1,7},{2,4},{3,1},{4,6},{5,3},{6,0},{7,5},{8,10},{9,15},{10,... | collective-permute-start | bytes 1572872 | tf_op jit(solution)/shard_map/ppermute | solution.py:412
